TPU v7x, 512 devices: a whole 4x8x8 slice. The times are simulated.
512 devices in a mesh: pipe: 16 (over x_lo, y), dp: 4 (over x_hi, core), expert: 8 (over z).
Axes of the slice: x: 4 (x_hi: 2, x_lo: 2; x = x_hi * 2 + x_lo), y: 8, z: 8, core: 2. Of those that a mesh axis runs over, the one named last changes fastest.
Arguments:
- entering: bfloat16 [16, 512, 4096], P('pipe', 'dp', 'expert'), may hold values from -6 to 6
- pending: bfloat16 [16, 512, 4096], P('pipe', 'dp', 'expert'), may hold values from -6 to 6
- stashed_in: bfloat16 [16, 512, 4096], P('pipe', 'dp', 'expert'), may hold values from -6 to 6
- forward_routes: int32 [16, 512, 2], P('pipe', 'dp'), may hold values from 0 to 3, all different within a row; in each aligned block of 128 rows (0 to 127, 128 to 255, ..., all dimensions but the last counted through in order) at most 64 rows name the same one
- backward_routes: int32 [16, 512, 2], P('pipe', 'dp'), may hold values from 0 to 3, all different within a row; in each aligned block of 128 rows (0 to 127, 128 to 255, ..., all dimensions but the last counted through in order) at most 64 rows name the same one
- norm_gains: float32 [16, 4096], P('pipe', 'expert'), may hold values from 0.5 to 1.5
- w_router: bfloat16 [16, 4096, 4], P('pipe', 'expert'), may hold values from -0.09375 to 0.09375
- w_gateup: bfloat16 [16, 4, 4096, 2, 1024], P('pipe', 'dp', None, None, 'expert'), may hold values from -0.09375 to 0.09375
- w_down: bfloat16 [16, 4, 1024, 4096], P('pipe', 'dp', 'expert'), may hold values from -0.1875 to 0.1875
Outputs:
- forward_out: bfloat16 [16, 512, 4096], P('pipe', 'dp', 'expert')
- input_grads: bfloat16 [16, 512, 4096], P('pipe', 'dp', 'expert')
- passed_forward: bfloat16 [16, 512, 4096], P('pipe', 'dp', 'expert')
- passed_backward: bfloat16 [16, 512, 4096], P('pipe', 'dp', 'expert')
- gain_grads: float32 [16, 4096], P('pipe', 'expert')
Inputs may be any that keep to these rules, and one draw needn't show every extreme that they name: `forward_routes`: each row names 2 different experts; in each aligned block of 128 rows (one sequence) every expert is named by exactly 64 rows. `backward_routes`: each row names 2 different experts; in each aligned block of 128 rows (one sequence) every expert is named by exactly 64 rows.
All inputs are finite; a program needn't handle non-finite values.
Results may differ from a plain program's by a relative error of at most 0.015.
Values may be sent and summed in bfloat16 or wider, within the bound.
No kernel may reach another device: no remote copies, remote signals or barrier semaphores. Data moves between devices by JAX's collectives and lax.ppermute only.
A program may use at most 64 MiB of HBM per device.

v0:
```python
import jax
import jax.numpy as jnp
from jax import lax
from jax.sharding import PartitionSpec as P

D = 4096


ROUTE_SCALE = 2.827
EPSILON = 1e-05


def sent_to_all(shard, axis):
    copies = jnp.broadcast_to(shard, (lax.axis_size(axis), *shard.shape))
    return lax.all_to_all(copies, axis, split_axis=0, concat_axis=0, tiled=True)


def taken_together(shard, axis):
    everything = sent_to_all(shard, axis)
    return jnp.sum(everything, axis=0)


def in_order(blocks, dim):
    dims = list(blocks.shape[1:])
    dims[dim] *= blocks.shape[0]
    return jnp.moveaxis(blocks, 0, dim).reshape(dims)


def gather_directly(shard, axis, dim):
    blocks = sent_to_all(shard, axis)
    return in_order(blocks, dim)


def shifted(block, axis, distance):
    devices = range(lax.axis_size(axis))
    route = [(i - distance, i) for i in devices if i - distance in devices]
    return lax.ppermute(block, axis, route)


def feature_sum(values):
    return taken_together(values, "expert")


def normalize(tokens, gain_row):
    values = tokens.astype(jnp.float32)
    squares = feature_sum(jnp.sum(values * values, axis=-1, keepdims=True))
    scaling = lax.rsqrt(squares / D + EPSILON)
    return (values, scaling, (values * scaling * gain_row).astype(jnp.bfloat16))


def gating(moe_in, router, routes):
    experts = router.shape[1]
    logits = feature_sum(jnp.dot(moe_in, router, preferred_element_type=jnp.float32))
    selection = (routes[:, :, None] == jnp.arange(experts, dtype=jnp.int32)[None, None, :]).astype(
        jnp.float32
    )
    chosen = jnp.sum(logits[:, None, :] * selection, axis=-1)
    lifted = jax.nn.sigmoid(chosen)
    lifted_sum = jnp.sum(lifted, axis=-1, keepdims=True)
    return (ROUTE_SCALE * lifted / lifted_sum, lifted, lifted_sum, selection)


def layout(routes, experts):
    capacity = routes.shape[0] * routes.shape[1] // experts
    flattened = routes.reshape(-1)
    member = (flattened[:, None] == jnp.arange(experts, dtype=jnp.int32)[None, :]).astype(jnp.int32)
    before = jnp.cumsum(member, axis=0) - member
    position = jnp.sum(before * member, axis=1)
    destination = flattened * capacity + position
    placing = (
        destination[:, None] == jnp.arange(experts * capacity, dtype=jnp.int32)[None, :]
    ).astype(jnp.bfloat16)
    return (capacity, destination, placing)


def spread(placing, route_rows):
    return jnp.einsum("rc,rd->cd", placing, route_rows, preferred_element_type=jnp.float32).astype(
        jnp.bfloat16
    )


def add_projection(gate_up, segment):
    return jnp.einsum("sxcd,xdkf->sxckf", segment, gate_up, preferred_element_type=jnp.float32)


def run_forward(tokens, routes, gain_row, router, gate_up, down_w):
    length, local_width = tokens.shape
    experts = router.shape[1]
    local_count = gate_up.shape[0]
    values, scaling, moe_in = normalize(tokens, gain_row)
    gate_weights, lifted, lifted_sum, selection = gating(moe_in, router, routes)
    capacity, destination, placing = layout(routes, experts)
    route_rows = jnp.repeat(moe_in, routes.shape[1], axis=0)
    buffer = spread(placing, route_rows).reshape(
        experts // local_count, local_count, capacity, local_width
    )

    def compute(received):
        projected = add_projection(gate_up, gather_directly(received, "expert", 3))
        gate_pre = projected[:, :, :, 0]
        second = projected[:, :, :, 1]
        inner_act = (jax.nn.silu(gate_pre) * second).astype(jnp.bfloat16)
        partial_value = jnp.einsum(
            "sxcf,xfd->sxcd", inner_act, down_w, preferred_element_type=jnp.float32
        )
        summed = lax.psum_scatter(
            partial_value.astype(jnp.bfloat16), "expert", scatter_dimension=3, tiled=True
        )
        return lax.all_to_all(summed, "dp", split_axis=0, concat_axis=0, tiled=True)

    results = compute(lax.all_to_all(buffer, "dp", split_axis=0, concat_axis=0, tiled=True))
    picked = jnp.take(
        results.reshape(experts * capacity, local_width), destination, axis=0
    ).reshape(length, routes.shape[1], local_width)
    return (values + jnp.sum(gate_weights[:, :, None] * picked.astype(jnp.float32), axis=1)).astype(
        jnp.bfloat16
    )


def run_backward(stashed, incoming, routes, gain_row, router, gate_up, down_w):
    length, local_width = stashed.shape
    experts = router.shape[1]
    local_count = gate_up.shape[0]
    chosen_count = routes.shape[1]
    values, scaling, moe_in = normalize(stashed, gain_row)
    gate_weights, lifted, lifted_sum, selection = gating(moe_in, router, routes)
    capacity, destination, placing = layout(routes, experts)
    slot_shape = (experts // local_count, local_count, capacity, local_width)
    row_buffer = spread(placing, jnp.repeat(moe_in, chosen_count, axis=0)).reshape(slot_shape)
    upstream_buffer = spread(placing, jnp.repeat(incoming, chosen_count, axis=0)).reshape(
        slot_shape
    )

    def compute(received):
        rows_in, up_in = received
        rows_piece = lax.all_gather(rows_in, "expert", axis=3, tiled=True)
        up_piece = lax.all_gather(up_in, "expert", axis=3, tiled=True)
        first_sum = jnp.einsum(
            "sxcd,xdkf->sxckf", rows_piece, gate_up, preferred_element_type=jnp.float32
        )
        second_sum = jnp.einsum(
            "sxcd,xfd->sxcf", up_piece, down_w, preferred_element_type=jnp.float32
        )
        gate_pre = first_sum[:, :, :, 0]
        second = first_sum[:, :, :, 1]
        lifted_act = jax.nn.sigmoid(gate_pre)
        activated = gate_pre * lifted_act
        inner_act = (activated * second).astype(jnp.bfloat16)
        gate_total = feature_sum(
            jnp.sum(inner_act.astype(jnp.float32) * second_sum, axis=-1)
        ).astype(jnp.bfloat16)
        grad_first = (
            second_sum * second * lifted_act * (1.0 + gate_pre * (1.0 - lifted_act))
        ).astype(jnp.bfloat16)
        grad_second = (second_sum * activated).astype(jnp.bfloat16)
        stacked = jnp.stack([grad_first, grad_second], axis=3)
        partial_value = jnp.einsum(
            "sxckf,xdkf->sxcd", stacked, gate_up, preferred_element_type=jnp.float32
        )
        summed = lax.psum_scatter(
            partial_value.astype(jnp.bfloat16), "expert", scatter_dimension=3, tiled=True
        )
        return (
            lax.all_to_all(summed, "dp", split_axis=0, concat_axis=0, tiled=True),
            lax.all_to_all(gate_total, "dp", split_axis=0, concat_axis=0, tiled=True),
        )

    back_rows, back_gate = compute(
        (
            lax.all_to_all(row_buffer, "dp", split_axis=0, concat_axis=0, tiled=True),
            lax.all_to_all(upstream_buffer, "dp", split_axis=0, concat_axis=0, tiled=True),
        )
    )
    back_rows = jnp.take(
        back_rows.reshape(experts * capacity, local_width), destination, axis=0
    ).reshape(length, chosen_count, local_width)
    back_gate = (
        jnp.take(back_gate.reshape(-1), destination, axis=0)
        .reshape(length, chosen_count)
        .astype(jnp.float32)
    )
    moe_cot = jnp.sum(gate_weights[:, :, None] * back_rows.astype(jnp.float32), axis=1).astype(
        jnp.bfloat16
    )
    mixed = jnp.sum(back_gate * lifted, axis=-1, keepdims=True) / lifted_sum
    chosen_cot = ROUTE_SCALE * (back_gate - mixed) / lifted_sum * lifted * (1.0 - lifted)
    logit_cot = jnp.sum(chosen_cot[:, :, None] * selection, axis=1)
    norm_cot = moe_cot.astype(jnp.float32) + jnp.dot(logit_cot, router.astype(jnp.float32).T)
    scaled = norm_cot * gain_row
    inner_product = feature_sum(jnp.sum(scaled * values, axis=-1, keepdims=True))
    token_cot = (
        incoming.astype(jnp.float32)
        + scaling * scaled
        - values * (scaling * scaling * scaling) * inner_product / D
    )
    gain_cot = jnp.sum(norm_cot * values * scaling, axis=0)
    return (token_cot.astype(jnp.bfloat16), gain_cot)


def local(
    entering,
    pending,
    stashed_in,
    forward_routes,
    backward_routes,
    norm_gains,
    w_router,
    w_gateup,
    w_down,
):
    gain_row = norm_gains[0]
    router = w_router[0]
    gate_up = w_gateup[0]
    down_w = w_down[0]
    produced = run_forward(entering[0], forward_routes[0], gain_row, router, gate_up, down_w)
    cotangent, gain_part = run_backward(
        stashed_in[0], pending[0], backward_routes[0], gain_row, router, gate_up, down_w
    )
    passed_forward = shifted(produced, "pipe", 1)
    passed_backward = shifted(cotangent, "pipe", -1)
    gain_total = lax.psum(gain_part, "dp")
    return (
        produced[None],
        cotangent[None],
        passed_forward[None],
        passed_backward[None],
        gain_total[None],
    )


def solution(mesh):
    placed = (
        P("pipe", "dp", "expert"),
        P("pipe", "dp", "expert"),
        P("pipe", "dp", "expert"),
        P("pipe", "dp", None),
        P("pipe", "dp", None),
        P("pipe", "expert"),
        P("pipe", "expert", None),
        P("pipe", "dp", None, None, "expert"),
        P("pipe", "dp", "expert", None),
    )
    return jax.shard_map(
        local,
        mesh=mesh,
        in_specs=placed,
        out_specs=(
            P("pipe", "dp", "expert"),
            P("pipe", "dp", "expert"),
            P("pipe", "dp", "expert"),
            P("pipe", "dp", "expert"),
            P("pipe", "expert"),
        ),
        check_vma=False,
    )
```

profile of v0, /device:TPU:2, one launch (start us, length us, event | category | flops | bytes accessed | tf_op | source)
XLA Modules:
  0.0 362.4 jit_solution(17408386707494603050)
XLA Ops:
  8.9 10.3 %all-to-all-start.5 = ((f32[8,128,1]{1,2,0:T(1,128)}), f32[8,128,1]{1,2,0:T(1,128)S(1)}, u32[]{:S(2)}, u32[]{:S(2)}) async-start(f32[8,128,1]{1,2,0:T(1,128)} %broadcast_in_dim.81), calls=%async_computation.6 | async-start | bytes 8192 | tf_op jit(solution)/shard_map/all_to_all | solution.py:15
  22.0 4.8 %all-to-all-done.5 = f32[8,128,1]{1,2,0:T(1,128)S(1)} async-done(((f32[8,128,1]{1,2,0:T(1,128)}), f32[8,128,1]{1,2,0:T(1,128)S(1)}, u32[]{:S(2)}, u32[]{:S(2)}) %all-to-all-start.5) | async-done | bytes 4128 | tf_op jit(solution)/shard_map/all_to_all | solution.py:15
  30.6 10.8 %all_to_all.68 = bf16[4,1,64,512]{3,2,1,0:T(8,128)(2,1)} all-to-all(bf16[4,1,64,512]{3,2,1,0:T(8,128)(2,1)S(1)} %bitcast.259), channel_id=1, replica_groups=mesh['pipe'=16,'dp'=4,'expert'=8] {'dp'}, dimensions={0} | all-to-all | bytes 524288 | tf_op jit(solution)/shard_map/all_to_all | solution.py:170
  43.8 10.6 %all_to_all.69 = bf16[4,1,64,512]{3,2,1,0:T(8,128)(2,1)} all-to-all(bf16[4,1,64,512]{3,2,1,0:T(8,128)(2,1)S(1)} %bitcast.260), channel_id=1, replica_groups=mesh['pipe'=16,'dp'=4,'expert'=8] {'dp'}, dimensions={0} | all-to-all | bytes 524288 | tf_op jit(solution)/shard_map/all_to_all | solution.py:171
  54.4 26.3 %all-gather.5.cloned.1.call-done = bf16[4,1,64,4096]{3,2,0,1:T(8,128)(2,1)} async-done(((bf16[4,1,64,512]{3,2,0,1:T(8,128)(2,1)}), bf16[4,1,64,4096]{3,2,0,1:T(8,128)(2,1)}) %all-gather.5.cloned.1.call-update) | async-done | bytes 2097168 | tf_op jit(solution)/shard_map/all_gather | solution.py:136
  83.7 41.4 %all-gather.3.cloned.1.call-done = bf16[4,1,64,4096]{3,2,0,1:T(8,128)(2,1)} async-done(((bf16[4,1,64,512]{3,2,0,1:T(8,128)(2,1)}), bf16[4,1,64,4096]{3,2,0,1:T(8,128)(2,1)}) %all-gather.3.cloned.1.call-update) | async-done | bytes 2097168 | tf_op jit(solution)/shard_map/all_gather | solution.py:137
  131.3 4.4 %all-to-all-start = ((f32[8,128,1]{1,2,0:T(1,128)}), f32[8,128,1]{1,2,0:T(1,128)S(1)}, u32[]{:S(2)}, u32[]{:S(2)}) async-start(f32[8,128,1]{1,2,0:T(1,128)} %broadcast_in_dim.43), calls=%async_computation | async-start | bytes 8192 | tf_op jit(solution)/shard_map/all_to_all | solution.py:15
  138.3 5.0 %all-to-all-done = f32[8,128,1]{1,2,0:T(1,128)S(1)} async-done(((f32[8,128,1]{1,2,0:T(1,128)}), f32[8,128,1]{1,2,0:T(1,128)S(1)}, u32[]{:S(2)}, u32[]{:S(2)}) %all-to-all-start) | async-done | bytes 4128 | tf_op jit(solution)/shard_map/all_to_all | solution.py:15
  147.5 7.6 %all-to-all-done.6 = f32[8,128,4]{1,2,0:T(4,128)S(1)} async-done(((f32[8,128,4]{1,2,0:T(4,128)}), f32[8,128,4]{1,2,0:T(4,128)S(1)}, u32[]{:S(2)}, u32[]{:S(2)}) %all-to-all-start.6) | async-done | bytes 16416 | tf_op jit(solution)/shard_map/all_to_all | solution.py:15
  161.2 5.6 %all-to-all-done.1 = f32[8,128,4]{1,2,0:T(4,128)S(1)} async-done(((f32[8,128,4]{1,2,0:T(4,128)}), f32[8,128,4]{1,2,0:T(4,128)S(1)}, u32[]{:S(2)}, u32[]{:S(2)}) %all-to-all-start.1) | async-done | bytes 16416 | tf_op jit(solution)/shard_map/all_to_all | solution.py:15
  170.2 7.6 %all-to-all-done.10 = f32[8,1,256]{2,1,0:T(1,128)S(1)} async-done(((f32[8,1,256]{2,1,0:T(1,128)}), f32[8,1,256]{2,1,0:T(1,128)S(1)}, u32[]{:S(2)}, u32[]{:S(2)}) %all-to-all-start.10) | async-done | bytes 8224 | tf_op jit(solution)/shard_map/all_to_all | solution.py:15
  179.2 3.5 all-to-all-start.11
  182.6 5.2 %all-to-all-done.11 = bf16[4,1,64]{2,1,0:T(2,128)(2,1)S(1)} async-done(((bf16[4,1,64]{2,1,0:T(2,128)(2,1)}), bf16[4,1,64]{2,1,0:T(2,128)(2,1)S(1)}, u32[]{:S(2)}, u32[]{:S(2)}) %all-to-all-start.11) | async-done | bytes 544 | tf_op jit(solution)/shard_map/all_to_all | solution.py:165
  190.2 3.4 all-to-all-start.9
  193.7 7.3 %all-to-all-done.9 = bf16[4,1,64,512]{3,2,1,0:T(8,128)(2,1)S(1)} async-done(((bf16[4,1,64,512]{3,2,1,0:T(8,128)(2,1)}), bf16[4,1,64,512]{3,2,1,0:T(8,128)(2,1)S(1)}, u32[]{:S(2)}, u32[]{:S(2)}) %all-to-all-start.9) | async-done | bytes 262176 | tf_op jit(solution)/shard_map/all_to_all | solution.py:164
  207.7 7.5 %all-to-all-done.12 = f32[8,128,1]{1,2,0:T(1,128)S(1)} async-done(((f32[8,128,1]{1,2,0:T(1,128)}), f32[8,128,1]{1,2,0:T(1,128)S(1)}, u32[]{:S(2)}, u32[]{:S(2)}) %all-to-all-start.12) | async-done | bytes 4128 | tf_op jit(solution)/shard_map/all_to_all | solution.py:15
  216.0 9.9 %all_to_all.70 = bf16[4,1,64,512]{3,2,1,0:T(8,128)(2,1)S(1)} all-to-all(bf16[4,1,64,512]{3,2,1,0:T(8,128)(2,1)S(1)} %bitcast.261), channel_id=1, replica_groups=mesh['pipe'=16,'dp'=4,'expert'=8] {'dp'}, dimensions={0} | all-to-all | bytes 524288 | tf_op jit(solution)/shard_map/all_to_all | solution.py:111
  226.2 53.6 %all_to_all.71 = bf16[8,4,1,64,512]{4,3,1,2,0:T(8,128)(2,1)S(1)} all-to-all(bf16[8,4,1,64,512]{4,3,1,2,0:T(8,128)(2,1)S(1)} %broadcast_in_dim.80), channel_id=1, replica_groups=mesh['pipe'=16,'dp'=4,'expert'=8] {'expert'}, dimensions={0} | all-to-all | bytes 4194304 | tf_op jit(solution)/shard_map/all_to_all | solution.py:15
  288.3 5.6 %collective-permute-start.1 = (bf16[128,512]{1,0:T(8,128)(2,1)S(1)}, bf16[128,512]{1,0:T(8,128)(2,1)S(1)}, u32[]{:S(2)}, u32[]{:S(2)}) collective-permute-start(bf16[128,512]{1,0:T(8,128)(2,1)S(1)} %get-tuple-element.21), channel_id=1, source_target_pairs={{32,0},{64,32},{96,64},{128,96},{160,128},{192,160},{224,192},{256... | collective-permute-start | bytes 393224 | tf_op jit(solution)/shard_map/ppermute | solution.py:37
  293.9 34.9 %reduce-scatter.3.cloned.1.call-done = bf16[4,1,64,512]{3,2,0,1:T(8,128)(2,1)} async-done(((bf16[4,1,64,4096]{3,2,0,1:T(8,128)(2,1)}), bf16[4,1,64,512]{3,2,0,1:T(8,128)(2,1)}) %reduce-scatter.3.cloned.1.call-update) | async-done | bytes 262160 | tf_op jit(solution)/shard_map/reduce_scatter | solution.py:106
  328.8 3.4 all-to-all-start.4
  332.3 10.9 %psum.7 = f32[1,512]{1,0:T(1,128)} all-reduce(f32[1,512]{1,0:T(1,128)S(1)} %bitcast.281), channel_id=1, replica_groups=mesh['pipe'=16,'dp'=4,'expert'=8] {'dp'}, use_global_device_ids=true, to_apply=%region_27.29 | all-reduce | flops 512 | bytes 4096 | tf_op jit(solution)/shard_map/psum | solution.py:221
  345.6 3.4 collective-permute-start
  349.7 4.9 %collective-permute-done = bf16[128,512]{1,0:T(8,128)(2,1)S(1)} collective-permute-done((bf16[128,512]{1,0:T(8,128)(2,1)S(1)}, bf16[128,512]{1,0:T(8,128)(2,1)S(1)}, u32[]{:S(2)}, u32[]{:S(2)}) %collective-permute-start) | collective-permute-done | bytes 131104 | tf_op jit(solution)/shard_map/ppermute | solution.py:37
  (146 shorter events, 60.4 us)
Async XLA Ops:
  7.2 118.0 %copy-start = (bf16[1,1,128,4096]{3,2,1,0:T(8,128)(2,1)S(1)}, bf16[1,1,128,4096]{3,2,1,0:T(8,128)(2,1)}, u32[]{:S(2)}) copy-start(bf16[1,1,128,4096]{3,2,1,0:T(8,128)(2,1)} %param.19) | copy-start | bytes 3145732
  8.9 17.9 %all-to-all-start.5 = ((f32[8,128,1]{1,2,0:T(1,128)}), f32[8,128,1]{1,2,0:T(1,128)S(1)}, u32[]{:S(2)}, u32[]{:S(2)}) async-start(f32[8,128,1]{1,2,0:T(1,128)} %broadcast_in_dim.81), calls=%async_computation.6 | async-start | bytes 8192 | tf_op jit(solution)/shard_map/all_to_all | solution.py:15
  19.2 61.5 %all-gather.5.cloned.1.call-start = ((), (), s32[]{:S(2)}) async-start(), calls=%async_computation.17 | async-start | bytes 2359296 | tf_op jit(solution)/shard_map/all_gather | solution.py:136
  20.3 21.2 %copy-start.4 = (bf16[1,128,512]{2,1,0:T(8,128)(2,1)S(1)}, bf16[1,128,512]{2,1,0:T(8,128)(2,1)}, u32[]{:S(2)}) copy-start(bf16[1,128,512]{2,1,0:T(8,128)(2,1)} %param.12) | copy-start | bytes 393220
  28.5 52.2 %copy-start.1 = (bf16[1,1,4096,2,128]{4,3,2,1,0:T(2,128)(2,1)S(1)}, bf16[1,1,4096,2,128]{4,3,2,1,0:T(2,128)(2,1)}, u32[]{:S(2)}) copy-start(bf16[1,1,4096,2,128]{4,3,2,1,0:T(2,128)(2,1)} %param.18) | copy-start | bytes 6291460
  41.5 83.6 %all-gather.3.cloned.1.call-start = ((), (), s32[]{:S(2)}) async-start(), calls=%async_computation.16 | async-start | bytes 2359296 | tf_op jit(solution)/shard_map/all_gather | solution.py:137
  54.4 135.8 %reduce-scatter.5.cloned.1.call-start = ((), (), s32[]{:S(2)}) async-start(), calls=%async_computation.18 | async-start | bytes 2359296 | tf_op jit(solution)/shard_map/reduce_scatter | solution.py:160
  129.7 8.3 %copy-start.3 = (bf16[1,128,512]{2,1,0:T(8,128)(2,1)S(1)}, bf16[1,128,512]{2,1,0:T(8,128)(2,1)}, u32[]{:S(2)}) copy-start(bf16[1,128,512]{2,1,0:T(8,128)(2,1)} %param.13) | copy-start | bytes 393220
  129.7 8.3 %copy-start.8 = (f32[1,512]{1,0:T(1,128)S(1)}, f32[1,512]{1,0:T(1,128)}, u32[]{:S(2)}) copy-start(f32[1,512]{1,0:T(1,128)} %param.16) | copy-start | bytes 6148
  129.7 8.3 %copy-start.11 = (bf16[1,512,4]{1,2,0:T(4,128)(2,1)S(1)}, bf16[1,512,4]{1,2,0:T(4,128)(2,1)}, u32[]{:S(2)}) copy-start(bf16[1,512,4]{1,2,0:T(4,128)(2,1)} %param.17) | copy-start | bytes 12292
  131.3 12.0 %all-to-all-start = ((f32[8,128,1]{1,2,0:T(1,128)}), f32[8,128,1]{1,2,0:T(1,128)S(1)}, u32[]{:S(2)}, u32[]{:S(2)}) async-start(f32[8,128,1]{1,2,0:T(1,128)} %broadcast_in_dim.43), calls=%async_computation | async-start | bytes 8192 | tf_op jit(solution)/shard_map/all_to_all | solution.py:15
  143.9 11.2 %all-to-all-start.6 = ((f32[8,128,4]{1,2,0:T(4,128)}), f32[8,128,4]{1,2,0:T(4,128)S(1)}, u32[]{:S(2)}, u32[]{:S(2)}) async-start(f32[8,128,4]{1,2,0:T(4,128)} %broadcast_in_dim.82), calls=%async_computation.7 | async-start | bytes 32768 | tf_op jit(solution)/shard_map/all_to_all | solution.py:15
  155.7 11.1 %all-to-all-start.1 = ((f32[8,128,4]{1,2,0:T(4,128)}), f32[8,128,4]{1,2,0:T(4,128)S(1)}, u32[]{:S(2)}, u32[]{:S(2)}) async-start(f32[8,128,4]{1,2,0:T(4,128)} %broadcast_in_dim.78), calls=%async_computation.1 | async-start | bytes 32768 | tf_op jit(solution)/shard_map/all_to_all | solution.py:15
  166.8 11.0 %all-to-all-start.10 = ((f32[8,1,256]{2,1,0:T(1,128)}), f32[8,1,256]{2,1,0:T(1,128)S(1)}, u32[]{:S(2)}, u32[]{:S(2)}) async-start(f32[8,1,256]{2,1,0:T(1,128)} %reshape.524), calls=%async_computation.12 | async-start | bytes 16384 | tf_op jit(solution)/shard_map/all_to_all | solution.py:15
  179.2 8.7 %all-to-all-start.11 = ((bf16[4,1,64]{2,1,0:T(2,128)(2,1)}), bf16[4,1,64]{2,1,0:T(2,128)(2,1)S(1)}, u32[]{:S(2)}, u32[]{:S(2)}) async-start(bf16[4,1,64]{2,1,0:T(2,128)(2,1)} %copy.166), calls=%async_computation.13 | async-start | bytes 4096 | tf_op jit(solution)/shard_map/all_to_all | solution.py:165
  190.2 10.9 %all-to-all-start.9 = ((bf16[4,1,64,512]{3,2,1,0:T(8,128)(2,1)}), bf16[4,1,64,512]{3,2,1,0:T(8,128)(2,1)S(1)}, u32[]{:S(2)}, u32[]{:S(2)}) async-start(bf16[4,1,64,512]{3,2,1,0:T(8,128)(2,1)} %bitcast.263), calls=%async_computation.11 | async-start | bytes 524288 | tf_op jit(solution)/shard_map/all_to_all | solution.py:164
  202.2 13.0 %copy-start.5 = (bf16[1,128,512]{2,1,0:T(8,128)(2,1)S(1)}, bf16[1,128,512]{2,1,0:T(8,128)(2,1)}, u32[]{:S(2)}) copy-start(bf16[1,128,512]{2,1,0:T(8,128)(2,1)} %param.12) | copy-start | bytes 393220
  202.2 13.0 %copy-start.10 = (f32[128]{0:T(128)S(1)}, f32[128]{0:T(128)}, u32[]{:S(2)}) copy-start(f32[128]{0:T(128)} %get-tuple-element.25) | copy-start | bytes 1540
  204.3 10.9 %all-to-all-start.12 = ((f32[8,128,1]{1,2,0:T(1,128)}), f32[8,128,1]{1,2,0:T(1,128)S(1)}, u32[]{:S(2)}, u32[]{:S(2)}) async-start(f32[8,128,1]{1,2,0:T(1,128)} %broadcast_in_dim.87), calls=%async_computation.14 | async-start | bytes 8192 | tf_op jit(solution)/shard_map/all_to_all | solution.py:15
  207.7 121.1 %reduce-scatter.3.cloned.1.call-start = ((), (), s32[]{:S(2)}) async-start(), calls=%async_computation.15 | async-start | bytes 2359296 | tf_op jit(solution)/shard_map/reduce_scatter | solution.py:106
  215.4 72.9 %copy-start.6 = (bf16[128,512]{1,0:T(8,128)(2,1)}, bf16[128,512]{1,0:T(8,128)(2,1)S(1)}, u32[]{:S(2)}) copy-start(bf16[128,512]{1,0:T(8,128)(2,1)S(1)} %get-tuple-element.21) | copy-start | bytes 393220
  288.3 54.9 %collective-permute-start.1 = (bf16[128,512]{1,0:T(8,128)(2,1)S(1)}, bf16[128,512]{1,0:T(8,128)(2,1)S(1)}, u32[]{:S(2)}, u32[]{:S(2)}) collective-permute-start(bf16[128,512]{1,0:T(8,128)(2,1)S(1)} %get-tuple-element.21), channel_id=1, source_target_pairs={{32,0},{64,32},{96,64},{128,96},{160,128},{192,160},{224,192},{256... | collective-permute-start | bytes 393224 | tf_op jit(solution)/shard_map/ppermute | solution.py:37
  328.8 14.5 %all-to-all-start.4 = ((bf16[4,1,64,512]{3,2,1,0:T(8,128)(2,1)}), bf16[4,1,64,512]{3,2,1,0:T(8,128)(2,1)S(1)}, u32[]{:S(2)}, u32[]{:S(2)}) async-start(bf16[4,1,64,512]{3,2,1,0:T(8,128)(2,1)} %bitcast.264), calls=%async_computation.5 | async-start | bytes 524288 | tf_op jit(solution)/shard_map/all_to_all | solution.py:109
  345.6 9.0 %collective-permute-start = (bf16[128,512]{1,0:T(8,128)(2,1)S(1)}, bf16[128,512]{1,0:T(8,128)(2,1)S(1)}, u32[]{:S(2)}, u32[]{:S(2)}) collective-permute-start(bf16[128,512]{1,0:T(8,128)(2,1)S(1)} %fusion.51), channel_id=1, source_target_pairs={{0,32},{32,64},{64,96},{96,128},{128,160},{160,192},{192,224},{224... | collective-permute-start | bytes 393224 | tf_op jit(solution)/shard_map/ppermute | solution.py:37
  (3 other events, 13.3 us)
Sparse Core Ops, SparseCore 0:
  41.6 39.0 all-gather.4
  82.8 42.2 all-gather.2
  129.9 44.7 reduce-scatter.4
  288.4 40.3 reduce-scatter.2
where the time goes:
time: 363 us; the launch traced here: 362 us
  waiting for transfers between devices  158 us (44%)
  blocking collectives  95.8 us (26%)
  starting transfers between devices  47.4 us (13%)
  local copies, waits for them, and re-layouts  21.8 us (6%)
  matrix products  15.3 us (4%)
  between operations  14.3 us (4%)
  other arithmetic  9.72 us (3%)
    all_to_all x1, blocking collectives, sent_to_all(): return lax.all_to_all(copies, axis, split_axis=0, concat_axis=0, tiled=True)  53.6 us
    all_gather x1, waiting for transfers between devices, compute(): up_piece = lax.all_gather(up_in, 'expert', axis=3, tiled=True)  41.4 us
    all_to_all x6, waiting for transfers between devices, sent_to_all(): return lax.all_to_all(copies, axis, split_axis=0, concat_axis=0, tiled=True)  38.1 us
    reduce_scatter x2, waiting for transfers between devices, compute(): lax.psum_scatter(partial_value.astype(jnp.bfloat16), 'expert', scatter_di...  34.9 us
    all_to_all x6, starting transfers between devices, sent_to_all(): return lax.all_to_all(copies, axis, split_axis=0, concat_axis=0, tiled=True)  28 us
    all_gather x1, waiting for transfers between devices, compute(): rows_piece = lax.all_gather(rows_in, 'expert', axis=3, tiled=True)  26.3 us
    psum x1, blocking collectives, local(): gain_total = lax.psum(gain_part, 'dp')  10.9 us
    all_to_all x1, blocking collectives, run_backward(): lax.all_to_all(row_buffer, 'dp', split_axis=0, concat_axis=0, tiled=True)  10.8 us
  transfers between devices with their start and end apart: 15, of which 12 were waited for; matrix products, arithmetic and copies ran while one was open for 5% of the time, Pallas kernels for 0%

commit v1 on v0

v1 whole, which is shorter than its diff:
```python
import jax
import jax.numpy as jnp
from jax import lax
from jax.sharding import PartitionSpec as P

D = 4096
ROUTE_SCALE = 2.827
EPSILON = 1e-05
F32 = jnp.float32
BF16 = jnp.bfloat16


def summed_over(values, axis):
    copies = jnp.broadcast_to(values, (lax.axis_size(axis), *values.shape))
    return jnp.sum(lax.all_to_all(copies, axis, split_axis=0, concat_axis=0, tiled=True), axis=0)


def exchanged(blocks, axis):
    return lax.all_to_all(blocks, axis, split_axis=0, concat_axis=0, tiled=True)


def shifted(block, axis, distance):
    devices = range(lax.axis_size(axis))
    route = [(i - distance, i) for i in devices if i - distance in devices]
    return lax.ppermute(block, axis, route)


def slots_of(routes, experts, capacity):
    length = routes.shape[0]
    names = routes.T
    member = (names[:, None, :] == jnp.arange(experts, dtype=jnp.int32)[None, :, None]).astype(F32)
    token = jnp.arange(length, dtype=jnp.int32)
    earlier = (token[:, None] < token[None, :]).astype(BF16)
    before = jnp.dot(
        jnp.sum(member, axis=0).astype(BF16), earlier, preferred_element_type=F32
    )
    position = jnp.sum(member * before[None], axis=1).astype(jnp.int32)
    slot = names * capacity + position
    every = jnp.arange(experts * capacity, dtype=jnp.int32)
    placed = slot[:, None, :] == every[None, :, None]
    return slot, placed, member


def gates_of(squares, raw_logits, member):
    scaling = lax.rsqrt(squares / D + EPSILON)
    chosen = jnp.sum(member * raw_logits[None], axis=1) * scaling[None]
    lifted = jax.nn.sigmoid(chosen)
    lifted_sum = jnp.sum(lifted, axis=0, keepdims=True)
    return scaling, chosen, lifted, lifted_sum, ROUTE_SCALE * lifted / lifted_sum


def split_three(values):
    high = values.astype(BF16)
    rest = values - high.astype(F32)
    middle = rest.astype(BF16)
    low = (rest - middle.astype(F32)).astype(BF16)
    return high, middle, low


def local(
    entering,
    pending,
    stashed_in,
    forward_routes,
    backward_routes,
    norm_gains,
    w_router,
    w_gateup,
    w_down,
):
    gain = norm_gains[0]
    router = w_router[0]
    gate_up = w_gateup[0, 0].reshape(D, -1)
    down_w = w_down[0, 0]
    hidden = down_w.shape[0]
    tokens, stashed, incoming = entering[0], stashed_in[0], pending[0]
    length, width = tokens.shape
    experts = router.shape[1]
    capacity = length * forward_routes.shape[2] // experts

    slot_f, placed_f, member_f = slots_of(forward_routes[0], experts, capacity)
    slot_b, placed_b, member_b = slots_of(backward_routes[0], experts, capacity)
    spread_f = (placed_f[0] | placed_f[1]).astype(BF16)
    spread_b = (placed_b[0] | placed_b[1]).astype(BF16)
    tokens32, stashed32 = tokens.astype(F32), stashed.astype(F32)
    scaled_f = (tokens32 * gain).astype(BF16)
    scaled_b = (stashed32 * gain).astype(BF16)

    def routed(spread, rows):
        return jnp.dot(spread, rows, preferred_element_type=F32).astype(BF16).reshape(
            experts, capacity, width
        )

    sent = jnp.concatenate(
        [routed(spread_f, scaled_f), routed(spread_b, scaled_b), routed(spread_b, incoming)], axis=1
    )
    arrived = exchanged(sent, "dp").reshape(experts, 3, capacity, width)
    slots = experts * capacity
    arrived = arrived.transpose(1, 0, 2, 3).reshape(3 * slots, width)
    whole = lax.all_gather(arrived, "expert", axis=1, tiled=True)

    (scaled_f2, scaled_b2), arrived2 = lax.optimization_barrier(((scaled_f, scaled_b), arrived))

    def sums_of(values32, scaled):
        squares = jnp.sum(values32 * values32, axis=-1)[None]
        logits = lax.dot_general(
            router, scaled, (((0,), (1,)), ((), ())), preferred_element_type=F32
        )
        return [squares, logits]

    sums = jnp.concatenate(
        sums_of(tokens32, scaled_f2)
        + sums_of(stashed32, scaled_b2)
        + [jnp.zeros((16 - 2 * (experts + 1), length), F32)],
        axis=0,
    )
    sums = summed_over(sums, "expert")
    r_f, _, _, _, gates_f = gates_of(sums[0], sums[1 : 1 + experts], member_f)
    r_b, chosen_b, lifted_b, lifted_sum_b, gates_b = gates_of(
        sums[1 + experts], sums[2 + experts : 2 + 2 * experts], member_b
    )

    def by_slot(placed, values):
        return jnp.sum(jnp.where(placed, values[:, None, :], 0.0), axis=(0, 2))

    twice = lambda v: jnp.broadcast_to(v[None], (2, length))
    scalars = jnp.stack(
        [
            by_slot(placed_f, twice(r_f)),
            by_slot(placed_f, gates_f),
            by_slot(placed_b, twice(r_b)),
            by_slot(placed_b, gates_b),
        ]
    )
    scalars = exchanged(scalars.reshape(4, experts, capacity).transpose(1, 0, 2), "dp")
    scalars = scalars.transpose(1, 0, 2).reshape(4, slots)
    row_r = jnp.concatenate([scalars[0], scalars[2]])[:, None]
    row_gate_f, row_r_b, row_gate_b = scalars[1][:, None], scalars[2][:, None], scalars[3][:, None]

    whole, row_r = lax.optimization_barrier((whole, row_r))
    projected = jnp.dot(whole[: 2 * slots], gate_up, preferred_element_type=F32) * row_r
    first, second = projected[:, :hidden], projected[:, hidden:]
    lifted_act = jax.nn.sigmoid(first)
    activated = first * lifted_act
    inner = (activated * second).astype(BF16)
    out_f = jnp.dot(inner[:slots], down_w, preferred_element_type=F32) * row_gate_f
    first, second = first[slots:], second[slots:]
    lifted_act, activated = lifted_act[slots:], activated[slots:]
    weighted = lax.dot_general(
        whole[2 * slots :], down_w, (((1,), (1,)), ((), ())), preferred_element_type=F32
    )
    gate_part = jnp.sum(inner[slots:].astype(F32) * weighted, axis=1)
    grad_first = (weighted * second * lifted_act * (1.0 + first * (1.0 - lifted_act))).astype(BF16)
    grad_second = (weighted * activated).astype(BF16)
    along_part = jnp.sum(
        grad_first.astype(F32) * first + grad_second.astype(F32) * second, axis=1
    )
    grads = jnp.concatenate([grad_first, grad_second], axis=1)
    out_b = (
        lax.dot_general(grads, gate_up, (((1,), (1,)), ((), ())), preferred_element_type=F32)
        * row_gate_b
    )
    partial = jnp.concatenate([out_f.astype(BF16), out_b.astype(BF16)], axis=0)
    summed = lax.psum_scatter(partial, "expert", scatter_dimension=1, tiled=True)

    parts = jnp.stack([gate_part, along_part])
    (parts, _) = lax.optimization_barrier((parts, partial))
    parts = summed_over(parts, "expert")
    parts = exchanged(parts.reshape(2, experts, capacity).transpose(1, 0, 2), "dp")
    parts = parts.transpose(1, 0, 2).reshape(2, slots)

    def by_token(values):
        return jnp.sum(jnp.where(placed_b, values[None, :, None], 0.0), axis=1)

    back_gate = by_token(parts[0].astype(BF16).astype(F32))
    along = by_token(parts[1])
    mixed = jnp.sum(back_gate * lifted_b, axis=0, keepdims=True) / lifted_sum_b
    chosen_cot = ROUTE_SCALE * (back_gate - mixed) / lifted_sum_b * lifted_b * (1.0 - lifted_b)
    logit_cot = jnp.sum(member_b * chosen_cot[:, None, :], axis=0)
    inner_r = jnp.sum(gates_b * along + chosen_cot * chosen_b, axis=0)
    router_part = lax.dot_general(
        logit_cot,
        router.astype(F32),
        (((0,), (1,)), ((), ())),
        precision=lax.Precision.HIGHEST,
        preferred_element_type=F32,
    )
    own_gain = jnp.sum(router_part * stashed32 * r_b[:, None], axis=0)
    base = (
        incoming.astype(F32)
        + (r_b[:, None] * router_part) * gain
        - stashed32 * (r_b * r_b * inner_r / D)[:, None]
    )

    gain_part = own_gain + (
        jnp.sum(
            summed[slots:].astype(F32) * arrived2[slots : 2 * slots].astype(F32) * row_r_b, axis=0
        )
        / gain
    )
    extra = jnp.concatenate(
        [v[None] for v in split_three(gain_part)] + [jnp.zeros((5, width), BF16)], axis=0
    )
    back = jnp.concatenate(
        [
            summed[:slots].reshape(experts, capacity, width),
            summed[slots:].reshape(experts, capacity, width),
            jnp.broadcast_to(extra[None], (experts, 8, width)),
        ],
        axis=1,
    )
    back = exchanged(back, "dp")

    def gathered(spread, rows):
        return lax.dot_general(
            spread,
            rows.reshape(slots, width),
            (((0,), (0,)), ((), ())),
            preferred_element_type=F32,
        )

    produced = (tokens32 + gathered(spread_f, back[:, :capacity])).astype(BF16)
    passed_forward = shifted(produced, "pipe", 1)
    moe_cot = gathered(spread_b, back[:, capacity : 2 * capacity])
    cotangent = (base + (r_b[:, None] * moe_cot) * gain).astype(BF16)
    passed_backward = shifted(cotangent, "pipe", -1)
    gain_total = jnp.sum(back[:, 2 * capacity : 2 * capacity + 3].astype(F32), axis=(0, 1))
    return (
        produced[None],
        cotangent[None],
        passed_forward[None],
        passed_backward[None],
        gain_total[None],
    )


def solution(mesh):
    placed = (
        P("pipe", "dp", "expert"),
        P("pipe", "dp", "expert"),
        P("pipe", "dp", "expert"),
        P("pipe", "dp", None),
        P("pipe", "dp", None),
        P("pipe", "expert"),
        P("pipe", "expert", None),
        P("pipe", "dp", None, None, "expert"),
        P("pipe", "dp", "expert", None),
    )
    return jax.shard_map(
        local,
        mesh=mesh,
        in_specs=placed,
        out_specs=(
            P("pipe", "dp", "expert"),
            P("pipe", "dp", "expert"),
            P("pipe", "dp", "expert"),
            P("pipe", "dp", "expert"),
            P("pipe", "expert"),
        ),
        check_vma=False,
    )
```

time: 363 us -> 222 us (0.61)
  the two profiles are of different devices: /device:TPU:2 before, /device:TPU:24 now
where the time goes in v1:
time: 222 us; the launch traced here: 221 us
  waiting for transfers between devices  105 us (47%)
  blocking collectives  55.2 us (25%)
  starting transfers between devices  15.1 us (7%)
  between operations  14.4 us (6%)
  matrix products  13.2 us (6%)
  other arithmetic  11.8 us (5%)
  local copies, waits for them, and re-layouts  6.02 us (3%)
    all_gather x1, waiting for transfers between devices, local(): whole = lax.all_gather(arrived, 'expert', axis=1, tiled=True)  50.6 us
    reduce_scatter x1, waiting for transfers between devices, local(): lax.psum_scatter(partial, 'expert', scatter_dimension=1, tiled=True)  33.5 us
    all_to_all x2, blocking collectives, summed_over(): lax.all_to_all(copies, axis, split_axis=0, concat_axis=0, tiled=True)  30.2 us
    all_to_all x2, blocking collectives, exchanged(): return lax.all_to_all(blocks, axis, split_axis=0, concat_axis=0, tiled=True)  25 us
    all_to_all x2, waiting for transfers between devices, exchanged(): return lax.all_to_all(blocks, axis, split_axis=0, concat_axis=0, tiled=True)  15.8 us
    all_to_all x2, starting transfers between devices, exchanged(): return lax.all_to_all(blocks, axis, split_axis=0, concat_axis=0, tiled=True)  8.5 us
    ppermute x2, starting transfers between devices, shifted(): return lax.ppermute(block, axis, route)  6.53 us
    ppermute x2, waiting for transfers between devices, shifted(): return lax.ppermute(block, axis, route)  5.54 us
  transfers between devices with their start and end apart: 6, of which 5 were waited for; matrix products, arithmetic and copies ran while one was open for 3% of the time, Pallas kernels for 0%

profile of v1, /device:TPU:24, one launch (start us, length us, event | category | flops | bytes accessed | tf_op | source)
XLA Modules:
  0.0 221.1 jit_solution(4778950045408556634)
XLA Ops:
  11.8 1.1 convolution_convert_fusion
  13.0 1.2 convolution_convert_fusion.1
  14.1 1.1 convolution_convert_fusion.2
  15.4 17.3 %all_to_all.30 = bf16[4,192,512]{2,1,0:T(8,128)(2,1)S(1)} all-to-all(bf16[4,192,512]{2,1,0:T(8,128)(2,1)S(1)} %pad_maximum_fusion.1), channel_id=1, replica_groups=mesh['pipe'=16,'dp'=4,'expert'=8] {'dp'}, dimensions={0} | all-to-all | bytes 1572864 | tf_op jit(solution)/shard_map/all_to_all | solution.py:19
  32.7 0.9 copy.21
  34.4 18.5 %all_to_all.31 = f32[8,16,128]{2,1,0:T(8,128)S(1)} all-to-all(f32[8,16,128]{2,1,0:T(8,128)S(1)} %broadcast_in_dim.127), channel_id=1, replica_groups=mesh['pipe'=16,'dp'=4,'expert'=8] {'expert'}, dimensions={0} | all-to-all | bytes 131072 | tf_op jit(solution)/shard_map/all_to_all | solution.py:15
  53.8 7.6 %all_to_all.32 = f32[4,1,256]{2,1,0:T(1,128)S(1)} all-to-all(f32[4,1,256]{2,1,0:T(1,128)S(1)} %reshape.297), channel_id=1, replica_groups=mesh['pipe'=16,'dp'=4,'expert'=8] {'dp'}, dimensions={0} | all-to-all | bytes 8192 | tf_op jit(solution)/shard_map/all_to_all | solution.py:19
  63.0 50.6 %all-gather.2.cloned.1.call-done = bf16[768,4096]{1,0:T(8,128)(2,1)} async-done(((bf16[768,512]{1,0:T(8,128)(2,1)}), bf16[768,4096]{1,0:T(8,128)(2,1)}) %all-gather.2.cloned.1.call-update) | async-done | bytes 6291472 | tf_op jit(solution)/shard_map/all_gather | solution.py:100
  113.7 4.2 %fusion.10 = f32[512,256]{0,1:T(8,128)S(1)} fusion(bf16[512,8,2,128]{3,2,1,0:T(2,128)(2,1)} %bitcast.167, bf16[768,4096]{1,0:T(8,128)(2,1)} %all-gather.2.cloned.1.call-done, f32[512]{0:T(512)S(1)} %pad_maximum_fusion.3), kind=kOutput, calls=%fused_computation.13 | convolution fusion | flops 1073872896 | bytes 6817792 | tf_op jit(solution)/shard_map/dot_general | solution.py:141
  118.7 2.6 %add_reduce_fusion = (f32[256]{0:T(256)S(1)}, bf16[256,128]{0,1:T(8,128)(2,1)S(1)}, bf16[256,128]{0,1:T(8,128)(2,1)S(1)}, f32[256]{0:T(256)S(1)}) fusion(f32[512,256]{0,1:T(8,128)S(1)} %fusion.10, f32[512,128]{0,1:T(8,128)S(1)} %get-tuple-element.46, f32[512,128]{0,1:T(8,128)S(1)} %get-tuple-element.45, bf16[512,128]{0,1:T(8,128)(2,1)S(1)} %get-tuple-element.44, ...), kind=kOutput, calls=%fused_computation.69 | convolution fusion | flops 269024768 | bytes 3868672 | tf_op jit(solution)/shard_map/dot_general | solution.py:149
  121.3 0.9 fusion.1
  122.2 2.4 %pad_maximum_fusion = bf16[512,4096]{1,0:T(8,128)(2,1)} fusion(bf16[256,4096]{1,0:T(8,128)(2,1)S(1)} %fusion.1, bf16[256,4096]{1,0:T(8,128)(2,1)S(1)} %fusion), kind=kLoop, calls=%fused_computation.4 | loop fusion | flops 8388608 | bytes 8388608 | tf_op jit(solution)/shard_map/concatenate | solution.py:163
  124.7 11.7 %all_to_all.33 = f32[8,2,256]{2,1,0:T(2,128)S(1)} all-to-all(f32[8,2,256]{2,1,0:T(2,128)S(1)} %broadcast_in_dim.134), channel_id=1, replica_groups=mesh['pipe'=16,'dp'=4,'expert'=8] {'expert'}, dimensions={0} | all-to-all | bytes 32768 | tf_op jit(solution)/shard_map/all_to_all | solution.py:15
  137.2 4.2 %all-to-all-start.4 = ((f32[4,1,128]{2,1,0:T(1,128)}), f32[4,1,128]{2,1,0:T(1,128)S(1)}, u32[]{:S(2)}, u32[]{:S(2)}) async-start(f32[4,1,128]{2,1,0:T(1,128)} %reshape.299), calls=%async_computation.5 | async-start | bytes 4096 | tf_op jit(solution)/shard_map/all_to_all | solution.py:19
  141.5 5.1 %all-to-all-done.4 = f32[4,1,128]{2,1,0:T(1,128)S(1)} async-done(((f32[4,1,128]{2,1,0:T(1,128)}), f32[4,1,128]{2,1,0:T(1,128)S(1)}, u32[]{:S(2)}, u32[]{:S(2)}) %all-to-all-start.4) | async-done | bytes 2080 | tf_op jit(solution)/shard_map/all_to_all | solution.py:19
  148.1 33.5 %reduce-scatter.2.cloned.1.call-done = bf16[512,512]{1,0:T(8,128)(2,1)} async-done(((bf16[512,4096]{1,0:T(8,128)(2,1)}), bf16[512,512]{1,0:T(8,128)(2,1)}) %reduce-scatter.2.cloned.1.call-update) | async-done | bytes 524304 | tf_op jit(solution)/shard_map/reduce_scatter | solution.py:164
  181.6 1.1 multiply_reduce_fusion
  182.9 1.1 fusion.81
  184.0 0.8 pad_maximum_fusion.2
  184.8 4.2 %all-to-all-start.5 = ((bf16[4,136,512]{2,1,0:T(8,128)(2,1)}), bf16[4,136,512]{2,1,0:T(8,128)(2,1)S(1)}, u32[]{:S(2)}, u32[]{:S(2)}) async-start(bf16[4,136,512]{2,1,0:T(8,128)(2,1)} %pad_maximum_fusion.2), calls=%async_computation.6 | async-start | bytes 1114112 | tf_op jit(solution)/shard_map/all_to_all | solution.py:19
  189.1 10.7 %all-to-all-done.5 = bf16[4,136,512]{2,1,0:T(8,128)(2,1)S(1)} async-done(((bf16[4,136,512]{2,1,0:T(8,128)(2,1)}), bf16[4,136,512]{2,1,0:T(8,128)(2,1)S(1)}, u32[]{:S(2)}, u32[]{:S(2)}) %all-to-all-start.5) | async-done | bytes 557088 | tf_op jit(solution)/shard_map/all_to_all | solution.py:19
  200.0 4.6 %collective-permute-start = (bf16[128,512]{1,0:T(8,128)(2,1)S(1)}, bf16[128,512]{1,0:T(8,128)(2,1)S(1)}, u32[]{:S(2)}, u32[]{:S(2)}) collective-permute-start(bf16[128,512]{1,0:T(8,128)(2,1)S(1)} %fusion.17), channel_id=1, source_target_pairs={{0,32},{32,64},{64,96},{96,128},{128,160},{160,192},{192,224},{224... | collective-permute-start | bytes 393224 | tf_op jit(solution)/shard_map/ppermute | solution.py:25
  204.9 1.9 collective-permute-start.1
  207.4 5.5 %collective-permute-done.1 = bf16[128,512]{1,0:T(8,128)(2,1)S(1)} collective-permute-done((bf16[128,512]{1,0:T(8,128)(2,1)S(1)}, bf16[128,512]{1,0:T(8,128)(2,1)S(1)}, u32[]{:S(2)}, u32[]{:S(2)}) %collective-permute-start.1) | collective-permute-done | bytes 131104 | tf_op jit(solution)/shard_map/ppermute | solution.py:25
  (101 shorter events, 13.6 us)
Async XLA Ops:
  7.2 110.8 %copy-start = (bf16[1,1,128,4096]{3,2,1,0:T(8,128)(2,1)S(1)}, bf16[1,1,128,4096]{3,2,1,0:T(8,128)(2,1)}, u32[]{:S(2)}) copy-start(bf16[1,1,128,4096]{3,2,1,0:T(8,128)(2,1)} %param.17) | copy-start | bytes 3145732
  7.2 106.5 %all-gather.2.cloned.1.call-start = ((), (), s32[]{:S(2)}) async-start(), calls=%async_computation.7 | async-start | bytes 7077888 | tf_op jit(solution)/shard_map/all_gather | solution.py:100
  15.3 18.4 %copy-start.1 = (bf16[1,128,512]{2,1,0:T(8,128)(2,1)S(1)}, bf16[1,128,512]{2,1,0:T(8,128)(2,1)}, u32[]{:S(2)}) copy-start(bf16[1,128,512]{2,1,0:T(8,128)(2,1)} %param.9) | copy-start | bytes 393220
  15.3 18.4 %copy-start.2 = (bf16[1,128,512]{2,1,0:T(8,128)(2,1)S(1)}, bf16[1,128,512]{2,1,0:T(8,128)(2,1)}, u32[]{:S(2)}) copy-start(bf16[1,128,512]{2,1,0:T(8,128)(2,1)} %param.11) | copy-start | bytes 393220
  15.3 18.4 %copy-start.6 = (f32[1,512]{1,0:T(1,128)S(1)}, f32[1,512]{1,0:T(1,128)}, u32[]{:S(2)}) copy-start(f32[1,512]{1,0:T(1,128)} %param.14) | copy-start | bytes 6148
  15.4 18.6 %copy-start.5 = (bf16[1,512,4]{1,2,0:T(4,128)(2,1)S(1)}, bf16[1,512,4]{1,2,0:T(4,128)(2,1)}, u32[]{:S(2)}) copy-start(bf16[1,512,4]{1,2,0:T(4,128)(2,1)} %param.15) | copy-start | bytes 12292
  32.7 20.1 %copy-start.8 = (s32[1,128,2]{1,2,0:T(2,128)S(1)}, s32[1,128,2]{1,2,0:T(2,128)}, u32[]{:S(2)}) copy-start(s32[1,128,2]{1,2,0:T(2,128)} %param.12) | copy-start | bytes 3076
  32.7 20.2 %copy-start.7 = (s32[1,128,2]{1,2,0:T(2,128)S(1)}, s32[1,128,2]{1,2,0:T(2,128)}, u32[]{:S(2)}) copy-start(s32[1,128,2]{1,2,0:T(2,128)} %param.13) | copy-start | bytes 3076
  33.7 147.9 %reduce-scatter.2.cloned.1.call-start = ((), (), s32[]{:S(2)}) async-start(), calls=%async_computation.8 | async-start | bytes 4718592 | tf_op jit(solution)/shard_map/reduce_scatter | solution.py:164
  118.7 2.6 %copy-start.9 = (bf16[1,1,4096,2,128]{4,3,2,1,0:T(2,128)(2,1)S(1)}, bf16[1,1,4096,2,128]{4,3,2,1,0:T(2,128)(2,1)}, u32[]{:S(2)}) copy-start(bf16[1,1,4096,2,128]{4,3,2,1,0:T(2,128)(2,1)} %param.16) | copy-start | bytes 6291460
  137.2 9.5 %all-to-all-start.4 = ((f32[4,1,128]{2,1,0:T(1,128)}), f32[4,1,128]{2,1,0:T(1,128)S(1)}, u32[]{:S(2)}, u32[]{:S(2)}) async-start(f32[4,1,128]{2,1,0:T(1,128)} %reshape.299), calls=%async_computation.5 | async-start | bytes 4096 | tf_op jit(solution)/shard_map/all_to_all | solution.py:19
  183.9 20.7 %copy-start.4 = (bf16[1,128,512]{2,1,0:T(8,128)(2,1)S(1)}, bf16[1,128,512]{2,1,0:T(8,128)(2,1)}, u32[]{:S(2)}) copy-start(bf16[1,128,512]{2,1,0:T(8,128)(2,1)} %param.10) | copy-start | bytes 393220
  184.8 14.9 %all-to-all-start.5 = ((bf16[4,136,512]{2,1,0:T(8,128)(2,1)}), bf16[4,136,512]{2,1,0:T(8,128)(2,1)S(1)}, u32[]{:S(2)}, u32[]{:S(2)}) async-start(bf16[4,136,512]{2,1,0:T(8,128)(2,1)} %pad_maximum_fusion.2), calls=%async_computation.6 | async-start | bytes 1114112 | tf_op jit(solution)/shard_map/all_to_all | solution.py:19
  200.0 14.3 %copy-start.3 = (bf16[128,512]{1,0:T(8,128)(2,1)}, bf16[128,512]{1,0:T(8,128)(2,1)S(1)}, u32[]{:S(2)}) copy-start(bf16[128,512]{1,0:T(8,128)(2,1)S(1)} %fusion.17) | copy-start | bytes 393220
  200.0 7.4 %collective-permute-start = (bf16[128,512]{1,0:T(8,128)(2,1)S(1)}, bf16[128,512]{1,0:T(8,128)(2,1)S(1)}, u32[]{:S(2)}, u32[]{:S(2)}) collective-permute-start(bf16[128,512]{1,0:T(8,128)(2,1)S(1)} %fusion.17), channel_id=1, source_target_pairs={{0,32},{32,64},{64,96},{96,128},{128,160},{160,192},{192,224},{224... | collective-permute-start | bytes 393224 | tf_op jit(solution)/shard_map/ppermute | solution.py:25
  204.9 9.4 %copy-start.10 = (bf16[128,512]{1,0:T(8,128)(2,1)}, bf16[128,512]{1,0:T(8,128)(2,1)S(1)}, u32[]{:S(2)}) copy-start(bf16[128,512]{1,0:T(8,128)(2,1)S(1)} %fusion.18) | copy-start | bytes 393220
  204.9 8.1 %collective-permute-start.1 = (bf16[128,512]{1,0:T(8,128)(2,1)S(1)}, bf16[128,512]{1,0:T(8,128)(2,1)S(1)}, u32[]{:S(2)}, u32[]{:S(2)}) collective-permute-start(bf16[128,512]{1,0:T(8,128)(2,1)S(1)} %fusion.18), channel_id=1, source_target_pairs={{32,0},{64,32},{96,64},{128,96},{160,128},{192,160},{224,192},{256... | collective-permute-start | bytes 393224 | tf_op jit(solution)/shard_map/ppermute | solution.py:25
Sparse Core Ops, SparseCore 0:
  33.8 79.7 all-gather.1
  124.8 56.8 reduce-scatter.1

commit v2 on v1

--- a/solution.py
+++ b/solution.py
@@ -1,6 +1,8 @@
 import jax
 import jax.numpy as jnp
 from jax import lax
+from jax.experimental import pallas as pl
+from jax.experimental.pallas import tpu as pltpu
 from jax.sharding import PartitionSpec as P
 
 D = 4096
@@ -23,6 +25,11 @@
     devices = range(lax.axis_size(axis))
     route = [(i - distance, i) for i in devices if i - distance in devices]
     return lax.ppermute(block, axis, route)
+
+
+def rotated(block, axis, distance):
+    size = lax.axis_size(axis)
+    return lax.ppermute(block, axis, [(i, (i + distance) % size) for i in range(size)])
 
 
 def slots_of(routes, experts, capacity):
@@ -49,12 +56,129 @@
     return scaling, chosen, lifted, lifted_sum, ROUTE_SCALE * lifted / lifted_sum
 
 
-def split_three(values):
-    high = values.astype(BF16)
-    rest = values - high.astype(F32)
-    middle = rest.astype(BF16)
-    low = (rest - middle.astype(F32)).astype(BF16)
-    return high, middle, low
+def dispatch_kernel(routes_f, routes_b, gain, tokens, stashed, incoming, sent):
+    experts, _, width = sent.shape
+    length = tokens.shape[0]
+    capacity = sent.shape[1] // 3
+    shape = (2 * experts, length)
+    row = lax.broadcasted_iota(jnp.int32, shape, 0)
+    forward = row < experts
+    expert = jnp.where(forward, row, row - experts)
+
+    def named(k):
+        return (
+            jnp.where(
+                forward,
+                jnp.broadcast_to(routes_f[k : k + 1, :], shape),
+                jnp.broadcast_to(routes_b[k : k + 1, :], shape),
+            )
+            == expert
+        )
+
+    member = named(0) | named(1)
+    square = (length, length)
+    earlier = jnp.where(
+        lax.broadcasted_iota(jnp.int32, square, 0) < lax.broadcasted_iota(jnp.int32, square, 1),
+        1.0,
+        0.0,
+    ).astype(BF16)
+    before = jnp.dot(
+        jnp.where(member, 1.0, 0.0).astype(BF16), earlier, preferred_element_type=F32
+    )
+    place = jnp.where(member, before.astype(jnp.int32), -1)
+    slot = lax.broadcasted_iota(jnp.int32, (capacity, length), 0)
+
+    def spread(first):
+        return jnp.concatenate(
+            [
+                jnp.where(slot == place[e : e + 1, :], 1.0, 0.0).astype(BF16)
+                for e in range(first, first + experts)
+            ],
+            axis=0,
+        )
+
+    spread_f, spread_b = spread(0), spread(experts)
+    scaled_f = (tokens[...].astype(F32) * gain[...]).astype(BF16)
+    scaled_b = (stashed[...].astype(F32) * gain[...]).astype(BF16)
+    for k, (moved, rows) in enumerate(
+        ((spread_f, scaled_f), (spread_b, scaled_b), (spread_b, incoming[...]))
+    ):
+        routed = jnp.dot(moved, rows, preferred_element_type=F32).astype(BF16)
+        for e in range(experts):
+            sent[e, k * capacity : (k + 1) * capacity, :] = routed[
+                e * capacity : (e + 1) * capacity
+            ]
+
+
+def expert_kernel(
+    whole, gate_up, down_w, row_r, row_gate, partial, gate_part, along_part, rows, outs, sums, took, left
+):
+    pieces, experts, _, width = whole.shape
+    capacity = whole.shape[2] // 3
+    slots = experts * capacity
+    hidden = down_w.shape[0]
+
+    def fetch(z, k):
+        return pltpu.make_async_copy(
+            whole.at[z, :, pl.ds(k * capacity, capacity), :], rows.at[z, k], took.at[z, k]
+        )
+
+    def put(z, k):
+        return pltpu.make_async_copy(
+            outs.at[z, k], partial.at[z, :, pl.ds(k * capacity, capacity), :], left.at[z, k]
+        )
+
+    for z in range(pieces):
+        for k in range(3):
+            fetch(z, k).start()
+    weighted = None
+    for z in range(pieces):
+        part = slice(z * width, (z + 1) * width)
+        for k in range(3):
+            fetch(z, k).wait()
+        values = rows[z, 0:2].reshape(2 * slots, width)
+        product = jnp.dot(values, gate_up[part, :], preferred_element_type=F32)
+        incoming = rows[z, 2].reshape(slots, width)
+        product_w = lax.dot_general(
+            incoming, down_w[:, part], (((1,), (1,)), ((), ())), preferred_element_type=F32
+        )
+        if z == 0:
+            sums[...] = product
+            weighted = product_w
+        else:
+            sums[...] += product
+            weighted += product_w
+    first = sums[:, :hidden] * row_r[...]
+    second = sums[:, hidden:] * row_r[...]
+    lifted = jax.nn.sigmoid(first)
+    activated = first * lifted
+    inner = (activated * second).astype(BF16)
+    inner_f = inner[:slots]
+    first, second, lifted, activated = first[slots:], second[slots:], lifted[slots:], activated[slots:]
+    gate_part[...] = jnp.sum(inner[slots:].astype(F32) * weighted, axis=1, keepdims=True)
+    grad_first = (weighted * second * lifted * (1.0 + first * (1.0 - lifted))).astype(BF16)
+    grad_second = (weighted * activated).astype(BF16)
+    along_part[...] = jnp.sum(
+        grad_first.astype(F32) * first + grad_second.astype(F32) * second, axis=1, keepdims=True
+    )
+    grads = jnp.concatenate([grad_first, grad_second], axis=1)
+    gate_f, gate_b = row_gate[:slots], row_gate[slots:]
+    for z in range(pieces):
+        part = slice(z * width, (z + 1) * width)
+        out_f = jnp.dot(inner_f, down_w[:, part], preferred_element_type=F32) * gate_f
+        outs[z, 0] = out_f.astype(BF16).reshape(experts, capacity, width)
+        put(z, 0).start()
+        out_b = (
+            lax.dot_general(
+                grads, gate_up[part, :], (((1,), (1,)), ((), ())), preferred_element_type=F32
+            )
+            * gate_b
+        )
+        outs[z, 1] = out_b.astype(BF16).reshape(experts, capacity, width)
+        put(z, 1).start()
+    for z in range(pieces):
+        for k in range(2):
+            put(z, k).wait()
 
 
 def local(
@@ -78,28 +202,36 @@
     experts = router.shape[1]
     capacity = length * forward_routes.shape[2] // experts
 
-    slot_f, placed_f, member_f = slots_of(forward_routes[0], experts, capacity)
-    slot_b, placed_b, member_b = slots_of(backward_routes[0], experts, capacity)
+    slots = experts * capacity
+    pieces = lax.axis_size("expert")
+    vmem = pl.BlockSpec(memory_space=pltpu.VMEM)
+    hbm = pl.BlockSpec(memory_space=pl.ANY)
+    sent = pl.pallas_call(
+        dispatch_kernel,
+        out_shape=jax.ShapeDtypeStruct((experts, 3 * capacity, width), BF16),
+        in_specs=[vmem] * 6,
+        out_specs=vmem,
+    )(
+        forward_routes[0].T,
+        backward_routes[0].T,
+        gain[None],
+        tokens,
+        stashed,
+        incoming,
+    )
+    arrived = exchanged(sent, "dp")
+    whole = lax.all_gather(arrived.reshape(3 * slots, width), "expert", axis=0, tiled=True)
+
+    (tokens, stashed, incoming, gain, routes_f, routes_b), arrived2 = lax.optimization_barrier(
+        ((tokens, stashed, incoming, gain, forward_routes[0], backward_routes[0]), arrived)
+    )
+    slot_f, placed_f, member_f = slots_of(routes_f, experts, capacity)
+    slot_b, placed_b, member_b = slots_of(routes_b, experts, capacity)
     spread_f = (placed_f[0] | placed_f[1]).astype(BF16)
     spread_b = (placed_b[0] | placed_b[1]).astype(BF16)
     tokens32, stashed32 = tokens.astype(F32), stashed.astype(F32)
-    scaled_f = (tokens32 * gain).astype(BF16)
-    scaled_b = (stashed32 * gain).astype(BF16)
-
-    def routed(spread, rows):
-        return jnp.dot(spread, rows, preferred_element_type=F32).astype(BF16).reshape(
-            experts, capacity, width
-        )
-
-    sent = jnp.concatenate(
-        [routed(spread_f, scaled_f), routed(spread_b, scaled_b), routed(spread_b, incoming)], axis=1
-    )
-    arrived = exchanged(sent, "dp").reshape(experts, 3, capacity, width)
-    slots = experts * capacity
-    arrived = arrived.transpose(1, 0, 2, 3).reshape(3 * slots, width)
-    whole = lax.all_gather(arrived, "expert", axis=1, tiled=True)
-
-    (scaled_f2, scaled_b2), arrived2 = lax.optimization_barrier(((scaled_f, scaled_b), arrived))
+    scaled_f2 = (tokens32 * gain).astype(BF16)
+    scaled_b2 = (stashed32 * gain).astype(BF16)
 
     def sums_of(values32, scaled):
         squares = jnp.sum(values32 * values32, axis=-1)[None]
@@ -135,36 +267,32 @@
     scalars = exchanged(scalars.reshape(4, experts, capacity).transpose(1, 0, 2), "dp")
     scalars = scalars.transpose(1, 0, 2).reshape(4, slots)
     row_r = jnp.concatenate([scalars[0], scalars[2]])[:, None]
-    row_gate_f, row_r_b, row_gate_b = scalars[1][:, None], scalars[2][:, None], scalars[3][:, None]
-
-    whole, row_r = lax.optimization_barrier((whole, row_r))
-    projected = jnp.dot(whole[: 2 * slots], gate_up, preferred_element_type=F32) * row_r
-    first, second = projected[:, :hidden], projected[:, hidden:]
-    lifted_act = jax.nn.sigmoid(first)
-    activated = first * lifted_act
-    inner = (activated * second).astype(BF16)
-    out_f = jnp.dot(inner[:slots], down_w, preferred_element_type=F32) * row_gate_f
-    first, second = first[slots:], second[slots:]
-    lifted_act, activated = lifted_act[slots:], activated[slots:]
-    weighted = lax.dot_general(
-        whole[2 * slots :], down_w, (((1,), (1,)), ((), ())), preferred_element_type=F32
-    )
-    gate_part = jnp.sum(inner[slots:].astype(F32) * weighted, axis=1)
-    grad_first = (weighted * second * lifted_act * (1.0 + first * (1.0 - lifted_act))).astype(BF16)
-    grad_second = (weighted * activated).astype(BF16)
-    along_part = jnp.sum(
-        grad_first.astype(F32) * first + grad_second.astype(F32) * second, axis=1
-    )
-    grads = jnp.concatenate([grad_first, grad_second], axis=1)
-    out_b = (
-        lax.dot_general(grads, gate_up, (((1,), (1,)), ((), ())), preferred_element_type=F32)
-        * row_gate_b
-    )
-    partial = jnp.concatenate([out_f.astype(BF16), out_b.astype(BF16)], axis=0)
-    summed = lax.psum_scatter(partial, "expert", scatter_dimension=1, tiled=True)
-
-    parts = jnp.stack([gate_part, along_part])
-    (parts, _) = lax.optimization_barrier((parts, partial))
+    row_gate = jnp.concatenate([scalars[1], scalars[3]])[:, None]
+    row_r_b = scalars[2].reshape(experts, capacity, 1)
+
+    partial, gate_part, along_part = pl.pallas_call(
+        expert_kernel,
+        out_shape=(
+            jax.ShapeDtypeStruct((pieces, experts, 2 * capacity, width), BF16),
+            jax.ShapeDtypeStruct((slots, 1), F32),
+            jax.ShapeDtypeStruct((slots, 1), F32),
+        ),
+        in_specs=[hbm] + [vmem] * 4,
+        out_specs=(hbm, vmem, vmem),
+        scratch_shapes=[
+            pltpu.VMEM((pieces, 3, experts, capacity, width), BF16),
+            pltpu.VMEM((pieces, 2, experts, capacity, width), BF16),
+            pltpu.VMEM((2 * slots, 2 * hidden), F32),
+            pltpu.SemaphoreType.DMA((pieces, 3)),
+            pltpu.SemaphoreType.DMA((pieces, 2)),
+        ],
+    )(whole.reshape(pieces, experts, 3 * capacity, width), gate_up, down_w, row_r, row_gate)
+    summed = lax.psum_scatter(
+        partial.reshape(pieces * 2 * slots, width), "expert", scatter_dimension=0, tiled=True
+    )
+    summed = summed.reshape(experts, 2 * capacity, width)
+
+    parts = jnp.stack([gate_part[:, 0], along_part[:, 0]])
     parts = summed_over(parts, "expert")
     parts = exchanged(parts.reshape(2, experts, capacity).transpose(1, 0, 2), "dp")
     parts = parts.transpose(1, 0, 2).reshape(2, slots)
@@ -192,24 +320,19 @@
         - stashed32 * (r_b * r_b * inner_r / D)[:, None]
     )
 
+    back = exchanged(summed, "dp")
     gain_part = own_gain + (
         jnp.sum(
-            summed[slots:].astype(F32) * arrived2[slots : 2 * slots].astype(F32) * row_r_b, axis=0
+            summed[:, capacity:].astype(F32)
+            * arrived2[:, capacity : 2 * capacity].astype(F32)
+            * row_r_b,
+            axis=(0, 1),
         )
         / gain
     )
-    extra = jnp.concatenate(
-        [v[None] for v in split_three(gain_part)] + [jnp.zeros((5, width), BF16)], axis=0
-    )
-    back = jnp.concatenate(
-        [
-            summed[:slots].reshape(experts, capacity, width),
-            summed[slots:].reshape(experts, capacity, width),
-            jnp.broadcast_to(extra[None], (experts, 8, width)),
-        ],
-        axis=1,
-    )
-    back = exchanged(back, "dp")
+    others = [rotated(gain_part[None], "dp", distance) for distance in range(1, experts)]
+    back, others = lax.optimization_barrier((back, others))
+    gain_total = gain_part + sum(other[0] for other in others)
 
     def gathered(spread, rows):
         return lax.dot_general(
@@ -224,7 +347,6 @@
     moe_cot = gathered(spread_b, back[:, capacity : 2 * capacity])
     cotangent = (base + (r_b[:, None] * moe_cot) * gain).astype(BF16)
     passed_backward = shifted(cotangent, "pipe", -1)
-    gain_total = jnp.sum(back[:, 2 * capacity : 2 * capacity + 3].astype(F32), axis=(0, 1))
     return (
         produced[None],
         cotangent[None],

time: 222 us -> 217 us (0.977)
  the two profiles are of different devices: /device:TPU:24 before, /device:TPU:2 now
where the time goes in v2:
time: 217 us
  waiting for transfers between devices  110 us (51%)
  starting transfers between devices  44.1 us (20%)
  blocking collectives  17.4 us (8%)
  between operations  14.4 us (7%)
  Pallas kernels  12 us (6%)
  local copies, waits for them, and re-layouts  9.85 us (5%)
  other arithmetic  5.28 us (2%)
  matrix products  3.2 us (1%)
    all_gather x1, waiting for transfers between devices, local(): lax.all_gather(arrived.reshape(3 * slots, width), 'expert', axis=0, tiled...  45 us
    reduce_scatter x1, waiting for transfers between devices, local(): lax.psum_scatter(partial.reshape(pieces * 2 * slots, width), 'expert', sc...  32.5 us
    all_to_all x1, blocking collectives, exchanged(): return lax.all_to_all(blocks, axis, split_axis=0, concat_axis=0, tiled=True)  17.4 us
    all_to_all x2, waiting for transfers between devices, summed_over(): lax.all_to_all(copies, axis, split_axis=0, concat_axis=0, tiled=True)  15.9 us
    all_to_all x2, starting transfers between devices, summed_over(): lax.all_to_all(copies, axis, split_axis=0, concat_axis=0, tiled=True)  14.4 us
    ppermute x3, starting transfers between devices, rotated(): lax.ppermute(block, axis, [(i, (i + distance) % size) for i in range(size)])  12.2 us
    all_to_all x3, starting transfers between devices, exchanged(): return lax.all_to_all(blocks, axis, split_axis=0, concat_axis=0, tiled=True)  10.1 us
    pallas_call x1, Pallas kernels, local(): pl.pallas_call(expert_kernel, out_shape=(jax.ShapeDtypeStruct((pieces, ex...  9.38 us
  transfers between devices with their start and end apart: 12, of which 9 were waited for; matrix products, arithmetic and copies ran while one was open for 7% of the time, Pallas kernels for 0%

profile of v2, /device:TPU:2, one launch (start us, length us, event | category | flops | bytes accessed | tf_op | source)
XLA Modules:
  0.0 216.7 jit_solution(13337269850634367200)
XLA Ops:
  7.3 2.6 %shard_map.128 = bf16[4,192,512]{2,1,0:T(8,128)(2,1)} custom-call(s32[2,128]{1,0:T(2,128)} %bitcast.105, s32[2,128]{1,0:T(2,128)} %bitcast.100, f32[1,512]{1,0:T(1,128)} %gain.1, bf16[128,512]{1,0:T(8,128)(2,1)} %bitcast.80, bf16[128,512]{1,0:T(8,128)(2,1)} %bitcast.84, bf16[128,512]{1,0:T(8,128)(2,1)} %bitcast.94), custom_call_target="tpu_custom_call" | custom-call | tf_op jit(solution)/shard_map/pallas_call | solution.py:209
  9.8 17.4 %all_to_all.30 = bf16[4,192,512]{2,1,0:T(8,128)(2,1)} all-to-all(bf16[4,192,512]{2,1,0:T(8,128)(2,1)} %shard_map.128), channel_id=1, replica_groups=mesh['pipe'=16,'dp'=4,'expert'=8] {'dp'}, dimensions={0} | all-to-all | bytes 1572864 | tf_op jit(solution)/shard_map/all_to_all | solution.py:21
  27.3 1.1 fusion.4
  31.2 10.3 %all-to-all-start.1 = ((f32[8,16,128]{2,1,0:T(8,128)}), f32[8,16,128]{2,1,0:T(8,128)S(1)}, u32[]{:S(2)}, u32[]{:S(2)}) async-start(f32[8,16,128]{2,1,0:T(8,128)} %broadcast_in_dim.127), calls=%async_computation.1 | async-start | bytes 131072 | tf_op jit(solution)/shard_map/all_to_all | solution.py:17
  41.9 8.2 %all-to-all-done.1 = f32[8,16,128]{2,1,0:T(8,128)S(1)} async-done(((f32[8,16,128]{2,1,0:T(8,128)}), f32[8,16,128]{2,1,0:T(8,128)S(1)}, u32[]{:S(2)}, u32[]{:S(2)}) %all-to-all-start.1) | async-done | bytes 65568 | tf_op jit(solution)/shard_map/all_to_all | solution.py:17
  51.6 3.2 %all-to-all-start.2 = ((f32[4,1,256]{2,1,0:T(1,128)}), f32[4,1,256]{2,1,0:T(1,128)S(1)}, u32[]{:S(2)}, u32[]{:S(2)}) async-start(f32[4,1,256]{2,1,0:T(1,128)} %reshape.258), calls=%async_computation.2 | async-start | bytes 8192 | tf_op jit(solution)/shard_map/all_to_all | solution.py:21
  54.9 1.6 copy.31
  56.4 3.6 %all-to-all-done.2 = f32[4,1,256]{2,1,0:T(1,128)S(1)} async-done(((f32[4,1,256]{2,1,0:T(1,128)}), f32[4,1,256]{2,1,0:T(1,128)S(1)}, u32[]{:S(2)}, u32[]{:S(2)}) %all-to-all-start.2) | async-done | bytes 4128 | tf_op jit(solution)/shard_map/all_to_all | solution.py:21
  63.4 45.0 %all-gather.2.cloned.1.call-done = bf16[6144,512]{1,0:T(8,128)(2,1)} async-done(((bf16[768,512]{1,0:T(8,128)(2,1)}), bf16[6144,512]{1,0:T(8,128)(2,1)}) %all-gather.2.cloned.1.call-update) | async-done | bytes 6291472 | tf_op jit(solution)/shard_map/all_gather | solution.py:223
  108.5 9.4 %shard_map.129 = (bf16[8,4,128,512]{3,2,1,0:T(8,128)(2,1)}, f32[256,1]{1,0:T(8,128)}, f32[256,1]{1,0:T(8,128)}) custom-call(bf16[8,4,192,512]{3,2,1,0:T(8,128)(2,1)} %bitcast.76, bf16[4096,256]{1,0:T(8,128)(2,1)} %bitcast.75, bf16[128,4096]{1,0:T(8,128)(2,1)} %bitcast.91, f32[512,1]{1,0:T(8,128)} %copy.24.row_r, f32[512,1]{1,0:T(8,128)} %copy.25.row_gate), custom_call_target="tpu_custom_call" | custom-call | tf_op jit(solution)/shard_map/pallas_call | solution.py:273
  119.6 4.0 %all-to-all-start.4 = ((f32[8,2,256]{2,1,0:T(2,128)}), f32[8,2,256]{2,1,0:T(2,128)S(1)}, u32[]{:S(2)}, u32[]{:S(2)}) async-start(f32[8,2,256]{2,1,0:T(2,128)} %broadcast_in_dim.135), calls=%async_computation.5 | async-start | bytes 32768 | tf_op jit(solution)/shard_map/all_to_all | solution.py:17
  123.7 7.7 %all-to-all-done.4 = f32[8,2,256]{2,1,0:T(2,128)S(1)} async-done(((f32[8,2,256]{2,1,0:T(2,128)}), f32[8,2,256]{2,1,0:T(2,128)S(1)}, u32[]{:S(2)}, u32[]{:S(2)}) %all-to-all-start.4) | async-done | bytes 16416 | tf_op jit(solution)/shard_map/all_to_all | solution.py:17
  132.2 3.3 %all-to-all-start.5 = ((f32[4,1,128]{2,1,0:T(1,128)}), f32[4,1,128]{2,1,0:T(1,128)S(1)}, u32[]{:S(2)}, u32[]{:S(2)}) async-start(f32[4,1,128]{2,1,0:T(1,128)} %reshape.260), calls=%async_computation.6 | async-start | bytes 4096 | tf_op jit(solution)/shard_map/all_to_all | solution.py:21
  135.6 5.2 %all-to-all-done.5 = f32[4,1,128]{2,1,0:T(1,128)S(1)} async-done(((f32[4,1,128]{2,1,0:T(1,128)}), f32[4,1,128]{2,1,0:T(1,128)S(1)}, u32[]{:S(2)}, u32[]{:S(2)}) %all-to-all-start.5) | async-done | bytes 2080 | tf_op jit(solution)/shard_map/all_to_all | solution.py:21
  142.3 32.5 %reduce-scatter.2.cloned.1.call-done = bf16[512,512]{1,0:T(8,128)(2,1)} async-done(((bf16[4096,512]{1,0:T(8,128)(2,1)}), bf16[512,512]{1,0:T(8,128)(2,1)}) %reduce-scatter.2.cloned.1.call-update) | async-done | bytes 524304 | tf_op jit(solution)/shard_map/reduce_scatter | solution.py:290
  174.8 3.5 %all-to-all-start.3 = ((bf16[4,128,512]{2,1,0:T(8,128)(2,1)}), bf16[4,128,512]{2,1,0:T(8,128)(2,1)S(1)}, u32[]{:S(2)}, u32[]{:S(2)}) async-start(bf16[4,128,512]{2,1,0:T(8,128)(2,1)} %bitcast.89), calls=%async_computation.4 | async-start | bytes 1048576 | tf_op jit(solution)/shard_map/all_to_all | solution.py:21
  178.3 1.1 multiply_reduce_fusion
  179.5 2.4 %collective-permute-start = (f32[1,512]{1,0:T(1,128)S(1)}, f32[1,512]{1,0:T(1,128)S(1)}, u32[]{:S(2)}, u32[]{:S(2)}) collective-permute-start(f32[1,512]{1,0:T(1,128)S(1)} %bitcast.118), channel_id=1, source_target_pairs={{0,8},{8,16},{16,24},{24,0},{1,9},{9,17},{17,25},{25,1},{2,10},{10... | collective-permute-start | bytes 6152 | tf_op jit(solution)/shard_map/ppermute | solution.py:32
  181.9 5.0 %collective-permute-start.1 = (f32[1,512]{1,0:T(1,128)S(1)}, f32[1,512]{1,0:T(1,128)S(1)}, u32[]{:S(2)}, u32[]{:S(2)}) collective-permute-start(f32[1,512]{1,0:T(1,128)S(1)} %bitcast.119), channel_id=1, source_target_pairs={{0,16},{8,24},{16,0},{24,8},{1,17},{9,25},{17,1},{25,9},{2,18},{10... | collective-permute-start | bytes 6152 | tf_op jit(solution)/shard_map/ppermute | solution.py:32
  186.9 4.8 %collective-permute-start.2 = (f32[1,512]{1,0:T(1,128)S(1)}, f32[1,512]{1,0:T(1,128)S(1)}, u32[]{:S(2)}, u32[]{:S(2)}) collective-permute-start(f32[1,512]{1,0:T(1,128)S(1)} %bitcast.120), channel_id=1, source_target_pairs={{0,24},{8,0},{16,8},{24,16},{1,25},{9,1},{17,9},{25,17},{2,26},{10... | collective-permute-start | bytes 6152 | tf_op jit(solution)/shard_map/ppermute | solution.py:32
  191.7 1.2 collective-permute-done.2
  193.3 5.5 %collective-permute-start.4 = (bf16[128,512]{1,0:T(8,128)(2,1)S(1)}, bf16[128,512]{1,0:T(8,128)(2,1)S(1)}, u32[]{:S(2)}, u32[]{:S(2)}) collective-permute-start(bf16[128,512]{1,0:T(8,128)(2,1)S(1)} %fusion.3), channel_id=1, source_target_pairs={{32,0},{64,32},{96,64},{128,96},{160,128},{192,160},{224,192},{256... | collective-permute-start | bytes 393224 | tf_op jit(solution)/shard_map/ppermute | solution.py:27
  199.1 1.9 collective-permute-start.3
  202.1 6.5 %collective-permute-done.3 = bf16[128,512]{1,0:T(8,128)(2,1)S(1)} collective-permute-done((bf16[128,512]{1,0:T(8,128)(2,1)S(1)}, bf16[128,512]{1,0:T(8,128)(2,1)S(1)}, u32[]{:S(2)}, u32[]{:S(2)}) %collective-permute-start.3) | collective-permute-done | bytes 131104 | tf_op jit(solution)/shard_map/ppermute | solution.py:27
  (102 shorter events, 15.1 us)
Async XLA Ops:
  7.2 21.2 %copy-start = (bf16[1,512,4]{1,2,0:T(4,128)(2,1)S(1)}, bf16[1,512,4]{1,2,0:T(4,128)(2,1)}, u32[]{:S(2)}) copy-start(bf16[1,512,4]{1,2,0:T(4,128)(2,1)} %param.15) | copy-start | bytes 12292
  7.2 34.4 %copy-start.9 = (s32[1,128,2]{1,2,0:T(2,128)S(1)}, s32[1,128,2]{1,2,0:T(2,128)}, u32[]{:S(2)}) copy-start(s32[1,128,2]{1,2,0:T(2,128)} %param.12) | copy-start | bytes 3076
  7.2 34.4 %copy-start.8 = (s32[1,128,2]{1,2,0:T(2,128)S(1)}, s32[1,128,2]{1,2,0:T(2,128)}, u32[]{:S(2)}) copy-start(s32[1,128,2]{1,2,0:T(2,128)} %param.13) | copy-start | bytes 3076
  7.2 47.7 %copy-start.1 = (bf16[1,1,4096,2,128]{4,3,2,1,0:T(2,128)(2,1)S(1)}, bf16[1,1,4096,2,128]{4,3,2,1,0:T(2,128)(2,1)}, u32[]{:S(2)}) copy-start(bf16[1,1,4096,2,128]{4,3,2,1,0:T(2,128)(2,1)} %param.16) | copy-start | bytes 6291460
  7.2 101.2 %all-gather.2.cloned.1.call-start = ((), (), s32[]{:S(2)}) async-start(), calls=%async_computation.7 | async-start | bytes 7077888 | tf_op jit(solution)/shard_map/all_gather | solution.py:223
  31.2 18.8 %all-to-all-start.1 = ((f32[8,16,128]{2,1,0:T(8,128)}), f32[8,16,128]{2,1,0:T(8,128)S(1)}, u32[]{:S(2)}, u32[]{:S(2)}) async-start(f32[8,16,128]{2,1,0:T(8,128)} %broadcast_in_dim.127), calls=%async_computation.1 | async-start | bytes 131072 | tf_op jit(solution)/shard_map/all_to_all | solution.py:17
  51.6 8.5 %all-to-all-start.2 = ((f32[4,1,256]{2,1,0:T(1,128)}), f32[4,1,256]{2,1,0:T(1,128)S(1)}, u32[]{:S(2)}, u32[]{:S(2)}) async-start(f32[4,1,256]{2,1,0:T(1,128)} %reshape.258), calls=%async_computation.2 | async-start | bytes 8192 | tf_op jit(solution)/shard_map/all_to_all | solution.py:21
  54.8 120.0 %reduce-scatter.2.cloned.1.call-start = ((), (), s32[]{:S(2)}) async-start(), calls=%async_computation.8 | async-start | bytes 4718592 | tf_op jit(solution)/shard_map/reduce_scatter | solution.py:290
  117.8 0.9 copy-start.7
  117.9 1.0 copy-start.6
  117.9 24.1 %copy-start.3 = (bf16[1,128,512]{2,1,0:T(8,128)(2,1)S(1)}, bf16[1,128,512]{2,1,0:T(8,128)(2,1)}, u32[]{:S(2)}) copy-start(bf16[1,128,512]{2,1,0:T(8,128)(2,1)} %param.11) | copy-start | bytes 393220
  117.9 61.6 %copy-start.10 = (f32[1,512]{1,0:T(1,128)S(1)}, f32[1,512]{1,0:T(1,128)}, u32[]{:S(2)}) copy-start(f32[1,512]{1,0:T(1,128)} %gain.1) | copy-start | bytes 6148
  117.9 75.1 %copy-start.4 = (bf16[1,128,512]{2,1,0:T(8,128)(2,1)S(1)}, bf16[1,128,512]{2,1,0:T(8,128)(2,1)}, u32[]{:S(2)}) copy-start(bf16[1,128,512]{2,1,0:T(8,128)(2,1)} %param.10) | copy-start | bytes 393220
  117.9 80.9 %copy-start.2 = (bf16[1,128,512]{2,1,0:T(8,128)(2,1)S(1)}, bf16[1,128,512]{2,1,0:T(8,128)(2,1)}, u32[]{:S(2)}) copy-start(bf16[1,128,512]{2,1,0:T(8,128)(2,1)} %param.9) | copy-start | bytes 393220
  119.6 11.8 %all-to-all-start.4 = ((f32[8,2,256]{2,1,0:T(2,128)}), f32[8,2,256]{2,1,0:T(2,128)S(1)}, u32[]{:S(2)}, u32[]{:S(2)}) async-start(f32[8,2,256]{2,1,0:T(2,128)} %broadcast_in_dim.135), calls=%async_computation.5 | async-start | bytes 32768 | tf_op jit(solution)/shard_map/all_to_all | solution.py:17
  132.2 8.6 %all-to-all-start.5 = ((f32[4,1,128]{2,1,0:T(1,128)}), f32[4,1,128]{2,1,0:T(1,128)S(1)}, u32[]{:S(2)}, u32[]{:S(2)}) async-start(f32[4,1,128]{2,1,0:T(1,128)} %reshape.260), calls=%async_computation.6 | async-start | bytes 4096 | tf_op jit(solution)/shard_map/all_to_all | solution.py:21
  174.8 18.1 %all-to-all-start.3 = ((bf16[4,128,512]{2,1,0:T(8,128)(2,1)}), bf16[4,128,512]{2,1,0:T(8,128)(2,1)S(1)}, u32[]{:S(2)}, u32[]{:S(2)}) async-start(bf16[4,128,512]{2,1,0:T(8,128)(2,1)} %bitcast.89), calls=%async_computation.4 | async-start | bytes 1048576 | tf_op jit(solution)/shard_map/all_to_all | solution.py:21
  179.5 12.2 %collective-permute-start = (f32[1,512]{1,0:T(1,128)S(1)}, f32[1,512]{1,0:T(1,128)S(1)}, u32[]{:S(2)}, u32[]{:S(2)}) collective-permute-start(f32[1,512]{1,0:T(1,128)S(1)} %bitcast.118), channel_id=1, source_target_pairs={{0,8},{8,16},{16,24},{24,0},{1,9},{9,17},{17,25},{25,1},{2,10},{10... | collective-permute-start | bytes 6152 | tf_op jit(solution)/shard_map/ppermute | solution.py:32
  181.9 9.9 %collective-permute-start.1 = (f32[1,512]{1,0:T(1,128)S(1)}, f32[1,512]{1,0:T(1,128)S(1)}, u32[]{:S(2)}, u32[]{:S(2)}) collective-permute-start(f32[1,512]{1,0:T(1,128)S(1)} %bitcast.119), channel_id=1, source_target_pairs={{0,16},{8,24},{16,0},{24,8},{1,17},{9,25},{17,1},{25,9},{2,18},{10... | collective-permute-start | bytes 6152 | tf_op jit(solution)/shard_map/ppermute | solution.py:32
  186.9 6.1 %collective-permute-start.2 = (f32[1,512]{1,0:T(1,128)S(1)}, f32[1,512]{1,0:T(1,128)S(1)}, u32[]{:S(2)}, u32[]{:S(2)}) collective-permute-start(f32[1,512]{1,0:T(1,128)S(1)} %bitcast.120), channel_id=1, source_target_pairs={{0,24},{8,0},{16,8},{24,16},{1,25},{9,1},{17,9},{25,17},{2,26},{10... | collective-permute-start | bytes 6152 | tf_op jit(solution)/shard_map/ppermute | solution.py:32
  193.3 16.6 %copy-start.11 = (bf16[128,512]{1,0:T(8,128)(2,1)}, bf16[128,512]{1,0:T(8,128)(2,1)S(1)}, u32[]{:S(2)}) copy-start(bf16[128,512]{1,0:T(8,128)(2,1)S(1)} %fusion.3) | copy-start | bytes 393220
  193.3 8.8 %collective-permute-start.4 = (bf16[128,512]{1,0:T(8,128)(2,1)S(1)}, bf16[128,512]{1,0:T(8,128)(2,1)S(1)}, u32[]{:S(2)}, u32[]{:S(2)}) collective-permute-start(bf16[128,512]{1,0:T(8,128)(2,1)S(1)} %fusion.3), channel_id=1, source_target_pairs={{32,0},{64,32},{96,64},{128,96},{160,128},{192,160},{224,192},{256... | collective-permute-start | bytes 393224 | tf_op jit(solution)/shard_map/ppermute | solution.py:27
  199.1 10.8 %copy-start.5 = (bf16[128,512]{1,0:T(8,128)(2,1)}, bf16[128,512]{1,0:T(8,128)(2,1)S(1)}, u32[]{:S(2)}) copy-start(bf16[128,512]{1,0:T(8,128)(2,1)S(1)} %fusion.2) | copy-start | bytes 393220
  199.1 9.5 %collective-permute-start.3 = (bf16[128,512]{1,0:T(8,128)(2,1)S(1)}, bf16[128,512]{1,0:T(8,128)(2,1)S(1)}, u32[]{:S(2)}, u32[]{:S(2)}) collective-permute-start(bf16[128,512]{1,0:T(8,128)(2,1)S(1)} %fusion.2), channel_id=1, source_target_pairs={{0,32},{32,64},{64,96},{96,128},{128,160},{160,192},{192,224},{224... | collective-permute-start | bytes 393224 | tf_op jit(solution)/shard_map/ppermute | solution.py:27
Sparse Core Ops, SparseCore 0:
  27.4 81.0 all-gather.1
  118.1 56.7 reduce-scatter.1

commit v3 on v2

--- a/solution.py
+++ b/solution.py
@@ -1,9 +1,12 @@
+import functools
+
 import jax
 import jax.numpy as jnp
 from jax import lax
 from jax.experimental import pallas as pl
 from jax.experimental.pallas import tpu as pltpu
 from jax.sharding import PartitionSpec as P
+
 
 D = 4096
 ROUTE_SCALE = 2.827
@@ -57,7 +60,7 @@
 
 
 def dispatch_kernel(routes_f, routes_b, gain, tokens, stashed, incoming, sent):
-    experts, _, width = sent.shape
+    experts, _, _ = sent.shape
     length = tokens.shape[0]
     capacity = sent.shape[1] // 3
     shape = (2 * experts, length)
@@ -110,39 +113,38 @@
             ]
 
 
-def expert_kernel(
-    whole, gate_up, down_w, row_r, row_gate, partial, gate_part, along_part, rows, outs, sums, took, left
-):
-    pieces, experts, _, width = whole.shape
-    capacity = whole.shape[2] // 3
-    slots = experts * capacity
+def expert_kernel(pieces, at, gate_up, down_w, row_r, row_gate, *refs):
+    arrived, refs = refs[: 2 * pieces], refs[2 * pieces :]
+    partial, refs = refs[: 2 * pieces], refs[2 * pieces :]
+    gate_part, along_part, gain_part, sums = refs
+    half, rows, width = arrived[0].shape
+    capacity = rows // 3
+    part_rows = half * capacity
+    slots = 2 * part_rows
     hidden = down_w.shape[0]
 
-    def fetch(z, k):
-        return pltpu.make_async_copy(
-            whole.at[z, :, pl.ds(k * capacity, capacity), :], rows.at[z, k], took.at[z, k]
-        )
-
-    def put(z, k):
-        return pltpu.make_async_copy(
-            outs.at[z, k], partial.at[z, :, pl.ds(k * capacity, capacity), :], left.at[z, k]
-        )
-
-    for z in range(pieces):
-        for k in range(3):
-            fetch(z, k).start()
+    def start(j):
+        return pl.multiple_of(((at[0] + j) % pieces) * width, width)
+
+    def taken(j, k):
+        return [
+            arrived[2 * j + c][:, k * capacity : (k + 1) * capacity, :].reshape(part_rows, width)
+            for c in range(2)
+        ]
+
     weighted = None
-    for z in range(pieces):
-        part = slice(z * width, (z + 1) * width)
-        for k in range(3):
-            fetch(z, k).wait()
-        values = rows[z, 0:2].reshape(2 * slots, width)
-        product = jnp.dot(values, gate_up[part, :], preferred_element_type=F32)
-        incoming = rows[z, 2].reshape(slots, width)
+    for j in range(pieces):
+        values = jnp.concatenate(taken(j, 0) + taken(j, 1), axis=0)
+        product = jnp.dot(
+            values, gate_up[pl.ds(start(j), width), :], preferred_element_type=F32
+        )
         product_w = lax.dot_general(
-            incoming, down_w[:, part], (((1,), (1,)), ((), ())), preferred_element_type=F32
-        )
-        if z == 0:
+            jnp.concatenate(taken(j, 2), axis=0),
+            down_w[:, pl.ds(start(j), width)],
+            (((1,), (1,)), ((), ())),
+            preferred_element_type=F32,
+        )
+        if j == 0:
             sums[...] = product
             weighted = product_w
         else:
@@ -162,23 +164,64 @@
         grad_first.astype(F32) * first + grad_second.astype(F32) * second, axis=1, keepdims=True
     )
     grads = jnp.concatenate([grad_first, grad_second], axis=1)
-    gate_f, gate_b = row_gate[:slots], row_gate[slots:]
-    for z in range(pieces):
-        part = slice(z * width, (z + 1) * width)
-        out_f = jnp.dot(inner_f, down_w[:, part], preferred_element_type=F32) * gate_f
-        outs[z, 0] = out_f.astype(BF16).reshape(experts, capacity, width)
-        put(z, 0).start()
+    gate_f, gate_b, r_b = row_gate[:slots], row_gate[slots:], row_r[slots:]
+    for j in range(pieces):
+        out_f = (
+            jnp.dot(inner_f, down_w[:, pl.ds(start(j), width)], preferred_element_type=F32) * gate_f
+        )
         out_b = (
             lax.dot_general(
-                grads, gate_up[part, :], (((1,), (1,)), ((), ())), preferred_element_type=F32
+                grads,
+                gate_up[pl.ds(start(j), width), :],
+                (((1,), (1,)), ((), ())),
+                preferred_element_type=F32,
             )
             * gate_b
         )
-        outs[z, 1] = out_b.astype(BF16).reshape(experts, capacity, width)
-        put(z, 1).start()
-    for z in range(pieces):
-        for k in range(2):
-            put(z, k).wait()
+        stashed = jnp.concatenate(taken(j, 1), axis=0).astype(F32)
+        gain_part[j : j + 1, :] = jnp.sum(out_b * r_b * stashed, axis=0, keepdims=True)
+        for k, out in enumerate((out_f.astype(BF16), out_b.astype(BF16))):
+            for c in range(2):
+                partial[2 * j + c][:, k * capacity : (k + 1) * capacity, :] = out[
+                    c * part_rows : (c + 1) * part_rows
+                ].reshape(half, capacity, width)
+
+
+def ring_gather(first, second, axis):
+    size = lax.axis_size(axis)
+    middle = size // 2
+    found = [[None, None] for _ in range(size)]
+    found[0] = [first, second]
+    for step in range(1, middle):
+        for c in range(2):
+            found[size - step][c] = rotated(found[(size - step + 1) % size][c], axis, 1)
+            found[step][c] = rotated(found[step - 1][c], axis, -1)
+    found[middle][0] = rotated(found[middle + 1][0], axis, 1)
+    found[middle][1] = rotated(found[middle - 1][1], axis, -1)
+    return [block for pair in found for block in pair]
+
+
+def ring_scatter(parts, axis):
+    size = lax.axis_size(axis)
+    middle = size // 2
+
+    def plus(a, b):
+        return (a.astype(F32) + b.astype(F32)).astype(BF16)
+
+    def passed(come, mine, distance):
+        return rotated(mine if come is None else plus(come, mine), axis, distance)
+
+    up = [passed(None, parts[2 * middle], 1), None]
+    down = [None, passed(None, parts[2 * middle + 1], -1)]
+    for turn in range(1, middle):
+        step = middle - turn
+        for c in range(2):
+            up[c] = passed(up[c], parts[2 * step + c], 1)
+            down[c] = passed(down[c], parts[2 * (size - step) + c], -1)
+    return [
+        (parts[c].astype(F32) + up[c].astype(F32) + down[c].astype(F32)).astype(BF16)
+        for c in range(2)
+    ]
 
 
 def local(
@@ -205,7 +248,6 @@
     slots = experts * capacity
     pieces = lax.axis_size("expert")
     vmem = pl.BlockSpec(memory_space=pltpu.VMEM)
-    hbm = pl.BlockSpec(memory_space=pl.ANY)
     sent = pl.pallas_call(
         dispatch_kernel,
         out_shape=jax.ShapeDtypeStruct((experts, 3 * capacity, width), BF16),
@@ -220,13 +262,13 @@
         incoming,
     )
     arrived = exchanged(sent, "dp")
-    whole = lax.all_gather(arrived.reshape(3 * slots, width), "expert", axis=0, tiled=True)
-
-    (tokens, stashed, incoming, gain, routes_f, routes_b), arrived2 = lax.optimization_barrier(
+    whole = ring_gather(arrived[: experts // 2], arrived[experts // 2 :], "expert")
+
+    (tokens, stashed, incoming, gain, routes_f, routes_b), _ = lax.optimization_barrier(
         ((tokens, stashed, incoming, gain, forward_routes[0], backward_routes[0]), arrived)
     )
-    slot_f, placed_f, member_f = slots_of(routes_f, experts, capacity)
-    slot_b, placed_b, member_b = slots_of(routes_b, experts, capacity)
+    _, placed_f, member_f = slots_of(routes_f, experts, capacity)
+    _, placed_b, member_b = slots_of(routes_b, experts, capacity)
     spread_f = (placed_f[0] | placed_f[1]).astype(BF16)
     spread_b = (placed_b[0] | placed_b[1]).astype(BF16)
     tokens32, stashed32 = tokens.astype(F32), stashed.astype(F32)
@@ -268,33 +310,30 @@
     scalars = scalars.transpose(1, 0, 2).reshape(4, slots)
     row_r = jnp.concatenate([scalars[0], scalars[2]])[:, None]
     row_gate = jnp.concatenate([scalars[1], scalars[3]])[:, None]
-    row_r_b = scalars[2].reshape(experts, capacity, 1)
-
-    partial, gate_part, along_part = pl.pallas_call(
-        expert_kernel,
+
+    at = lax.axis_index("expert")
+    part = jax.ShapeDtypeStruct((experts // 2, 2 * capacity, width), BF16)
+    *partial, gate_part, along_part, rows_gain = pl.pallas_call(
+        functools.partial(expert_kernel, pieces),
         out_shape=(
-            jax.ShapeDtypeStruct((pieces, experts, 2 * capacity, width), BF16),
+            *[part] * (2 * pieces),
             jax.ShapeDtypeStruct((slots, 1), F32),
             jax.ShapeDtypeStruct((slots, 1), F32),
+            jax.ShapeDtypeStruct((pieces, width), F32),
         ),
-        in_specs=[hbm] + [vmem] * 4,
-        out_specs=(hbm, vmem, vmem),
-        scratch_shapes=[
-            pltpu.VMEM((pieces, 3, experts, capacity, width), BF16),
-            pltpu.VMEM((pieces, 2, experts, capacity, width), BF16),
-            pltpu.VMEM((2 * slots, 2 * hidden), F32),
-            pltpu.SemaphoreType.DMA((pieces, 3)),
-            pltpu.SemaphoreType.DMA((pieces, 2)),
-        ],
-    )(whole.reshape(pieces, experts, 3 * capacity, width), gate_up, down_w, row_r, row_gate)
-    summed = lax.psum_scatter(
-        partial.reshape(pieces * 2 * slots, width), "expert", scatter_dimension=0, tiled=True
-    )
-    summed = summed.reshape(experts, 2 * capacity, width)
-
-    parts = jnp.stack([gate_part[:, 0], along_part[:, 0]])
-    parts = summed_over(parts, "expert")
-    parts = exchanged(parts.reshape(2, experts, capacity).transpose(1, 0, 2), "dp")
+        in_specs=[pl.BlockSpec(memory_space=pltpu.SMEM)] + [vmem] * (4 + 2 * pieces),
+        out_specs=(vmem,) * (2 * pieces + 3),
+        scratch_shapes=[pltpu.VMEM((2 * slots, 2 * hidden), F32)],
+    )(at[None].astype(jnp.int32), gate_up, down_w, row_r, row_gate, *whole)
+    summed = jnp.concatenate(ring_scatter(partial, "expert"), axis=0)
+
+    parts = jnp.concatenate([gate_part[:, 0], along_part[:, 0]])
+    parts = jnp.stack([jnp.broadcast_to(parts, (pieces, 2 * slots)), jnp.roll(rows_gain, at, axis=0)], 1)
+    parts = exchanged(parts, "expert")
+    parts = jnp.sum(parts, axis=0)
+    rows_gain = parts[1]
+    parts = parts[0].reshape(2, experts, capacity).transpose(1, 0, 2)
+    parts = exchanged(parts, "dp")
     parts = parts.transpose(1, 0, 2).reshape(2, slots)
 
     def by_token(values):
@@ -314,6 +353,9 @@
         preferred_element_type=F32,
     )
     own_gain = jnp.sum(router_part * stashed32 * r_b[:, None], axis=0)
+    own_gain = own_gain + rows_gain / gain
+    gain_total = exchanged(jnp.broadcast_to(own_gain, (experts, 1, width)), "dp")
+    gain_total = jnp.sum(gain_total, axis=(0, 1))
     base = (
         incoming.astype(F32)
         + (r_b[:, None] * router_part) * gain
@@ -321,18 +363,6 @@
     )
 
     back = exchanged(summed, "dp")
-    gain_part = own_gain + (
-        jnp.sum(
-            summed[:, capacity:].astype(F32)
-            * arrived2[:, capacity : 2 * capacity].astype(F32)
-            * row_r_b,
-            axis=(0, 1),
-        )
-        / gain
-    )
-    others = [rotated(gain_part[None], "dp", distance) for distance in range(1, experts)]
-    back, others = lax.optimization_barrier((back, others))
-    gain_total = gain_part + sum(other[0] for other in others)
 
     def gathered(spread, rows):
         return lax.dot_general(

time: 217 us -> 240 us (1.11)
  the two profiles are of different devices: /device:TPU:2 before, /device:TPU:56 now
where the time goes in v3:
time: 240 us; the launch traced here: 238 us
  starting transfers between devices  127 us (53%)
  waiting for transfers between devices  33.2 us (14%)
  blocking collectives  25.2 us (10%)
  other arithmetic  19.2 us (8%)
  local copies, waits for them, and re-layouts  17 us (7%)
  Pallas kernels  11.6 us (5%)
  matrix products  3.72 us (2%)
    ppermute x28, starting transfers between devices, rotated(): lax.ppermute(block, axis, [(i, (i + distance) % size) for i in range(size)])  99.7 us
    all_to_all x2, blocking collectives, exchanged(): return lax.all_to_all(blocks, axis, split_axis=0, concat_axis=0, tiled=True)  25.2 us
    all_to_all x4, waiting for transfers between devices, exchanged(): return lax.all_to_all(blocks, axis, split_axis=0, concat_axis=0, tiled=True)  20.8 us
    all_to_all x4, starting transfers between devices, exchanged(): return lax.all_to_all(blocks, axis, split_axis=0, concat_axis=0, tiled=True)  15 us
    pallas_call x1, Pallas kernels, local(): pl.pallas_call(functools.partial(expert_kernel, pieces), out_shape=(*[par...  9.14 us
    ppermute x2, starting transfers between devices, shifted(): return lax.ppermute(block, axis, route)  7.95 us
    all_to_all x1, waiting for transfers between devices, summed_over(): lax.all_to_all(copies, axis, split_axis=0, concat_axis=0, tiled=True)  6.23 us
    ppermute x28, waiting for transfers between devices, rotated(): lax.ppermute(block, axis, [(i, (i + distance) % size) for i in range(size)])  6.13 us
  transfers between devices with their start and end apart: 35, of which 8 were waited for; matrix products, arithmetic and copies ran while one was open for 13% of the time, Pallas kernels for 0%

profile of v3, /device:TPU:56, one launch (start us, length us, event | category | flops | bytes accessed | tf_op | source)
XLA Modules:
  0.0 238.1 jit_solution(5589443437904259113)
XLA Ops:
  3.2 17.6 %all_to_all.35 = bf16[4,192,512]{2,1,0:T(8,128)(2,1)S(1)} all-to-all(bf16[4,192,512]{2,1,0:T(8,128)(2,1)} %shard_map.128), channel_id=1, replica_groups=mesh['pipe'=16,'dp'=4,'expert'=8] {'dp'}, dimensions={0} | all-to-all | bytes 1572864 | tf_op jit(solution)/shard_map/all_to_all | solution.py:24
  22.9 10.9 %collective-permute-start.1 = (bf16[2,192,512]{2,1,0:T(8,128)(2,1)S(1)}, bf16[2,192,512]{2,1,0:T(8,128)(2,1)S(1)}, u32[]{:S(2)}, u32[]{:S(2)}) collective-permute-start(bf16[2,192,512]{2,1,0:T(8,128)(2,1)S(1)} %get-tuple-element.77.refs_1_), channel_id=1, source_target_pairs={{0,7},{1,0},{2,1},{3,2},{4,3},{5,4},{6,5},{7,6},{8,15},{9,8},{10,9... | collective-permute-start | bytes 1179656 | tf_op jit(solution)/shard_map/ppermute | solution.py:35
  37.7 5.1 %collective-permute-start = (bf16[2,192,512]{2,1,0:T(8,128)(2,1)S(1)}, bf16[2,192,512]{2,1,0:T(8,128)(2,1)}, u32[]{:S(2)}, u32[]{:S(2)}) collective-permute-start(bf16[2,192,512]{2,1,0:T(8,128)(2,1)S(1)} %get-tuple-element.78.refs_0_), channel_id=1, source_target_pairs={{0,7},{1,0},{2,1},{3,2},{4,3},{5,4},{6,5},{7,6},{8,15},{9,8},{10,9... | collective-permute-start | bytes 1179656 | tf_op jit(solution)/shard_map/ppermute | solution.py:35
  46.3 4.0 %all-to-all-start.1 = ((f32[8,16,128]{2,1,0:T(8,128)}), f32[8,16,128]{2,1,0:T(8,128)}, u32[]{:S(2)}, u32[]{:S(2)}) async-start(f32[8,16,128]{2,1,0:T(8,128)} %broadcast_in_dim.126), calls=%async_computation.1 | async-start | bytes 131072 | tf_op jit(solution)/shard_map/all_to_all | solution.py:20
  52.4 6.2 %all-to-all-done.1 = f32[8,16,128]{2,1,0:T(8,128)} async-done(((f32[8,16,128]{2,1,0:T(8,128)}), f32[8,16,128]{2,1,0:T(8,128)}, u32[]{:S(2)}, u32[]{:S(2)}) %all-to-all-start.1) | async-done | bytes 65568 | tf_op jit(solution)/shard_map/all_to_all | solution.py:20
  64.0 3.5 %collective-permute-start.7 = (bf16[2,192,512]{2,1,0:T(8,128)(2,1)}, bf16[2,192,512]{2,1,0:T(8,128)(2,1)}, u32[]{:S(2)}, u32[]{:S(2)}) collective-permute-start(bf16[2,192,512]{2,1,0:T(8,128)(2,1)} %collective-permute-done.6.refs_14_), channel_id=1, source_target_pairs={{0,1},{1,2},{2,3},{3,4},{4,5},{5,6},{6,7},{7,0},{8,9},{9,10},{10,1... | collective-permute-start | bytes 1179656 | tf_op jit(solution)/shard_map/ppermute | solution.py:35
  71.2 4.6 %collective-permute-start.2 = (bf16[2,192,512]{2,1,0:T(8,128)(2,1)}, bf16[2,192,512]{2,1,0:T(8,128)(2,1)}, u32[]{:S(2)}, u32[]{:S(2)}) collective-permute-start(bf16[2,192,512]{2,1,0:T(8,128)(2,1)} %collective-permute-done.refs_2_), channel_id=1, source_target_pairs={{0,7},{1,0},{2,1},{3,2},{4,3},{5,4},{6,5},{7,6},{8,15},{9,8},{10,9... | collective-permute-start | bytes 1179656 | tf_op jit(solution)/shard_map/ppermute | solution.py:35
  92.9 4.6 %collective-permute-start.4 = (bf16[2,192,512]{2,1,0:T(8,128)(2,1)}, bf16[2,192,512]{2,1,0:T(8,128)(2,1)}, u32[]{:S(2)}, u32[]{:S(2)}) collective-permute-start(bf16[2,192,512]{2,1,0:T(8,128)(2,1)} %collective-permute-done.2.refs_4_), channel_id=1, source_target_pairs={{0,7},{1,0},{2,1},{3,2},{4,3},{5,4},{6,5},{7,6},{8,15},{9,8},{10,9... | collective-permute-start | bytes 1179656 | tf_op jit(solution)/shard_map/ppermute | solution.py:35
  97.6 3.5 %collective-permute-start.10 = (bf16[2,192,512]{2,1,0:T(8,128)(2,1)}, bf16[2,192,512]{2,1,0:T(8,128)(2,1)}, u32[]{:S(2)}, u32[]{:S(2)}) collective-permute-start(bf16[2,192,512]{2,1,0:T(8,128)(2,1)} %collective-permute-done.5.refs_7_), channel_id=1, source_target_pairs={{0,7},{1,0},{2,1},{3,2},{4,3},{5,4},{6,5},{7,6},{8,15},{9,8},{10,9... | collective-permute-start | bytes 1179656 | tf_op jit(solution)/shard_map/ppermute | solution.py:35
  109.8 3.6 %all-to-all-done.2 = f32[4,1,256]{2,1,0:T(1,128)S(1)} async-done(((f32[4,1,256]{2,1,0:T(1,128)}), f32[4,1,256]{2,1,0:T(1,128)S(1)}, u32[]{:S(2)}, u32[]{:S(2)}) %all-to-all-start.2) | async-done | bytes 4128 | tf_op jit(solution)/shard_map/all_to_all | solution.py:24
  116.9 9.1 %shard_map.129 = (bf16[2,128,512]{2,1,0:T(8,128)(2,1)}, bf16[2,128,512]{2,1,0:T(8,128)(2,1)}, bf16[2,128,512]{2,1,0:T(8,128)(2,1)}, bf16[2,128,512]{2,1,0:T(8,12...) custom-call(s32[1]{0:T(128)} %bitcast.10.at, ...), custom_call_target="tpu_custom_call" | custom-call | tf_op jit(solution)/shard_map/pallas_call | solution.py:316
  129.6 4.2 %all-to-all-start.4 = ((f32[8,2,512]{2,1,0:T(2,128)}), f32[8,2,512]{2,1,0:T(2,128)S(1)}, u32[]{:S(2)}, u32[]{:S(2)}) async-start(f32[8,2,512]{2,1,0:T(2,128)} %pad_maximum_fusion.1), calls=%async_computation.4 | async-start | bytes 65536 | tf_op jit(solution)/shard_map/all_to_all | solution.py:24
  133.8 8.0 %all-to-all-done.4 = f32[8,2,512]{2,1,0:T(2,128)S(1)} async-done(((f32[8,2,512]{2,1,0:T(2,128)}), f32[8,2,512]{2,1,0:T(2,128)S(1)}, u32[]{:S(2)}, u32[]{:S(2)}) %all-to-all-start.4) | async-done | bytes 32800 | tf_op jit(solution)/shard_map/all_to_all | solution.py:24
  148.3 4.6 %collective-permute-start.18 = (bf16[2,128,512]{2,1,0:T(8,128)(2,1)}, bf16[2,128,512]{2,1,0:T(8,128)(2,1)S(1)}, u32[]{:S(2)}, u32[]{:S(2)}) collective-permute-start(bf16[2,128,512]{2,1,0:T(8,128)(2,1)} %get-tuple-element.40), channel_id=1, source_target_pairs={{0,7},{1,0},{2,1},{3,2},{4,3},{5,4},{6,5},{7,6},{8,15},{9,8},{10,9... | collective-permute-start | bytes 786440 | tf_op jit(solution)/shard_map/ppermute | solution.py:35
  154.9 5.1 %collective-permute-start.24 = (bf16[2,128,512]{2,1,0:T(8,128)(2,1)}, bf16[2,128,512]{2,1,0:T(8,128)(2,1)S(1)}, u32[]{:S(2)}, u32[]{:S(2)}) collective-permute-start(bf16[2,128,512]{2,1,0:T(8,128)(2,1)} %get-tuple-element.47), channel_id=1, source_target_pairs={{0,7},{1,0},{2,1},{3,2},{4,3},{5,4},{6,5},{7,6},{8,15},{9,8},{10,9... | collective-permute-start | bytes 786440 | tf_op jit(solution)/shard_map/ppermute | solution.py:35
  165.3 5.3 %collective-permute-start.19 = (bf16[2,128,512]{2,1,0:T(8,128)(2,1)S(1)}, bf16[2,128,512]{2,1,0:T(8,128)(2,1)S(1)}, u32[]{:S(2)}, u32[]{:S(2)}) collective-permute-start(bf16[2,128,512]{2,1,0:T(8,128)(2,1)S(1)} %add_convert_fusion.8), channel_id=1, source_target_pairs={{0,7},{1,0},{2,1},{3,2},{4,3},{5,4},{6,5},{7,6},{8,15},{9,8},{10,9... | collective-permute-start | bytes 786440 | tf_op jit(solution)/shard_map/ppermute | solution.py:35
  172.8 5.3 %collective-permute-start.25 = (bf16[2,128,512]{2,1,0:T(8,128)(2,1)S(1)}, bf16[2,128,512]{2,1,0:T(8,128)(2,1)S(1)}, u32[]{:S(2)}, u32[]{:S(2)}) collective-permute-start(bf16[2,128,512]{2,1,0:T(8,128)(2,1)S(1)} %add_convert_fusion.3), channel_id=1, source_target_pairs={{0,7},{1,0},{2,1},{3,2},{4,3},{5,4},{6,5},{7,6},{8,15},{9,8},{10,9... | collective-permute-start | bytes 786440 | tf_op jit(solution)/shard_map/ppermute | solution.py:35
  180.3 5.1 %collective-permute-start.20 = (bf16[2,128,512]{2,1,0:T(8,128)(2,1)S(1)}, bf16[2,128,512]{2,1,0:T(8,128)(2,1)S(1)}, u32[]{:S(2)}, u32[]{:S(2)}) collective-permute-start(bf16[2,128,512]{2,1,0:T(8,128)(2,1)S(1)} %add_convert_fusion.7), channel_id=1, source_target_pairs={{0,7},{1,0},{2,1},{3,2},{4,3},{5,4},{6,5},{7,6},{8,15},{9,8},{10,9... | collective-permute-start | bytes 786440 | tf_op jit(solution)/shard_map/ppermute | solution.py:35
  188.1 3.5 %collective-permute-start.23 = (bf16[2,128,512]{2,1,0:T(8,128)(2,1)S(1)}, bf16[2,128,512]{2,1,0:T(8,128)(2,1)S(1)}, u32[]{:S(2)}, u32[]{:S(2)}) collective-permute-start(bf16[2,128,512]{2,1,0:T(8,128)(2,1)S(1)} %add_convert_fusion.4), channel_id=1, source_target_pairs={{0,1},{1,2},{2,3},{3,4},{4,5},{5,6},{6,7},{7,0},{8,9},{9,10},{10,1... | collective-permute-start | bytes 786440 | tf_op jit(solution)/shard_map/ppermute | solution.py:35
  194.8 5.6 %collective-permute-start.27 = (bf16[2,128,512]{2,1,0:T(8,128)(2,1)S(1)}, bf16[2,128,512]{2,1,0:T(8,128)(2,1)S(1)}, u32[]{:S(2)}, u32[]{:S(2)}) collective-permute-start(bf16[2,128,512]{2,1,0:T(8,128)(2,1)S(1)} %add_convert_fusion.1), channel_id=1, source_target_pairs={{0,7},{1,0},{2,1},{3,2},{4,3},{5,4},{6,5},{7,6},{8,15},{9,8},{10,9... | collective-permute-start | bytes 786440 | tf_op jit(solution)/shard_map/ppermute | solution.py:35
  205.3 4.4 %all-to-all-start.3 = ((bf16[4,128,512]{2,1,0:T(8,128)(2,1)}), bf16[4,128,512]{2,1,0:T(8,128)(2,1)S(1)}, u32[]{:S(2)}, u32[]{:S(2)}) async-start(bf16[4,128,512]{2,1,0:T(8,128)(2,1)} %pad_maximum_fusion), calls=%async_computation.3 | async-start | bytes 1048576 | tf_op jit(solution)/shard_map/all_to_all | solution.py:24
  210.7 9.3 %all-to-all-done.3 = bf16[4,128,512]{2,1,0:T(8,128)(2,1)S(1)} async-done(((bf16[4,128,512]{2,1,0:T(8,128)(2,1)}), bf16[4,128,512]{2,1,0:T(8,128)(2,1)S(1)}, u32[]{:S(2)}, u32[]{:S(2)}) %all-to-all-start.3) | async-done | bytes 524320 | tf_op jit(solution)/shard_map/all_to_all | solution.py:24
  223.8 4.7 %collective-permute-start.28 = (bf16[128,512]{1,0:T(8,128)(2,1)S(1)}, bf16[128,512]{1,0:T(8,128)(2,1)S(1)}, u32[]{:S(2)}, u32[]{:S(2)}) collective-permute-start(bf16[128,512]{1,0:T(8,128)(2,1)S(1)} %fusion.2), channel_id=1, source_target_pairs={{0,32},{32,64},{64,96},{96,128},{128,160},{160,192},{192,224},{224... | collective-permute-start | bytes 393224 | tf_op jit(solution)/shard_map/ppermute | solution.py:30
  228.6 7.7 %all_to_all.36 = f32[4,1,512]{2,1,0:T(1,128)S(1)} all-to-all(f32[4,1,512]{2,1,0:T(1,128)S(1)} %broadcast_in_dim.141), channel_id=1, replica_groups=mesh['pipe'=16,'dp'=4,'expert'=8] {'dp'}, dimensions={0} | all-to-all | bytes 16384 | tf_op jit(solution)/shard_map/all_to_all | solution.py:24
  (212 shorter events, 91.1 us)
Async XLA Ops:
  22.9 38.7 %collective-permute-start.1 = (bf16[2,192,512]{2,1,0:T(8,128)(2,1)S(1)}, bf16[2,192,512]{2,1,0:T(8,128)(2,1)S(1)}, u32[]{:S(2)}, u32[]{:S(2)}) collective-permute-start(bf16[2,192,512]{2,1,0:T(8,128)(2,1)S(1)} %get-tuple-element.77.refs_1_), channel_id=1, source_target_pairs={{0,7},{1,0},{2,1},{3,2},{4,3},{5,4},{6,5},{7,6},{8,15},{9,8},{10,9... | collective-permute-start | bytes 1179656 | tf_op jit(solution)/shard_map/ppermute | solution.py:35
  33.9 34.9 %collective-permute-start.11 = (bf16[2,192,512]{2,1,0:T(8,128)(2,1)S(1)}, bf16[2,192,512]{2,1,0:T(8,128)(2,1)}, u32[]{:S(2)}, u32[]{:S(2)}) collective-permute-start(bf16[2,192,512]{2,1,0:T(8,128)(2,1)S(1)} %get-tuple-element.77.refs_1_), channel_id=1, source_target_pairs={{0,1},{1,2},{2,3},{3,4},{4,5},{5,6},{6,7},{7,0},{8,9},{9,10},{10,1... | collective-permute-start | bytes 1179656 | tf_op jit(solution)/shard_map/ppermute | solution.py:35
  35.8 28.2 %collective-permute-start.6 = (bf16[2,192,512]{2,1,0:T(8,128)(2,1)S(1)}, bf16[2,192,512]{2,1,0:T(8,128)(2,1)}, u32[]{:S(2)}, u32[]{:S(2)}) collective-permute-start(bf16[2,192,512]{2,1,0:T(8,128)(2,1)S(1)} %get-tuple-element.78.refs_0_), channel_id=1, source_target_pairs={{0,1},{1,2},{2,3},{3,4},{4,5},{5,6},{6,7},{7,0},{8,9},{9,10},{10,1... | collective-permute-start | bytes 1179656 | tf_op jit(solution)/shard_map/ppermute | solution.py:35
  37.7 33.5 %collective-permute-start = (bf16[2,192,512]{2,1,0:T(8,128)(2,1)S(1)}, bf16[2,192,512]{2,1,0:T(8,128)(2,1)}, u32[]{:S(2)}, u32[]{:S(2)}) collective-permute-start(bf16[2,192,512]{2,1,0:T(8,128)(2,1)S(1)} %get-tuple-element.78.refs_0_), channel_id=1, source_target_pairs={{0,7},{1,0},{2,1},{3,2},{4,3},{5,4},{6,5},{7,6},{8,15},{9,8},{10,9... | collective-permute-start | bytes 1179656 | tf_op jit(solution)/shard_map/ppermute | solution.py:35
  64.0 15.4 %collective-permute-start.7 = (bf16[2,192,512]{2,1,0:T(8,128)(2,1)}, bf16[2,192,512]{2,1,0:T(8,128)(2,1)}, u32[]{:S(2)}, u32[]{:S(2)}) collective-permute-start(bf16[2,192,512]{2,1,0:T(8,128)(2,1)} %collective-permute-done.6.refs_14_), channel_id=1, source_target_pairs={{0,1},{1,2},{2,3},{3,4},{4,5},{5,6},{6,7},{7,0},{8,9},{9,10},{10,1... | collective-permute-start | bytes 1179656 | tf_op jit(solution)/shard_map/ppermute | solution.py:35
  68.7 21.8 %collective-permute-start.12 = (bf16[2,192,512]{2,1,0:T(8,128)(2,1)}, bf16[2,192,512]{2,1,0:T(8,128)(2,1)}, u32[]{:S(2)}, u32[]{:S(2)}) collective-permute-start(bf16[2,192,512]{2,1,0:T(8,128)(2,1)} %collective-permute-done.11.refs_15_), channel_id=1, source_target_pairs={{0,1},{1,2},{2,3},{3,4},{4,5},{5,6},{6,7},{7,0},{8,9},{9,10},{10,1... | collective-permute-start | bytes 1179656 | tf_op jit(solution)/shard_map/ppermute | solution.py:35
  71.2 21.7 %collective-permute-start.2 = (bf16[2,192,512]{2,1,0:T(8,128)(2,1)}, bf16[2,192,512]{2,1,0:T(8,128)(2,1)}, u32[]{:S(2)}, u32[]{:S(2)}) collective-permute-start(bf16[2,192,512]{2,1,0:T(8,128)(2,1)} %collective-permute-done.refs_2_), channel_id=1, source_target_pairs={{0,7},{1,0},{2,1},{3,2},{4,3},{5,4},{6,5},{7,6},{8,15},{9,8},{10,9... | collective-permute-start | bytes 1179656 | tf_op jit(solution)/shard_map/ppermute | solution.py:35
  75.8 21.7 %collective-permute-start.5 = (bf16[2,192,512]{2,1,0:T(8,128)(2,1)}, bf16[2,192,512]{2,1,0:T(8,128)(2,1)}, u32[]{:S(2)}, u32[]{:S(2)}) collective-permute-start(bf16[2,192,512]{2,1,0:T(8,128)(2,1)} %collective-permute-done.3.refs_5_), channel_id=1, source_target_pairs={{0,7},{1,0},{2,1},{3,2},{4,3},{5,4},{6,5},{7,6},{8,15},{9,8},{10,9... | collective-permute-start | bytes 1179656 | tf_op jit(solution)/shard_map/ppermute | solution.py:35
  79.4 21.7 %collective-permute-start.8 = (bf16[2,192,512]{2,1,0:T(8,128)(2,1)}, bf16[2,192,512]{2,1,0:T(8,128)(2,1)}, u32[]{:S(2)}, u32[]{:S(2)}) collective-permute-start(bf16[2,192,512]{2,1,0:T(8,128)(2,1)} %collective-permute-done.7.refs_12_), channel_id=1, source_target_pairs={{0,1},{1,2},{2,3},{3,4},{4,5},{5,6},{6,7},{7,0},{8,9},{9,10},{10,1... | collective-permute-start | bytes 1179656 | tf_op jit(solution)/shard_map/ppermute | solution.py:35
  90.5 26.3 %collective-permute-start.13 = (bf16[2,192,512]{2,1,0:T(8,128)(2,1)}, bf16[2,192,512]{2,1,0:T(8,128)(2,1)}, u32[]{:S(2)}, u32[]{:S(2)}) collective-permute-start(bf16[2,192,512]{2,1,0:T(8,128)(2,1)} %collective-permute-done.12.refs_13_), channel_id=1, source_target_pairs={{0,1},{1,2},{2,3},{3,4},{4,5},{5,6},{6,7},{7,0},{8,9},{9,10},{10,1... | collective-permute-start | bytes 1179656 | tf_op jit(solution)/shard_map/ppermute | solution.py:35
  92.9 23.9 %collective-permute-start.4 = (bf16[2,192,512]{2,1,0:T(8,128)(2,1)}, bf16[2,192,512]{2,1,0:T(8,128)(2,1)}, u32[]{:S(2)}, u32[]{:S(2)}) collective-permute-start(bf16[2,192,512]{2,1,0:T(8,128)(2,1)} %collective-permute-done.2.refs_4_), channel_id=1, source_target_pairs={{0,7},{1,0},{2,1},{3,2},{4,3},{5,4},{6,5},{7,6},{8,15},{9,8},{10,9... | collective-permute-start | bytes 1179656 | tf_op jit(solution)/shard_map/ppermute | solution.py:35
  97.6 19.3 %collective-permute-start.10 = (bf16[2,192,512]{2,1,0:T(8,128)(2,1)}, bf16[2,192,512]{2,1,0:T(8,128)(2,1)}, u32[]{:S(2)}, u32[]{:S(2)}) collective-permute-start(bf16[2,192,512]{2,1,0:T(8,128)(2,1)} %collective-permute-done.5.refs_7_), channel_id=1, source_target_pairs={{0,7},{1,0},{2,1},{3,2},{4,3},{5,4},{6,5},{7,6},{8,15},{9,8},{10,9... | collective-permute-start | bytes 1179656 | tf_op jit(solution)/shard_map/ppermute | solution.py:35
  101.1 15.7 %collective-permute-start.9 = (bf16[2,192,512]{2,1,0:T(8,128)(2,1)}, bf16[2,192,512]{2,1,0:T(8,128)(2,1)}, u32[]{:S(2)}, u32[]{:S(2)}) collective-permute-start(bf16[2,192,512]{2,1,0:T(8,128)(2,1)} %collective-permute-done.8.refs_10_), channel_id=1, source_target_pairs={{0,1},{1,2},{2,3},{3,4},{4,5},{5,6},{6,7},{7,0},{8,9},{9,10},{10,1... | collective-permute-start | bytes 1179656 | tf_op jit(solution)/shard_map/ppermute | solution.py:35
  142.6 17.4 %all-to-all-start.5 = ((f32[4,1,128]{2,1,0:T(1,128)}), f32[4,1,128]{2,1,0:T(1,128)S(1)}, u32[]{:S(2)}, u32[]{:S(2)}) async-start(f32[4,1,128]{2,1,0:T(1,128)} %reshape.241), calls=%async_computation.5 | async-start | bytes 4096 | tf_op jit(solution)/shard_map/all_to_all | solution.py:24
  145.9 15.3 %collective-permute-start.14 = (bf16[2,128,512]{2,1,0:T(8,128)(2,1)}, bf16[2,128,512]{2,1,0:T(8,128)(2,1)S(1)}, u32[]{:S(2)}, u32[]{:S(2)}) collective-permute-start(bf16[2,128,512]{2,1,0:T(8,128)(2,1)} %get-tuple-element.36), channel_id=1, source_target_pairs={{0,1},{1,2},{2,3},{3,4},{4,5},{5,6},{6,7},{7,0},{8,9},{9,10},{10,1... | collective-permute-start | bytes 786440 | tf_op jit(solution)/shard_map/ppermute | solution.py:35
  148.3 15.9 %collective-permute-start.18 = (bf16[2,128,512]{2,1,0:T(8,128)(2,1)}, bf16[2,128,512]{2,1,0:T(8,128)(2,1)S(1)}, u32[]{:S(2)}, u32[]{:S(2)}) collective-permute-start(bf16[2,128,512]{2,1,0:T(8,128)(2,1)} %get-tuple-element.40), channel_id=1, source_target_pairs={{0,7},{1,0},{2,1},{3,2},{4,3},{5,4},{6,5},{7,6},{8,15},{9,8},{10,9... | collective-permute-start | bytes 786440 | tf_op jit(solution)/shard_map/ppermute | solution.py:35
  152.9 17.6 %collective-permute-start.21 = (bf16[2,128,512]{2,1,0:T(8,128)(2,1)}, bf16[2,128,512]{2,1,0:T(8,128)(2,1)S(1)}, u32[]{:S(2)}, u32[]{:S(2)}) collective-permute-start(bf16[2,128,512]{2,1,0:T(8,128)(2,1)} %get-tuple-element.44), channel_id=1, source_target_pairs={{0,1},{1,2},{2,3},{3,4},{4,5},{5,6},{6,7},{7,0},{8,9},{9,10},{10,1... | collective-permute-start | bytes 786440 | tf_op jit(solution)/shard_map/ppermute | solution.py:35
  154.9 17.8 %collective-permute-start.24 = (bf16[2,128,512]{2,1,0:T(8,128)(2,1)}, bf16[2,128,512]{2,1,0:T(8,128)(2,1)S(1)}, u32[]{:S(2)}, u32[]{:S(2)}) collective-permute-start(bf16[2,128,512]{2,1,0:T(8,128)(2,1)} %get-tuple-element.47), channel_id=1, source_target_pairs={{0,7},{1,0},{2,1},{3,2},{4,3},{5,4},{6,5},{7,6},{8,15},{9,8},{10,9... | collective-permute-start | bytes 786440 | tf_op jit(solution)/shard_map/ppermute | solution.py:35
  162.2 15.9 %collective-permute-start.15 = (bf16[2,128,512]{2,1,0:T(8,128)(2,1)S(1)}, bf16[2,128,512]{2,1,0:T(8,128)(2,1)S(1)}, u32[]{:S(2)}, u32[]{:S(2)}) collective-permute-start(bf16[2,128,512]{2,1,0:T(8,128)(2,1)S(1)} %add_convert_fusion.11), channel_id=1, source_target_pairs={{0,1},{1,2},{2,3},{3,4},{4,5},{5,6},{6,7},{7,0},{8,9},{9,10},{10,1... | collective-permute-start | bytes 786440 | tf_op jit(solution)/shard_map/ppermute | solution.py:35
  165.3 15.0 %collective-permute-start.19 = (bf16[2,128,512]{2,1,0:T(8,128)(2,1)S(1)}, bf16[2,128,512]{2,1,0:T(8,128)(2,1)S(1)}, u32[]{:S(2)}, u32[]{:S(2)}) collective-permute-start(bf16[2,128,512]{2,1,0:T(8,128)(2,1)S(1)} %add_convert_fusion.8), channel_id=1, source_target_pairs={{0,7},{1,0},{2,1},{3,2},{4,3},{5,4},{6,5},{7,6},{8,15},{9,8},{10,9... | collective-permute-start | bytes 786440 | tf_op jit(solution)/shard_map/ppermute | solution.py:35
  170.6 17.3 %collective-permute-start.22 = (bf16[2,128,512]{2,1,0:T(8,128)(2,1)S(1)}, bf16[2,128,512]{2,1,0:T(8,128)(2,1)S(1)}, u32[]{:S(2)}, u32[]{:S(2)}) collective-permute-start(bf16[2,128,512]{2,1,0:T(8,128)(2,1)S(1)} %add_convert_fusion.5), channel_id=1, source_target_pairs={{0,1},{1,2},{2,3},{3,4},{4,5},{5,6},{6,7},{7,0},{8,9},{9,10},{10,1... | collective-permute-start | bytes 786440 | tf_op jit(solution)/shard_map/ppermute | solution.py:35
  180.3 20.1 %collective-permute-start.20 = (bf16[2,128,512]{2,1,0:T(8,128)(2,1)S(1)}, bf16[2,128,512]{2,1,0:T(8,128)(2,1)S(1)}, u32[]{:S(2)}, u32[]{:S(2)}) collective-permute-start(bf16[2,128,512]{2,1,0:T(8,128)(2,1)S(1)} %add_convert_fusion.7), channel_id=1, source_target_pairs={{0,7},{1,0},{2,1},{3,2},{4,3},{5,4},{6,5},{7,6},{8,15},{9,8},{10,9... | collective-permute-start | bytes 786440 | tf_op jit(solution)/shard_map/ppermute | solution.py:35
  188.1 14.9 %collective-permute-start.23 = (bf16[2,128,512]{2,1,0:T(8,128)(2,1)S(1)}, bf16[2,128,512]{2,1,0:T(8,128)(2,1)S(1)}, u32[]{:S(2)}, u32[]{:S(2)}) collective-permute-start(bf16[2,128,512]{2,1,0:T(8,128)(2,1)S(1)} %add_convert_fusion.4), channel_id=1, source_target_pairs={{0,1},{1,2},{2,3},{3,4},{4,5},{5,6},{6,7},{7,0},{8,9},{9,10},{10,1... | collective-permute-start | bytes 786440 | tf_op jit(solution)/shard_map/ppermute | solution.py:35
  220.3 16.5 %collective-permute-start.29 = (bf16[128,512]{1,0:T(8,128)(2,1)S(1)}, bf16[128,512]{1,0:T(8,128)(2,1)S(1)}, u32[]{:S(2)}, u32[]{:S(2)}) collective-permute-start(bf16[128,512]{1,0:T(8,128)(2,1)S(1)} %fusion.3), channel_id=1, source_target_pairs={{32,0},{64,32},{96,64},{128,96},{160,128},{192,160},{224,192},{256... | collective-permute-start | bytes 393224 | tf_op jit(solution)/shard_map/ppermute | solution.py:30
  (47 other events, 1268.1 us)

commit v4 on v2

--- a/solution.py
+++ b/solution.py
@@ -111,7 +111,22 @@
 
 
 def expert_kernel(
-    whole, gate_up, down_w, row_r, row_gate, partial, gate_part, along_part, rows, outs, sums, took, left
+    whole,
+    gate_up_hbm,
+    down_w,
+    row_r,
+    row_gate,
+    partial,
+    gate_part,
+    along_part,
+    gain_part,
+    rows,
+    outs,
+    sums,
+    gate_up,
+    took,
+    loaded,
+    left,
 ):
     pieces, experts, _, width = whole.shape
     capacity = whole.shape[2] // 3
@@ -123,17 +138,23 @@
             whole.at[z, :, pl.ds(k * capacity, capacity), :], rows.at[z, k], took.at[z, k]
         )
 
+    def load(z):
+        part = pl.ds(z * width, width)
+        return pltpu.make_async_copy(gate_up_hbm.at[part, :], gate_up.at[part, :], loaded.at[z])
+
     def put(z, k):
         return pltpu.make_async_copy(
             outs.at[z, k], partial.at[z, :, pl.ds(k * capacity, capacity), :], left.at[z, k]
         )
 
     for z in range(pieces):
+        load(z).start()
         for k in range(3):
             fetch(z, k).start()
     weighted = None
     for z in range(pieces):
         part = slice(z * width, (z + 1) * width)
+        load(z).wait()
         for k in range(3):
             fetch(z, k).wait()
         values = rows[z, 0:2].reshape(2 * slots, width)
@@ -162,7 +183,7 @@
         grad_first.astype(F32) * first + grad_second.astype(F32) * second, axis=1, keepdims=True
     )
     grads = jnp.concatenate([grad_first, grad_second], axis=1)
-    gate_f, gate_b = row_gate[:slots], row_gate[slots:]
+    gate_f, gate_b, r_b = row_gate[:slots], row_gate[slots:], row_r[slots:]
     for z in range(pieces):
         part = slice(z * width, (z + 1) * width)
         out_f = jnp.dot(inner_f, down_w[:, part], preferred_element_type=F32) * gate_f
@@ -176,6 +197,8 @@
         )
         outs[z, 1] = out_b.astype(BF16).reshape(experts, capacity, width)
         put(z, 1).start()
+        stashed = rows[z, 1].reshape(slots, width).astype(F32)
+        gain_part[z : z + 1, :] = jnp.sum(out_b * r_b * stashed, axis=0, keepdims=True)
     for z in range(pieces):
         for k in range(2):
             put(z, k).wait()
@@ -205,7 +228,7 @@
     slots = experts * capacity
     pieces = lax.axis_size("expert")
     vmem = pl.BlockSpec(memory_space=pltpu.VMEM)
-    hbm = pl.BlockSpec(memory_space=pl.ANY)
+    hbm = pl.BlockSpec(memory_space=pltpu.HBM)
     sent = pl.pallas_call(
         dispatch_kernel,
         out_shape=jax.ShapeDtypeStruct((experts, 3 * capacity, width), BF16),
@@ -222,7 +245,7 @@
     arrived = exchanged(sent, "dp")
     whole = lax.all_gather(arrived.reshape(3 * slots, width), "expert", axis=0, tiled=True)
 
-    (tokens, stashed, incoming, gain, routes_f, routes_b), arrived2 = lax.optimization_barrier(
+    (tokens, stashed, incoming, gain, routes_f, routes_b), _ = lax.optimization_barrier(
         ((tokens, stashed, incoming, gain, forward_routes[0], backward_routes[0]), arrived)
     )
     slot_f, placed_f, member_f = slots_of(routes_f, experts, capacity)
@@ -268,22 +291,24 @@
     scalars = scalars.transpose(1, 0, 2).reshape(4, slots)
     row_r = jnp.concatenate([scalars[0], scalars[2]])[:, None]
     row_gate = jnp.concatenate([scalars[1], scalars[3]])[:, None]
-    row_r_b = scalars[2].reshape(experts, capacity, 1)
-
-    partial, gate_part, along_part = pl.pallas_call(
+
+    partial, gate_part, along_part, rows_gain = pl.pallas_call(
         expert_kernel,
         out_shape=(
             jax.ShapeDtypeStruct((pieces, experts, 2 * capacity, width), BF16),
             jax.ShapeDtypeStruct((slots, 1), F32),
             jax.ShapeDtypeStruct((slots, 1), F32),
+            jax.ShapeDtypeStruct((pieces, width), F32),
         ),
-        in_specs=[hbm] + [vmem] * 4,
-        out_specs=(hbm, vmem, vmem),
+        in_specs=[hbm] * 2 + [vmem] * 3,
+        out_specs=(hbm, vmem, vmem, vmem),
         scratch_shapes=[
             pltpu.VMEM((pieces, 3, experts, capacity, width), BF16),
             pltpu.VMEM((pieces, 2, experts, capacity, width), BF16),
             pltpu.VMEM((2 * slots, 2 * hidden), F32),
+            pltpu.VMEM((D, 2 * hidden), BF16),
             pltpu.SemaphoreType.DMA((pieces, 3)),
+            pltpu.SemaphoreType.DMA((pieces,)),
             pltpu.SemaphoreType.DMA((pieces, 2)),
         ],
     )(whole.reshape(pieces, experts, 3 * capacity, width), gate_up, down_w, row_r, row_gate)
@@ -292,9 +317,13 @@
     )
     summed = summed.reshape(experts, 2 * capacity, width)
 
-    parts = jnp.stack([gate_part[:, 0], along_part[:, 0]])
-    parts = summed_over(parts, "expert")
-    parts = exchanged(parts.reshape(2, experts, capacity).transpose(1, 0, 2), "dp")
+    parts = jnp.concatenate([gate_part[:, 0], along_part[:, 0]])
+    parts = jnp.stack([jnp.broadcast_to(parts, (pieces, 2 * slots)), rows_gain], 1)
+    parts = exchanged(parts, "expert")
+    parts = jnp.sum(parts, axis=0)
+    rows_gain = parts[1]
+    parts = parts[0].reshape(2, experts, capacity).transpose(1, 0, 2)
+    parts = exchanged(parts, "dp")
     parts = parts.transpose(1, 0, 2).reshape(2, slots)
 
     def by_token(values):
@@ -314,6 +343,8 @@
         preferred_element_type=F32,
     )
     own_gain = jnp.sum(router_part * stashed32 * r_b[:, None], axis=0)
+    gain_total = summed_over((own_gain + rows_gain / gain)[None], "dp")[0]
+    summed, gain_total = lax.optimization_barrier((summed, gain_total))
     base = (
         incoming.astype(F32)
         + (r_b[:, None] * router_part) * gain
@@ -321,19 +352,6 @@
     )
 
     back = exchanged(summed, "dp")
-    gain_part = own_gain + (
-        jnp.sum(
-            summed[:, capacity:].astype(F32)
-            * arrived2[:, capacity : 2 * capacity].astype(F32)
-            * row_r_b,
-            axis=(0, 1),
-        )
-        / gain
-    )
-    others = [rotated(gain_part[None], "dp", distance) for distance in range(1, experts)]
-    back, others = lax.optimization_barrier((back, others))
-    gain_total = gain_part + sum(other[0] for other in others)
-
     def gathered(spread, rows):
         return lax.dot_general(
             spread,

time: 217 us -> 213 us (0.982)
  blocking collectives: 17.4 us -> 37.7 us
  starting transfers between devices: 44.1 us -> 27.8 us
  waiting for transfers between devices: 110 us -> 103 us
    all_to_all x1 -> x3, blocking collectives: 17.4 us -> 37.7 us  [exchanged(): return lax.all_to_all(blocks, axis, split_axis=0, concat_axis=0, tiled=True)]
    ppermute x3 -> x0, starting transfers between devices: 12.2 us -> none  [rotated(): lax.ppermute(block, axis, [(i, (i + distance) % size) for i in range(size)])]
    reduce_scatter x1, waiting for transfers between devices: 32.5 us -> 24 us  [local(): lax.psum_scatter(partial.reshape(pieces * 2 * slots, width), 'expert', sc...]
    all_to_all x3 -> x2, waiting for transfers between devices: 8.8 us -> 13.8 us  [exchanged(): return lax.all_to_all(blocks, axis, split_axis=0, concat_axis=0, tiled=True)]
    all_to_all x3 -> x2, starting transfers between devices: 10.1 us -> 6.72 us  [exchanged(): return lax.all_to_all(blocks, axis, split_axis=0, concat_axis=0, tiled=True)]
    all_to_all x2, waiting for transfers between devices: 15.9 us -> 13.4 us  [summed_over(): lax.all_to_all(copies, axis, split_axis=0, concat_axis=0, tiled=True)]
    unnamed x31 -> x33, local copies, waits for them, and re-layouts: 5.27 us -> 4.69 us
  transfers between devices with their start and end apart: 12 -> 8, of which waited for: 9 -> 8; matrix products, arithmetic and copies ran while one was open for 7% -> 7% of each run, Pallas kernels for 0% -> 0%
where the time goes in v4:
time: 213 us; the launch traced here: 212 us
  waiting for transfers between devices  103 us (48%)
  blocking collectives  37.7 us (18%)
  starting transfers between devices  27.8 us (13%)
  between operations  14.4 us (7%)
  Pallas kernels  12.5 us (6%)
  local copies, waits for them, and re-layouts  9.32 us (4%)
  other arithmetic  4.15 us (2%)
  matrix products  3.2 us (2%)
    all_gather x1, waiting for transfers between devices, local(): lax.all_gather(arrived.reshape(3 * slots, width), 'expert', axis=0, tiled...  45 us
    all_to_all x3, blocking collectives, exchanged(): return lax.all_to_all(blocks, axis, split_axis=0, concat_axis=0, tiled=True)  37.7 us
    reduce_scatter x1, waiting for transfers between devices, local(): lax.psum_scatter(partial.reshape(pieces * 2 * slots, width), 'expert', sc...  24 us
    all_to_all x2, waiting for transfers between devices, exchanged(): return lax.all_to_all(blocks, axis, split_axis=0, concat_axis=0, tiled=True)  13.8 us
    all_to_all x2, starting transfers between devices, summed_over(): lax.all_to_all(copies, axis, split_axis=0, concat_axis=0, tiled=True)  13.6 us
    all_to_all x2, waiting for transfers between devices, summed_over(): lax.all_to_all(copies, axis, split_axis=0, concat_axis=0, tiled=True)  13.4 us
    pallas_call x1, Pallas kernels, local(): pl.pallas_call(expert_kernel, out_shape=(jax.ShapeDtypeStruct((pieces, ex...  9.95 us
    ppermute x2, starting transfers between devices, shifted(): return lax.ppermute(block, axis, route)  7.46 us
  transfers between devices with their start and end apart: 8, of which 8 were waited for; matrix products, arithmetic and copies ran while one was open for 7% of the time, Pallas kernels for 0%

profile of v4, /device:TPU:2, one launch (start us, length us, event | category | flops | bytes accessed | tf_op | source)
XLA Modules:
  0.0 212.4 jit_solution(1614392683235526586)
XLA Ops:
  7.3 2.6 %shard_map.128 = bf16[4,192,512]{2,1,0:T(8,128)(2,1)} custom-call(s32[2,128]{1,0:T(2,128)} %bitcast.101, s32[2,128]{1,0:T(2,128)} %bitcast.96, f32[1,512]{1,0:T(1,128)} %gain.1, bf16[128,512]{1,0:T(8,128)(2,1)} %bitcast.77, bf16[128,512]{1,0:T(8,128)(2,1)} %bitcast.81, bf16[128,512]{1,0:T(8,128)(2,1)} %bitcast.90), custom_call_target="tpu_custom_call" | custom-call | tf_op jit(solution)/shard_map/pallas_call | solution.py:232
  9.8 17.4 %all_to_all.35 = bf16[4,192,512]{2,1,0:T(8,128)(2,1)} all-to-all(bf16[4,192,512]{2,1,0:T(8,128)(2,1)} %shard_map.128), channel_id=1, replica_groups=mesh['pipe'=16,'dp'=4,'expert'=8] {'dp'}, dimensions={0} | all-to-all | bytes 1572864 | tf_op jit(solution)/shard_map/all_to_all | solution.py:21
  27.2 1.1 fusion.4
  28.4 1.1 convolution_bitcast_fusion
  29.4 1.1 convolution_bitcast_fusion.1
  31.2 10.3 %all-to-all-start.1 = ((f32[8,16,128]{2,1,0:T(8,128)}), f32[8,16,128]{2,1,0:T(8,128)S(1)}, u32[]{:S(2)}, u32[]{:S(2)}) async-start(f32[8,16,128]{2,1,0:T(8,128)} %broadcast_in_dim.123), calls=%async_computation.1 | async-start | bytes 131072 | tf_op jit(solution)/shard_map/all_to_all | solution.py:17
  41.8 8.2 %all-to-all-done.1 = f32[8,16,128]{2,1,0:T(8,128)S(1)} async-done(((f32[8,16,128]{2,1,0:T(8,128)}), f32[8,16,128]{2,1,0:T(8,128)S(1)}, u32[]{:S(2)}, u32[]{:S(2)}) %all-to-all-start.1) | async-done | bytes 65568 | tf_op jit(solution)/shard_map/all_to_all | solution.py:17
  51.5 3.2 %all-to-all-start.2 = ((f32[4,1,256]{2,1,0:T(1,128)}), f32[4,1,256]{2,1,0:T(1,128)S(1)}, u32[]{:S(2)}, u32[]{:S(2)}) async-start(f32[4,1,256]{2,1,0:T(1,128)} %reshape.257), calls=%async_computation.2 | async-start | bytes 8192 | tf_op jit(solution)/shard_map/all_to_all | solution.py:21
  54.9 1.6 copy.35
  56.4 3.6 %all-to-all-done.2 = f32[4,1,256]{2,1,0:T(1,128)S(1)} async-done(((f32[4,1,256]{2,1,0:T(1,128)}), f32[4,1,256]{2,1,0:T(1,128)S(1)}, u32[]{:S(2)}, u32[]{:S(2)}) %all-to-all-start.2) | async-done | bytes 4128 | tf_op jit(solution)/shard_map/all_to_all | solution.py:21
  61.5 0.9 copy.28.row_gate
  62.6 0.9 copy.27.row_r
  63.4 45.0 %all-gather.2.cloned.1.call-done = bf16[6144,512]{1,0:T(8,128)(2,1)} async-done(((bf16[768,512]{1,0:T(8,128)(2,1)}), bf16[6144,512]{1,0:T(8,128)(2,1)}) %all-gather.2.cloned.1.call-update) | async-done | bytes 6291472 | tf_op jit(solution)/shard_map/all_gather | solution.py:246
  108.4 10.0 %shard_map.129 = (bf16[8,4,128,512]{3,2,1,0:T(8,128)(2,1)}, f32[256,1]{1,0:T(8,128)}, f32[256,1]{1,0:T(8,128)}, f32[8,512]{1,0:T(8,128)}) custom-call(bf16[8,4,192,512]{3,2,1,0:T(8,128)(2,1)} %bitcast.73, bf16[4096,256]{1,0:T(8,128)(2,1)} %bitcast.72, bf16[128,4096]{1,0:T(8,128)(2,1)} %bitcast.86, f32[512,1]{1,0:T(8,128)} %copy.27.row_r, f32[512,1]{1,0:T(8,128)} %copy.28.row_gate), custom_call_target="tpu_custom_call" | custom-call | tf_op jit(solution)/shard_map/pallas_call | solution.py:295
  119.6 11.9 %all_to_all.36 = f32[8,2,512]{2,1,0:T(2,128)S(1)} all-to-all(f32[8,2,512]{2,1,0:T(2,128)S(1)} %copy.29), channel_id=1, replica_groups=mesh['pipe'=16,'dp'=4,'expert'=8] {'expert'}, dimensions={0} | all-to-all | bytes 65536 | tf_op jit(solution)/shard_map/all_to_all | solution.py:21
  131.7 8.4 %all_to_all.37 = f32[4,1,128]{2,1,0:T(1,128)S(1)} all-to-all(f32[4,1,128]{2,1,0:T(1,128)S(1)} %reshape.259), channel_id=1, replica_groups=mesh['pipe'=16,'dp'=4,'expert'=8] {'dp'}, dimensions={0} | all-to-all | bytes 4096 | tf_op jit(solution)/shard_map/all_to_all | solution.py:21
  142.3 3.2 %all-to-all-start.5 = ((f32[4,1,512]{2,1,0:T(1,128)}), f32[4,1,512]{2,1,0:T(1,128)S(1)}, u32[]{:S(2)}, u32[]{:S(2)}) async-start(f32[4,1,512]{2,1,0:T(1,128)} %broadcast_in_dim.132), calls=%async_computation.6 | async-start | bytes 16384 | tf_op jit(solution)/shard_map/all_to_all | solution.py:17
  145.6 5.2 %all-to-all-done.5 = f32[4,1,512]{2,1,0:T(1,128)S(1)} async-done(((f32[4,1,512]{2,1,0:T(1,128)}), f32[4,1,512]{2,1,0:T(1,128)S(1)}, u32[]{:S(2)}, u32[]{:S(2)}) %all-to-all-start.5) | async-done | bytes 8224 | tf_op jit(solution)/shard_map/all_to_all | solution.py:17
  151.4 24.0 %reduce-scatter.2.cloned.1.call-done = bf16[512,512]{1,0:T(8,128)(2,1)} async-done(((bf16[4096,512]{1,0:T(8,128)(2,1)}), bf16[512,512]{1,0:T(8,128)(2,1)}) %reduce-scatter.2.cloned.1.call-update) | async-done | bytes 524304 | tf_op jit(solution)/shard_map/reduce_scatter | solution.py:315
  175.4 3.5 %all-to-all-start.6 = ((bf16[4,128,512]{2,1,0:T(8,128)(2,1)}), bf16[4,128,512]{2,1,0:T(8,128)(2,1)S(1)}, u32[]{:S(2)}, u32[]{:S(2)}) async-start(bf16[4,128,512]{2,1,0:T(8,128)(2,1)} %bitcast.88), calls=%async_computation.7 | async-start | bytes 1048576 | tf_op jit(solution)/shard_map/all_to_all | solution.py:21
  178.9 10.2 %all-to-all-done.6 = bf16[4,128,512]{2,1,0:T(8,128)(2,1)S(1)} async-done(((bf16[4,128,512]{2,1,0:T(8,128)(2,1)}), bf16[4,128,512]{2,1,0:T(8,128)(2,1)S(1)}, u32[]{:S(2)}, u32[]{:S(2)}) %all-to-all-start.6) | async-done | bytes 524320 | tf_op jit(solution)/shard_map/all_to_all | solution.py:21
  189.5 5.5 %collective-permute-start.1 = (bf16[128,512]{1,0:T(8,128)(2,1)S(1)}, bf16[128,512]{1,0:T(8,128)(2,1)S(1)}, u32[]{:S(2)}, u32[]{:S(2)}) collective-permute-start(bf16[128,512]{1,0:T(8,128)(2,1)S(1)} %fusion.3), channel_id=1, source_target_pairs={{32,0},{64,32},{96,64},{128,96},{160,128},{192,160},{224,192},{256... | collective-permute-start | bytes 393224 | tf_op jit(solution)/shard_map/ppermute | solution.py:27
  195.3 1.9 collective-permute-start
  197.5 6.7 %collective-permute-done = bf16[128,512]{1,0:T(8,128)(2,1)S(1)} collective-permute-done((bf16[128,512]{1,0:T(8,128)(2,1)S(1)}, bf16[128,512]{1,0:T(8,128)(2,1)S(1)}, u32[]{:S(2)}, u32[]{:S(2)}) %collective-permute-start) | collective-permute-done | bytes 131104 | tf_op jit(solution)/shard_map/ppermute | solution.py:27
  (100 shorter events, 10.6 us)
Async XLA Ops:
  7.2 21.2 %copy-start = (bf16[1,512,4]{1,2,0:T(4,128)(2,1)S(1)}, bf16[1,512,4]{1,2,0:T(4,128)(2,1)}, u32[]{:S(2)}) copy-start(bf16[1,512,4]{1,2,0:T(4,128)(2,1)} %param.15) | copy-start | bytes 12292
  7.2 34.4 %copy-start.9 = (s32[1,128,2]{1,2,0:T(2,128)S(1)}, s32[1,128,2]{1,2,0:T(2,128)}, u32[]{:S(2)}) copy-start(s32[1,128,2]{1,2,0:T(2,128)} %param.12) | copy-start | bytes 3076
  7.2 34.4 %copy-start.8 = (s32[1,128,2]{1,2,0:T(2,128)S(1)}, s32[1,128,2]{1,2,0:T(2,128)}, u32[]{:S(2)}) copy-start(s32[1,128,2]{1,2,0:T(2,128)} %param.13) | copy-start | bytes 3076
  7.2 47.7 %copy-start.1 = (bf16[1,1,4096,2,128]{4,3,2,1,0:T(2,128)(2,1)S(1)}, bf16[1,1,4096,2,128]{4,3,2,1,0:T(2,128)(2,1)}, u32[]{:S(2)}) copy-start(bf16[1,1,4096,2,128]{4,3,2,1,0:T(2,128)(2,1)} %param.16) | copy-start | bytes 6291460
  7.2 101.2 %all-gather.2.cloned.1.call-start = ((), (), s32[]{:S(2)}) async-start(), calls=%async_computation.8 | async-start | bytes 7077888 | tf_op jit(solution)/shard_map/all_gather | solution.py:246
  31.2 18.8 %all-to-all-start.1 = ((f32[8,16,128]{2,1,0:T(8,128)}), f32[8,16,128]{2,1,0:T(8,128)S(1)}, u32[]{:S(2)}, u32[]{:S(2)}) async-start(f32[8,16,128]{2,1,0:T(8,128)} %broadcast_in_dim.123), calls=%async_computation.1 | async-start | bytes 131072 | tf_op jit(solution)/shard_map/all_to_all | solution.py:17
  51.5 8.5 %all-to-all-start.2 = ((f32[4,1,256]{2,1,0:T(1,128)}), f32[4,1,256]{2,1,0:T(1,128)S(1)}, u32[]{:S(2)}, u32[]{:S(2)}) async-start(f32[4,1,256]{2,1,0:T(1,128)} %reshape.257), calls=%async_computation.2 | async-start | bytes 8192 | tf_op jit(solution)/shard_map/all_to_all | solution.py:21
  54.8 120.6 %reduce-scatter.2.cloned.1.call-start = ((), (), s32[]{:S(2)}) async-start(), calls=%async_computation.9 | async-start | bytes 4718592 | tf_op jit(solution)/shard_map/reduce_scatter | solution.py:315
  118.4 0.9 copy-start.7
  118.4 1.0 copy-start.6
  118.4 1.1 copy-start.10
  118.4 22.9 %copy-start.3 = (bf16[1,128,512]{2,1,0:T(8,128)(2,1)S(1)}, bf16[1,128,512]{2,1,0:T(8,128)(2,1)}, u32[]{:S(2)}) copy-start(bf16[1,128,512]{2,1,0:T(8,128)(2,1)} %param.11) | copy-start | bytes 393220
  118.4 23.2 %copy-start.11 = (f32[1,512]{1,0:T(1,128)S(1)}, f32[1,512]{1,0:T(1,128)}, u32[]{:S(2)}) copy-start(f32[1,512]{1,0:T(1,128)} %gain.1) | copy-start | bytes 6148
  118.5 70.7 %copy-start.4 = (bf16[1,128,512]{2,1,0:T(8,128)(2,1)S(1)}, bf16[1,128,512]{2,1,0:T(8,128)(2,1)}, u32[]{:S(2)}) copy-start(bf16[1,128,512]{2,1,0:T(8,128)(2,1)} %param.10) | copy-start | bytes 393220
  118.5 76.6 %copy-start.2 = (bf16[1,128,512]{2,1,0:T(8,128)(2,1)S(1)}, bf16[1,128,512]{2,1,0:T(8,128)(2,1)}, u32[]{:S(2)}) copy-start(bf16[1,128,512]{2,1,0:T(8,128)(2,1)} %param.9) | copy-start | bytes 393220
  142.3 8.5 %all-to-all-start.5 = ((f32[4,1,512]{2,1,0:T(1,128)}), f32[4,1,512]{2,1,0:T(1,128)S(1)}, u32[]{:S(2)}, u32[]{:S(2)}) async-start(f32[4,1,512]{2,1,0:T(1,128)} %broadcast_in_dim.132), calls=%async_computation.6 | async-start | bytes 16384 | tf_op jit(solution)/shard_map/all_to_all | solution.py:17
  175.4 13.8 %all-to-all-start.6 = ((bf16[4,128,512]{2,1,0:T(8,128)(2,1)}), bf16[4,128,512]{2,1,0:T(8,128)(2,1)S(1)}, u32[]{:S(2)}, u32[]{:S(2)}) async-start(bf16[4,128,512]{2,1,0:T(8,128)(2,1)} %bitcast.88), calls=%async_computation.7 | async-start | bytes 1048576 | tf_op jit(solution)/shard_map/all_to_all | solution.py:21
  189.5 16.1 %copy-start.12 = (bf16[128,512]{1,0:T(8,128)(2,1)}, bf16[128,512]{1,0:T(8,128)(2,1)S(1)}, u32[]{:S(2)}) copy-start(bf16[128,512]{1,0:T(8,128)(2,1)S(1)} %fusion.3) | copy-start | bytes 393220
  189.5 8.1 %collective-permute-start.1 = (bf16[128,512]{1,0:T(8,128)(2,1)S(1)}, bf16[128,512]{1,0:T(8,128)(2,1)S(1)}, u32[]{:S(2)}, u32[]{:S(2)}) collective-permute-start(bf16[128,512]{1,0:T(8,128)(2,1)S(1)} %fusion.3), channel_id=1, source_target_pairs={{32,0},{64,32},{96,64},{128,96},{160,128},{192,160},{224,192},{256... | collective-permute-start | bytes 393224 | tf_op jit(solution)/shard_map/ppermute | solution.py:27
  195.3 10.3 %copy-start.5 = (bf16[128,512]{1,0:T(8,128)(2,1)}, bf16[128,512]{1,0:T(8,128)(2,1)S(1)}, u32[]{:S(2)}) copy-start(bf16[128,512]{1,0:T(8,128)(2,1)S(1)} %fusion.2) | copy-start | bytes 393220
  195.3 9.0 %collective-permute-start = (bf16[128,512]{1,0:T(8,128)(2,1)S(1)}, bf16[128,512]{1,0:T(8,128)(2,1)S(1)}, u32[]{:S(2)}, u32[]{:S(2)}) collective-permute-start(bf16[128,512]{1,0:T(8,128)(2,1)S(1)} %fusion.2), channel_id=1, source_target_pairs={{0,32},{32,64},{64,96},{96,128},{128,160},{160,192},{192,224},{224... | collective-permute-start | bytes 393224 | tf_op jit(solution)/shard_map/ppermute | solution.py:27
Sparse Core Ops, SparseCore 0:
  27.4 81.0 all-gather.1
  118.6 56.7 reduce-scatter.1

commit v5 on v4

--- a/solution.py
+++ b/solution.py
@@ -1,3 +1,5 @@
+import functools
+
 import jax
 import jax.numpy as jnp
 from jax import lax
@@ -30,6 +32,17 @@
 def rotated(block, axis, distance):
     size = lax.axis_size(axis)
     return lax.ppermute(block, axis, [(i, (i + distance) % size) for i in range(size)])
+
+
+def ring_gather(block, axis):
+    size = lax.axis_size(axis)
+    middle = size // 2
+    found = [block] + [None] * (size - 1)
+    for step in range(1, middle):
+        found[size - step] = rotated(found[(size - step + 1) % size], axis, 1)
+        found[step] = rotated(found[step - 1], axis, -1)
+    found[middle] = rotated(found[middle + 1], axis, 1)
+    return found
 
 
 def slots_of(routes, experts, capacity):
@@ -111,31 +124,35 @@
 
 
 def expert_kernel(
+    pieces,
+    at,
     whole,
     gate_up_hbm,
     down_w,
     row_r,
     row_gate,
-    partial,
-    gate_part,
-    along_part,
-    gain_part,
-    rows,
-    outs,
-    sums,
-    gate_up,
-    took,
-    loaded,
-    left,
+    *refs,
 ):
-    pieces, experts, _, width = whole.shape
-    capacity = whole.shape[2] // 3
+    ringed, refs = refs[:pieces], refs[pieces:]
+    partial, gate_part, along_part, gain_part, rows, outs, sums, gate_up, took, came, loaded, left = refs
+    experts, capacity, width = rows.shape[2:]
     slots = experts * capacity
     hidden = down_w.shape[0]
 
-    def fetch(z, k):
+    def fetch(z, k, e):
         return pltpu.make_async_copy(
-            whole.at[z, :, pl.ds(k * capacity, capacity), :], rows.at[z, k], took.at[z, k]
+            whole.at[z, pl.ds((3 * e + k) * capacity, capacity), :],
+            rows.at[z, k, e],
+            took.at[z, k, e],
+        )
+
+    fetched = [(k, e) for k in range(3) for e in range(experts) if k == 0 or e < experts - 1]
+
+    def place(j, k):
+        return pltpu.make_async_copy(
+            ringed[j].at[pl.ds((k - 1) * capacity, capacity), :],
+            rows.at[(at[0] + j) % pieces, k, experts - 1],
+            came.at[j, k - 1],
         )
 
     def load(z):
@@ -149,14 +166,19 @@
 
     for z in range(pieces):
         load(z).start()
-        for k in range(3):
-            fetch(z, k).start()
+        for k, e in fetched:
+            fetch(z, k, e).start()
+        for k in range(1, 3):
+            place(z, k).start()
+    for j in range(pieces):
+        for k in range(1, 3):
+            place(j, k).wait()
     weighted = None
     for z in range(pieces):
         part = slice(z * width, (z + 1) * width)
         load(z).wait()
-        for k in range(3):
-            fetch(z, k).wait()
+        for k, e in fetched:
+            fetch(z, k, e).wait()
         values = rows[z, 0:2].reshape(2 * slots, width)
         product = jnp.dot(values, gate_up[part, :], preferred_element_type=F32)
         incoming = rows[z, 2].reshape(slots, width)
@@ -243,7 +265,10 @@
         incoming,
     )
     arrived = exchanged(sent, "dp")
-    whole = lax.all_gather(arrived.reshape(3 * slots, width), "expert", axis=0, tiled=True)
+    arrived_rows = arrived.reshape(3 * slots, width)
+    native = 3 * slots - 2 * capacity
+    whole = lax.all_gather(arrived_rows[:native], "expert", axis=0, tiled=True)
+    ringed = ring_gather(arrived_rows[native:], "expert")
 
     (tokens, stashed, incoming, gain, routes_f, routes_b), _ = lax.optimization_barrier(
         ((tokens, stashed, incoming, gain, forward_routes[0], backward_routes[0]), arrived)
@@ -293,25 +318,34 @@
     row_gate = jnp.concatenate([scalars[1], scalars[3]])[:, None]
 
     partial, gate_part, along_part, rows_gain = pl.pallas_call(
-        expert_kernel,
+        functools.partial(expert_kernel, pieces),
         out_shape=(
             jax.ShapeDtypeStruct((pieces, experts, 2 * capacity, width), BF16),
             jax.ShapeDtypeStruct((slots, 1), F32),
             jax.ShapeDtypeStruct((slots, 1), F32),
             jax.ShapeDtypeStruct((pieces, width), F32),
         ),
-        in_specs=[hbm] * 2 + [vmem] * 3,
+        in_specs=[pl.BlockSpec(memory_space=pltpu.SMEM)] + [hbm] * 2 + [vmem] * 3 + [hbm] * pieces,
         out_specs=(hbm, vmem, vmem, vmem),
         scratch_shapes=[
             pltpu.VMEM((pieces, 3, experts, capacity, width), BF16),
             pltpu.VMEM((pieces, 2, experts, capacity, width), BF16),
             pltpu.VMEM((2 * slots, 2 * hidden), F32),
             pltpu.VMEM((D, 2 * hidden), BF16),
-            pltpu.SemaphoreType.DMA((pieces, 3)),
+            pltpu.SemaphoreType.DMA((pieces, 3, experts)),
+            pltpu.SemaphoreType.DMA((pieces, 2)),
             pltpu.SemaphoreType.DMA((pieces,)),
             pltpu.SemaphoreType.DMA((pieces, 2)),
         ],
-    )(whole.reshape(pieces, experts, 3 * capacity, width), gate_up, down_w, row_r, row_gate)
+    )(
+        lax.axis_index("expert")[None].astype(jnp.int32),
+        whole.reshape(pieces, native, width),
+        gate_up,
+        down_w,
+        row_r,
+        row_gate,
+        *ringed,
+    )
     summed = lax.psum_scatter(
         partial.reshape(pieces * 2 * slots, width), "expert", scatter_dimension=0, tiled=True
     )

time: 213 us -> 215 us (level)
  starting transfers between devices: 27.8 us -> 50.8 us
  waiting for transfers between devices: 103 us -> 82.5 us
  Pallas kernels: 12.5 us -> 14.7 us
    all_gather x1, waiting for transfers between devices: 45 us -> 12.1 us  [local(): whole = lax.all_gather(arrived_rows[:native], 'expert', axis=0, tiled=True)]
    ppermute x0 -> x7, starting transfers between devices: none -> 28.9 us  [rotated(): lax.ppermute(block, axis, [(i, (i + distance) % size) for i in range(size)])]
    ppermute x0 -> x7, waiting for transfers between devices: none -> 11.4 us  [rotated(): lax.ppermute(block, axis, [(i, (i + distance) % size) for i in range(size)])]
    all_to_all x2, starting transfers between devices: 13.6 us -> 7.72 us  [summed_over(): lax.all_to_all(copies, axis, split_axis=0, concat_axis=0, tiled=True)]
    unnamed x33 -> x49, local copies, waits for them, and re-layouts: 4.69 us -> 4.76 us
  transfers between devices with their start and end apart: 8 -> 15, of which waited for: 8 -> 11; matrix products, arithmetic and copies ran while one was open for 7% -> 5% of each run, Pallas kernels for 0% -> 0%
where the time goes in v5:
time: 215 us; the launch traced here: 214 us
  waiting for transfers between devices  82.5 us (38%)
  starting transfers between devices  50.8 us (24%)
  blocking collectives  36.4 us (17%)
  Pallas kernels  14.7 us (7%)
  between operations  14.6 us (7%)
  local copies, waits for them, and re-layouts  10.3 us (5%)
  other arithmetic  3.13 us (1%)
    all_to_all x3, blocking collectives, exchanged(): return lax.all_to_all(blocks, axis, split_axis=0, concat_axis=0, tiled=True)  36.4 us
    ppermute x7, starting transfers between devices, rotated(): lax.ppermute(block, axis, [(i, (i + distance) % size) for i in range(size)])  28.9 us
    reduce_scatter x1, waiting for transfers between devices, local(): lax.psum_scatter(partial.reshape(pieces * 2 * slots, width), 'expert', sc...  24 us
    all_to_all x2, waiting for transfers between devices, summed_over(): lax.all_to_all(copies, axis, split_axis=0, concat_axis=0, tiled=True)  14.1 us
    all_to_all x2, waiting for transfers between devices, exchanged(): return lax.all_to_all(blocks, axis, split_axis=0, concat_axis=0, tiled=True)  13.8 us
    all_gather x1, waiting for transfers between devices, local(): whole = lax.all_gather(arrived_rows[:native], 'expert', axis=0, tiled=True)  12.1 us
    pallas_call x1, Pallas kernels, local(): pl.pallas_call(functools.partial(expert_kernel, pieces), out_shape=(jax.S...  12.1 us
    ppermute x7, waiting for transfers between devices, rotated(): lax.ppermute(block, axis, [(i, (i + distance) % size) for i in range(size)])  11.4 us
  transfers between devices with their start and end apart: 15, of which 11 were waited for; matrix products, arithmetic and copies ran while one was open for 5% of the time, Pallas kernels for 0%

profile of v5, /device:TPU:2, one launch (start us, length us, event | category | flops | bytes accessed | tf_op | source)
XLA Modules:
  0.0 214.0 jit_solution(14004900347265393495)
XLA Ops:
  7.3 2.7 %shard_map.128 = bf16[4,192,512]{2,1,0:T(8,128)(2,1)} custom-call(s32[2,128]{1,0:T(2,128)} %bitcast.103, s32[2,128]{1,0:T(2,128)} %bitcast.98, f32[1,512]{1,0:T(1,128)} %gain.1, bf16[128,512]{1,0:T(8,128)(2,1)} %bitcast.79, bf16[128,512]{1,0:T(8,128)(2,1)} %bitcast.83, bf16[128,512]{1,0:T(8,128)(2,1)} %bitcast.92), custom_call_target="tpu_custom_call" | custom-call | tf_op jit(solution)/shard_map/pallas_call | solution.py:254
  10.0 16.6 %all_to_all.35 = bf16[4,192,512]{2,1,0:T(8,128)(2,1)S(1)} all-to-all(bf16[4,192,512]{2,1,0:T(8,128)(2,1)} %shard_map.128), channel_id=1, replica_groups=mesh['pipe'=16,'dp'=4,'expert'=8] {'dp'}, dimensions={0} | all-to-all | bytes 1572864 | tf_op jit(solution)/shard_map/all_to_all | solution.py:23
  27.5 4.3 %collective-permute-start.3 = (bf16[128,512]{1,0:T(8,128)(2,1)S(1)}, bf16[128,512]{1,0:T(8,128)(2,1)S(1)}, u32[]{:S(2)}, u32[]{:S(2)}) collective-permute-start(bf16[128,512]{1,0:T(8,128)(2,1)S(1)} %slice.98.refs_0_), channel_id=1, source_target_pairs={{0,1},{1,2},{2,3},{3,4},{4,5},{5,6},{6,7},{7,0},{8,9},{9,10},{10,1... | collective-permute-start | bytes 393224 | tf_op jit(solution)/shard_map/ppermute | solution.py:34
  31.8 8.6 %collective-permute-start = (bf16[128,512]{1,0:T(8,128)(2,1)S(1)}, bf16[128,512]{1,0:T(8,128)(2,1)S(1)}, u32[]{:S(2)}, u32[]{:S(2)}) collective-permute-start(bf16[128,512]{1,0:T(8,128)(2,1)S(1)} %slice.98.refs_0_), channel_id=1, source_target_pairs={{0,7},{1,0},{2,1},{3,2},{4,3},{5,4},{6,5},{7,6},{8,15},{9,8},{10,9... | collective-permute-start | bytes 393224 | tf_op jit(solution)/shard_map/ppermute | solution.py:34
  41.6 4.5 %all-to-all-start.1 = ((f32[8,16,128]{2,1,0:T(8,128)}), f32[8,16,128]{2,1,0:T(8,128)S(1)}, u32[]{:S(2)}, u32[]{:S(2)}) async-start(f32[8,16,128]{2,1,0:T(8,128)} %broadcast_in_dim.127), calls=%async_computation.1 | async-start | bytes 131072 | tf_op jit(solution)/shard_map/all_to_all | solution.py:19
  46.4 8.9 %all-to-all-done.1 = f32[8,16,128]{2,1,0:T(8,128)S(1)} async-done(((f32[8,16,128]{2,1,0:T(8,128)}), f32[8,16,128]{2,1,0:T(8,128)S(1)}, u32[]{:S(2)}, u32[]{:S(2)}) %all-to-all-start.1) | async-done | bytes 65568 | tf_op jit(solution)/shard_map/all_to_all | solution.py:19
  55.5 2.5 %collective-permute-start.4 = (bf16[128,512]{1,0:T(8,128)(2,1)S(1)}, bf16[128,512]{1,0:T(8,128)(2,1)S(1)}, u32[]{:S(2)}, u32[]{:S(2)}) collective-permute-start(bf16[128,512]{1,0:T(8,128)(2,1)S(1)} %collective-permute-done.3.refs_7_), channel_id=1, source_target_pairs={{0,1},{1,2},{2,3},{3,4},{4,5},{5,6},{6,7},{7,0},{8,9},{9,10},{10,1... | collective-permute-start | bytes 393224 | tf_op jit(solution)/shard_map/ppermute | solution.py:34
  58.6 4.6 %collective-permute-start.1 = (bf16[128,512]{1,0:T(8,128)(2,1)S(1)}, bf16[128,512]{1,0:T(8,128)(2,1)S(1)}, u32[]{:S(2)}, u32[]{:S(2)}) collective-permute-start(bf16[128,512]{1,0:T(8,128)(2,1)S(1)} %collective-permute-done.refs_1_), channel_id=1, source_target_pairs={{0,7},{1,0},{2,1},{3,2},{4,3},{5,4},{6,5},{7,6},{8,15},{9,8},{10,9... | collective-permute-start | bytes 393224 | tf_op jit(solution)/shard_map/ppermute | solution.py:34
  63.2 3.4 %collective-permute-done.4.refs_6_ = bf16[128,512]{1,0:T(8,128)(2,1)S(1)} collective-permute-done((bf16[128,512]{1,0:T(8,128)(2,1)S(1)}, bf16[128,512]{1,0:T(8,128)(2,1)S(1)}, u32[]{:S(2)}, u32[]{:S(2)}) %collective-permute-start.4) | collective-permute-done | bytes 131104 | tf_op jit(solution)/shard_map/ppermute | solution.py:34
  69.2 3.2 %all-to-all-start.2 = ((f32[4,1,256]{2,1,0:T(1,128)}), f32[4,1,256]{2,1,0:T(1,128)S(1)}, u32[]{:S(2)}, u32[]{:S(2)}) async-start(f32[4,1,256]{2,1,0:T(1,128)} %reshape.257), calls=%async_computation.2 | async-start | bytes 8192 | tf_op jit(solution)/shard_map/all_to_all | solution.py:23
  74.1 3.6 %all-to-all-done.2 = f32[4,1,256]{2,1,0:T(1,128)S(1)} async-done(((f32[4,1,256]{2,1,0:T(1,128)}), f32[4,1,256]{2,1,0:T(1,128)S(1)}, u32[]{:S(2)}, u32[]{:S(2)}) %all-to-all-start.2) | async-done | bytes 4128 | tf_op jit(solution)/shard_map/all_to_all | solution.py:23
  79.2 5.1 %collective-permute-start.2 = (bf16[128,512]{1,0:T(8,128)(2,1)S(1)}, bf16[128,512]{1,0:T(8,128)(2,1)S(1)}, u32[]{:S(2)}, u32[]{:S(2)}) collective-permute-start(bf16[128,512]{1,0:T(8,128)(2,1)S(1)} %collective-permute-done.1.refs_2_), channel_id=1, source_target_pairs={{0,7},{1,0},{2,1},{3,2},{4,3},{5,4},{6,5},{7,6},{8,15},{9,8},{10,9... | collective-permute-start | bytes 393224 | tf_op jit(solution)/shard_map/ppermute | solution.py:34
  90.6 5.6 %collective-permute-done.6.refs_4_ = bf16[128,512]{1,0:T(8,128)(2,1)S(1)} collective-permute-done((bf16[128,512]{1,0:T(8,128)(2,1)S(1)}, bf16[128,512]{1,0:T(8,128)(2,1)S(1)}, u32[]{:S(2)}, u32[]{:S(2)}) %collective-permute-start.6) | collective-permute-done | bytes 131104 | tf_op jit(solution)/shard_map/ppermute | solution.py:34
  96.2 12.1 %all-gather.2.cloned.1.call-done = bf16[5120,512]{1,0:T(8,128)(2,1)} async-done(((bf16[640,512]{1,0:T(8,128)(2,1)}), bf16[5120,512]{1,0:T(8,128)(2,1)}) %all-gather.2.cloned.1.call-update) | async-done | bytes 5242896 | tf_op jit(solution)/shard_map/all_gather | solution.py:270
  108.4 12.1 %shard_map.129 = (bf16[8,4,128,512]{3,2,1,0:T(8,128)(2,1)}, f32[256,1]{1,0:T(8,128)}, f32[256,1]{1,0:T(8,128)}, f32[8,512]{1,0:T(8,128)}) custom-call(s32[1]{0:T(128)} %bitcast.10.at, bf16[8,640,512]{2,1,0:T(8,128)(2,1)} %bitcast.74, bf16[4096,256]{1,0:T(8,128)(2,1)} %bitcast.73, bf16[128,4096]{1,0:T(8,128)(2,1)} %bitcast.88, f32[512,1]{1,0:T(8,128)} %copy.27.row_r, ...), custom_call_target="tpu_custom_call" | custom-call | tf_op jit(solution)/shard_map/pallas_call | solution.py:320
  121.7 12.1 %all_to_all.36 = f32[8,2,512]{2,1,0:T(2,128)S(1)} all-to-all(f32[8,2,512]{2,1,0:T(2,128)S(1)} %copy.29), channel_id=1, replica_groups=mesh['pipe'=16,'dp'=4,'expert'=8] {'expert'}, dimensions={0} | all-to-all | bytes 65536 | tf_op jit(solution)/shard_map/all_to_all | solution.py:23
  134.0 7.7 %all_to_all.37 = f32[4,1,128]{2,1,0:T(1,128)S(1)} all-to-all(f32[4,1,128]{2,1,0:T(1,128)S(1)} %reshape.259), channel_id=1, replica_groups=mesh['pipe'=16,'dp'=4,'expert'=8] {'dp'}, dimensions={0} | all-to-all | bytes 4096 | tf_op jit(solution)/shard_map/all_to_all | solution.py:23
  143.8 3.2 %all-to-all-start.5 = ((f32[4,1,512]{2,1,0:T(1,128)}), f32[4,1,512]{2,1,0:T(1,128)S(1)}, u32[]{:S(2)}, u32[]{:S(2)}) async-start(f32[4,1,512]{2,1,0:T(1,128)} %broadcast_in_dim.136), calls=%async_computation.6 | async-start | bytes 16384 | tf_op jit(solution)/shard_map/all_to_all | solution.py:19
  147.1 5.2 %all-to-all-done.5 = f32[4,1,512]{2,1,0:T(1,128)S(1)} async-done(((f32[4,1,512]{2,1,0:T(1,128)}), f32[4,1,512]{2,1,0:T(1,128)S(1)}, u32[]{:S(2)}, u32[]{:S(2)}) %all-to-all-start.5) | async-done | bytes 8224 | tf_op jit(solution)/shard_map/all_to_all | solution.py:19
  153.0 24.0 %reduce-scatter.2.cloned.1.call-done = bf16[512,512]{1,0:T(8,128)(2,1)} async-done(((bf16[4096,512]{1,0:T(8,128)(2,1)}), bf16[512,512]{1,0:T(8,128)(2,1)}) %reduce-scatter.2.cloned.1.call-update) | async-done | bytes 524304 | tf_op jit(solution)/shard_map/reduce_scatter | solution.py:349
  177.0 3.5 %all-to-all-start.6 = ((bf16[4,128,512]{2,1,0:T(8,128)(2,1)}), bf16[4,128,512]{2,1,0:T(8,128)(2,1)S(1)}, u32[]{:S(2)}, u32[]{:S(2)}) async-start(bf16[4,128,512]{2,1,0:T(8,128)(2,1)} %bitcast.90), calls=%async_computation.7 | async-start | bytes 1048576 | tf_op jit(solution)/shard_map/all_to_all | solution.py:23
  180.5 10.2 %all-to-all-done.6 = bf16[4,128,512]{2,1,0:T(8,128)(2,1)S(1)} async-done(((bf16[4,128,512]{2,1,0:T(8,128)(2,1)}), bf16[4,128,512]{2,1,0:T(8,128)(2,1)S(1)}, u32[]{:S(2)}, u32[]{:S(2)}) %all-to-all-start.6) | async-done | bytes 524320 | tf_op jit(solution)/shard_map/all_to_all | solution.py:23
  191.1 5.5 %collective-permute-start.8 = (bf16[128,512]{1,0:T(8,128)(2,1)S(1)}, bf16[128,512]{1,0:T(8,128)(2,1)S(1)}, u32[]{:S(2)}, u32[]{:S(2)}) collective-permute-start(bf16[128,512]{1,0:T(8,128)(2,1)S(1)} %fusion.3), channel_id=1, source_target_pairs={{32,0},{64,32},{96,64},{128,96},{160,128},{192,160},{224,192},{256... | collective-permute-start | bytes 393224 | tf_op jit(solution)/shard_map/ppermute | solution.py:29
  199.1 6.7 %collective-permute-done.7 = bf16[128,512]{1,0:T(8,128)(2,1)S(1)} collective-permute-done((bf16[128,512]{1,0:T(8,128)(2,1)S(1)}, bf16[128,512]{1,0:T(8,128)(2,1)S(1)}, u32[]{:S(2)}, u32[]{:S(2)}) %collective-permute-start.7) | collective-permute-done | bytes 131104 | tf_op jit(solution)/shard_map/ppermute | solution.py:29
  (132 shorter events, 23.5 us)
Async XLA Ops:
  7.2 33.4 %copy-start = (bf16[1,512,4]{1,2,0:T(4,128)(2,1)S(1)}, bf16[1,512,4]{1,2,0:T(4,128)(2,1)}, u32[]{:S(2)}) copy-start(bf16[1,512,4]{1,2,0:T(4,128)(2,1)} %param.15) | copy-start | bytes 12292
  7.2 38.9 %copy-start.17 = (s32[1,128,2]{1,2,0:T(2,128)S(1)}, s32[1,128,2]{1,2,0:T(2,128)}, u32[]{:S(2)}) copy-start(s32[1,128,2]{1,2,0:T(2,128)} %param.12) | copy-start | bytes 3076
  7.2 38.9 %copy-start.16 = (s32[1,128,2]{1,2,0:T(2,128)S(1)}, s32[1,128,2]{1,2,0:T(2,128)}, u32[]{:S(2)}) copy-start(s32[1,128,2]{1,2,0:T(2,128)} %param.13) | copy-start | bytes 3076
  7.2 65.3 %copy-start.1 = (bf16[1,1,4096,2,128]{4,3,2,1,0:T(2,128)(2,1)S(1)}, bf16[1,1,4096,2,128]{4,3,2,1,0:T(2,128)(2,1)}, u32[]{:S(2)}) copy-start(bf16[1,1,4096,2,128]{4,3,2,1,0:T(2,128)(2,1)} %param.16) | copy-start | bytes 6291460
  7.2 101.1 %all-gather.2.cloned.1.call-start = ((), (), s32[]{:S(2)}) async-start(), calls=%async_computation.8 | async-start | bytes 5898240 | tf_op jit(solution)/shard_map/all_gather | solution.py:270
  27.5 80.8 %copy-start.4 = (bf16[128,512]{1,0:T(8,128)(2,1)}, bf16[128,512]{1,0:T(8,128)(2,1)S(1)}, u32[]{:S(2)}) copy-start(bf16[128,512]{1,0:T(8,128)(2,1)S(1)} %slice.98.refs_0_) | copy-start | bytes 393220
  27.5 28.0 %collective-permute-start.3 = (bf16[128,512]{1,0:T(8,128)(2,1)S(1)}, bf16[128,512]{1,0:T(8,128)(2,1)S(1)}, u32[]{:S(2)}, u32[]{:S(2)}) collective-permute-start(bf16[128,512]{1,0:T(8,128)(2,1)S(1)} %slice.98.refs_0_), channel_id=1, source_target_pairs={{0,1},{1,2},{2,3},{3,4},{4,5},{5,6},{6,7},{7,0},{8,9},{9,10},{10,1... | collective-permute-start | bytes 393224 | tf_op jit(solution)/shard_map/ppermute | solution.py:34
  31.8 26.8 %collective-permute-start = (bf16[128,512]{1,0:T(8,128)(2,1)S(1)}, bf16[128,512]{1,0:T(8,128)(2,1)S(1)}, u32[]{:S(2)}, u32[]{:S(2)}) collective-permute-start(bf16[128,512]{1,0:T(8,128)(2,1)S(1)} %slice.98.refs_0_), channel_id=1, source_target_pairs={{0,7},{1,0},{2,1},{3,2},{4,3},{5,4},{6,5},{7,6},{8,15},{9,8},{10,9... | collective-permute-start | bytes 393224 | tf_op jit(solution)/shard_map/ppermute | solution.py:34
  41.6 13.7 %all-to-all-start.1 = ((f32[8,16,128]{2,1,0:T(8,128)}), f32[8,16,128]{2,1,0:T(8,128)S(1)}, u32[]{:S(2)}, u32[]{:S(2)}) async-start(f32[8,16,128]{2,1,0:T(8,128)} %broadcast_in_dim.127), calls=%async_computation.1 | async-start | bytes 131072 | tf_op jit(solution)/shard_map/all_to_all | solution.py:19
  55.5 52.8 %copy-start.5 = (bf16[128,512]{1,0:T(8,128)(2,1)}, bf16[128,512]{1,0:T(8,128)(2,1)S(1)}, u32[]{:S(2)}) copy-start(bf16[128,512]{1,0:T(8,128)(2,1)S(1)} %collective-permute-done.3.refs_7_) | copy-start | bytes 393220
  55.5 11.1 %collective-permute-start.4 = (bf16[128,512]{1,0:T(8,128)(2,1)S(1)}, bf16[128,512]{1,0:T(8,128)(2,1)S(1)}, u32[]{:S(2)}, u32[]{:S(2)}) collective-permute-start(bf16[128,512]{1,0:T(8,128)(2,1)S(1)} %collective-permute-done.3.refs_7_), channel_id=1, source_target_pairs={{0,1},{1,2},{2,3},{3,4},{4,5},{5,6},{6,7},{7,0},{8,9},{9,10},{10,1... | collective-permute-start | bytes 393224 | tf_op jit(solution)/shard_map/ppermute | solution.py:34
  58.6 49.7 %copy-start.6 = (bf16[128,512]{1,0:T(8,128)(2,1)}, bf16[128,512]{1,0:T(8,128)(2,1)S(1)}, u32[]{:S(2)}) copy-start(bf16[128,512]{1,0:T(8,128)(2,1)S(1)} %collective-permute-done.refs_1_) | copy-start | bytes 393220
  58.6 20.6 %collective-permute-start.1 = (bf16[128,512]{1,0:T(8,128)(2,1)S(1)}, bf16[128,512]{1,0:T(8,128)(2,1)S(1)}, u32[]{:S(2)}, u32[]{:S(2)}) collective-permute-start(bf16[128,512]{1,0:T(8,128)(2,1)S(1)} %collective-permute-done.refs_1_), channel_id=1, source_target_pairs={{0,7},{1,0},{2,1},{3,2},{4,3},{5,4},{6,5},{7,6},{8,15},{9,8},{10,9... | collective-permute-start | bytes 393224 | tf_op jit(solution)/shard_map/ppermute | solution.py:34
  66.6 41.8 %copy-start.7 = (bf16[128,512]{1,0:T(8,128)(2,1)}, bf16[128,512]{1,0:T(8,128)(2,1)S(1)}, u32[]{:S(2)}) copy-start(bf16[128,512]{1,0:T(8,128)(2,1)S(1)} %collective-permute-done.4.refs_6_) | copy-start | bytes 393220
  66.6 17.8 %collective-permute-start.5 = (bf16[128,512]{1,0:T(8,128)(2,1)S(1)}, bf16[128,512]{1,0:T(8,128)(2,1)S(1)}, u32[]{:S(2)}, u32[]{:S(2)}) collective-permute-start(bf16[128,512]{1,0:T(8,128)(2,1)S(1)} %collective-permute-done.4.refs_6_), channel_id=1, source_target_pairs={{0,1},{1,2},{2,3},{3,4},{4,5},{5,6},{6,7},{7,0},{8,9},{9,10},{10,1... | collective-permute-start | bytes 393224 | tf_op jit(solution)/shard_map/ppermute | solution.py:34
  69.2 8.5 %all-to-all-start.2 = ((f32[4,1,256]{2,1,0:T(1,128)}), f32[4,1,256]{2,1,0:T(1,128)S(1)}, u32[]{:S(2)}, u32[]{:S(2)}) async-start(f32[4,1,256]{2,1,0:T(1,128)} %reshape.257), calls=%async_computation.2 | async-start | bytes 8192 | tf_op jit(solution)/shard_map/all_to_all | solution.py:23
  72.5 104.5 %reduce-scatter.2.cloned.1.call-start = ((), (), s32[]{:S(2)}) async-start(), calls=%async_computation.9 | async-start | bytes 4718592 | tf_op jit(solution)/shard_map/reduce_scatter | solution.py:349
  79.2 11.4 %collective-permute-start.2 = (bf16[128,512]{1,0:T(8,128)(2,1)S(1)}, bf16[128,512]{1,0:T(8,128)(2,1)S(1)}, u32[]{:S(2)}, u32[]{:S(2)}) collective-permute-start(bf16[128,512]{1,0:T(8,128)(2,1)S(1)} %collective-permute-done.1.refs_2_), channel_id=1, source_target_pairs={{0,7},{1,0},{2,1},{3,2},{4,3},{5,4},{6,5},{7,6},{8,15},{9,8},{10,9... | collective-permute-start | bytes 393224 | tf_op jit(solution)/shard_map/ppermute | solution.py:34
  84.4 11.9 %collective-permute-start.6 = (bf16[128,512]{1,0:T(8,128)(2,1)S(1)}, bf16[128,512]{1,0:T(8,128)(2,1)S(1)}, u32[]{:S(2)}, u32[]{:S(2)}) collective-permute-start(bf16[128,512]{1,0:T(8,128)(2,1)S(1)} %collective-permute-done.5.refs_5_), channel_id=1, source_target_pairs={{0,1},{1,2},{2,3},{3,4},{4,5},{5,6},{6,7},{7,0},{8,9},{9,10},{10,1... | collective-permute-start | bytes 393224 | tf_op jit(solution)/shard_map/ppermute | solution.py:34
  120.5 70.3 %copy-start.12 = (bf16[1,128,512]{2,1,0:T(8,128)(2,1)S(1)}, bf16[1,128,512]{2,1,0:T(8,128)(2,1)}, u32[]{:S(2)}) copy-start(bf16[1,128,512]{2,1,0:T(8,128)(2,1)} %param.10) | copy-start | bytes 393220
  143.8 8.5 %all-to-all-start.5 = ((f32[4,1,512]{2,1,0:T(1,128)}), f32[4,1,512]{2,1,0:T(1,128)S(1)}, u32[]{:S(2)}, u32[]{:S(2)}) async-start(f32[4,1,512]{2,1,0:T(1,128)} %broadcast_in_dim.136), calls=%async_computation.6 | async-start | bytes 16384 | tf_op jit(solution)/shard_map/all_to_all | solution.py:19
  177.0 13.8 %all-to-all-start.6 = ((bf16[4,128,512]{2,1,0:T(8,128)(2,1)}), bf16[4,128,512]{2,1,0:T(8,128)(2,1)S(1)}, u32[]{:S(2)}, u32[]{:S(2)}) async-start(bf16[4,128,512]{2,1,0:T(8,128)(2,1)} %bitcast.90), calls=%async_computation.7 | async-start | bytes 1048576 | tf_op jit(solution)/shard_map/all_to_all | solution.py:23
  191.1 8.1 %collective-permute-start.8 = (bf16[128,512]{1,0:T(8,128)(2,1)S(1)}, bf16[128,512]{1,0:T(8,128)(2,1)S(1)}, u32[]{:S(2)}, u32[]{:S(2)}) collective-permute-start(bf16[128,512]{1,0:T(8,128)(2,1)S(1)} %fusion.3), channel_id=1, source_target_pairs={{32,0},{64,32},{96,64},{128,96},{160,128},{192,160},{224,192},{256... | collective-permute-start | bytes 393224 | tf_op jit(solution)/shard_map/ppermute | solution.py:29
  196.9 9.0 %collective-permute-start.7 = (bf16[128,512]{1,0:T(8,128)(2,1)S(1)}, bf16[128,512]{1,0:T(8,128)(2,1)S(1)}, u32[]{:S(2)}, u32[]{:S(2)}) collective-permute-start(bf16[128,512]{1,0:T(8,128)(2,1)S(1)} %fusion.2), channel_id=1, source_target_pairs={{0,32},{32,64},{64,96},{96,128},{128,160},{160,192},{192,224},{224... | collective-permute-start | bytes 393224 | tf_op jit(solution)/shard_map/ppermute | solution.py:29
  (12 other events, 212.2 us)
Sparse Core Ops, SparseCore 0:
  27.6 80.6 all-gather.1
  120.6 56.3 reduce-scatter.1

commit v6 on v4

--- a/solution.py
+++ b/solution.py
@@ -147,18 +147,25 @@
             outs.at[z, k], partial.at[z, :, pl.ds(k * capacity, capacity), :], left.at[z, k]
         )
 
-    for z in range(pieces):
+    def begin(z):
         load(z).start()
         for k in range(3):
             fetch(z, k).start()
+
+    ahead = pieces // 2
+    for z in range(ahead):
+        begin(z)
     weighted = None
     for z in range(pieces):
         part = slice(z * width, (z + 1) * width)
         load(z).wait()
-        for k in range(3):
-            fetch(z, k).wait()
+        fetch(z, 0).wait()
+        if z + ahead < pieces:
+            begin(z + ahead)
+        fetch(z, 1).wait()
         values = rows[z, 0:2].reshape(2 * slots, width)
         product = jnp.dot(values, gate_up[part, :], preferred_element_type=F32)
+        fetch(z, 2).wait()
         incoming = rows[z, 2].reshape(slots, width)
         product_w = lax.dot_general(
             incoming, down_w[:, part], (((1,), (1,)), ((), ())), preferred_element_type=F32

time: 213 us -> 214 us (level)
  no operation moved by 1% of the time
where the time goes in v6:
time: 214 us; the launch traced here: 213 us
  waiting for transfers between devices  103 us (48%)
  blocking collectives  37.7 us (18%)
  starting transfers between devices  27.8 us (13%)
  between operations  14.4 us (7%)
  Pallas kernels  13.3 us (6%)
  local copies, waits for them, and re-layouts  9.32 us (4%)
  other arithmetic  4.15 us (2%)
  matrix products  3.2 us (1%)
    all_gather x1, waiting for transfers between devices, local(): lax.all_gather(arrived.reshape(3 * slots, width), 'expert', axis=0, tiled...  45 us
    all_to_all x3, blocking collectives, exchanged(): return lax.all_to_all(blocks, axis, split_axis=0, concat_axis=0, tiled=True)  37.7 us
    reduce_scatter x1, waiting for transfers between devices, local(): lax.psum_scatter(partial.reshape(pieces * 2 * slots, width), 'expert', sc...  24 us
    all_to_all x2, waiting for transfers between devices, exchanged(): return lax.all_to_all(blocks, axis, split_axis=0, concat_axis=0, tiled=True)  13.8 us
    all_to_all x2, starting transfers between devices, summed_over(): lax.all_to_all(copies, axis, split_axis=0, concat_axis=0, tiled=True)  13.6 us
    all_to_all x2, waiting for transfers between devices, summed_over(): lax.all_to_all(copies, axis, split_axis=0, concat_axis=0, tiled=True)  13.4 us
    pallas_call x1, Pallas kernels, local(): pl.pallas_call(expert_kernel, out_shape=(jax.ShapeDtypeStruct((pieces, ex...  10.7 us
    ppermute x2, starting transfers between devices, shifted(): return lax.ppermute(block, axis, route)  7.45 us
  transfers between devices with their start and end apart: 8, of which 8 were waited for; matrix products, arithmetic and copies ran while one was open for 7% of the time, Pallas kernels for 0%

profile of v6, /device:TPU:2, one launch (start us, length us, event | category | flops | bytes accessed | tf_op | source)
XLA Modules:
  0.0 213.2 jit_solution(1387727822987553061)
XLA Ops:
  7.3 2.6 %shard_map.128 = bf16[4,192,512]{2,1,0:T(8,128)(2,1)} custom-call(s32[2,128]{1,0:T(2,128)} %bitcast.101, s32[2,128]{1,0:T(2,128)} %bitcast.96, f32[1,512]{1,0:T(1,128)} %gain.1, bf16[128,512]{1,0:T(8,128)(2,1)} %bitcast.77, bf16[128,512]{1,0:T(8,128)(2,1)} %bitcast.81, bf16[128,512]{1,0:T(8,128)(2,1)} %bitcast.90), custom_call_target="tpu_custom_call" | custom-call | tf_op jit(solution)/shard_map/pallas_call | solution.py:239
  9.8 17.4 %all_to_all.35 = bf16[4,192,512]{2,1,0:T(8,128)(2,1)} all-to-all(bf16[4,192,512]{2,1,0:T(8,128)(2,1)} %shard_map.128), channel_id=1, replica_groups=mesh['pipe'=16,'dp'=4,'expert'=8] {'dp'}, dimensions={0} | all-to-all | bytes 1572864 | tf_op jit(solution)/shard_map/all_to_all | solution.py:21
  27.2 1.1 fusion.4
  28.4 1.1 convolution_bitcast_fusion
  29.4 1.1 convolution_bitcast_fusion.1
  31.2 10.3 %all-to-all-start.1 = ((f32[8,16,128]{2,1,0:T(8,128)}), f32[8,16,128]{2,1,0:T(8,128)S(1)}, u32[]{:S(2)}, u32[]{:S(2)}) async-start(f32[8,16,128]{2,1,0:T(8,128)} %broadcast_in_dim.123), calls=%async_computation.1 | async-start | bytes 131072 | tf_op jit(solution)/shard_map/all_to_all | solution.py:17
  41.8 8.2 %all-to-all-done.1 = f32[8,16,128]{2,1,0:T(8,128)S(1)} async-done(((f32[8,16,128]{2,1,0:T(8,128)}), f32[8,16,128]{2,1,0:T(8,128)S(1)}, u32[]{:S(2)}, u32[]{:S(2)}) %all-to-all-start.1) | async-done | bytes 65568 | tf_op jit(solution)/shard_map/all_to_all | solution.py:17
  51.5 3.2 %all-to-all-start.2 = ((f32[4,1,256]{2,1,0:T(1,128)}), f32[4,1,256]{2,1,0:T(1,128)S(1)}, u32[]{:S(2)}, u32[]{:S(2)}) async-start(f32[4,1,256]{2,1,0:T(1,128)} %reshape.257), calls=%async_computation.2 | async-start | bytes 8192 | tf_op jit(solution)/shard_map/all_to_all | solution.py:21
  54.9 1.6 copy.35
  56.4 3.6 %all-to-all-done.2 = f32[4,1,256]{2,1,0:T(1,128)S(1)} async-done(((f32[4,1,256]{2,1,0:T(1,128)}), f32[4,1,256]{2,1,0:T(1,128)S(1)}, u32[]{:S(2)}, u32[]{:S(2)}) %all-to-all-start.2) | async-done | bytes 4128 | tf_op jit(solution)/shard_map/all_to_all | solution.py:21
  61.5 0.9 copy.28.row_gate
  62.6 0.9 copy.27.row_r
  63.4 45.0 %all-gather.2.cloned.1.call-done = bf16[6144,512]{1,0:T(8,128)(2,1)} async-done(((bf16[768,512]{1,0:T(8,128)(2,1)}), bf16[6144,512]{1,0:T(8,128)(2,1)}) %all-gather.2.cloned.1.call-update) | async-done | bytes 6291472 | tf_op jit(solution)/shard_map/all_gather | solution.py:253
  108.4 10.7 %shard_map.129 = (bf16[8,4,128,512]{3,2,1,0:T(8,128)(2,1)}, f32[256,1]{1,0:T(8,128)}, f32[256,1]{1,0:T(8,128)}, f32[8,512]{1,0:T(8,128)}) custom-call(bf16[8,4,192,512]{3,2,1,0:T(8,128)(2,1)} %bitcast.73, bf16[4096,256]{1,0:T(8,128)(2,1)} %bitcast.72, bf16[128,4096]{1,0:T(8,128)(2,1)} %bitcast.86, f32[512,1]{1,0:T(8,128)} %copy.27.row_r, f32[512,1]{1,0:T(8,128)} %copy.28.row_gate), custom_call_target="tpu_custom_call" | custom-call | tf_op jit(solution)/shard_map/pallas_call | solution.py:302
  120.4 11.9 %all_to_all.36 = f32[8,2,512]{2,1,0:T(2,128)S(1)} all-to-all(f32[8,2,512]{2,1,0:T(2,128)S(1)} %copy.29), channel_id=1, replica_groups=mesh['pipe'=16,'dp'=4,'expert'=8] {'expert'}, dimensions={0} | all-to-all | bytes 65536 | tf_op jit(solution)/shard_map/all_to_all | solution.py:21
  132.5 8.4 %all_to_all.37 = f32[4,1,128]{2,1,0:T(1,128)S(1)} all-to-all(f32[4,1,128]{2,1,0:T(1,128)S(1)} %reshape.259), channel_id=1, replica_groups=mesh['pipe'=16,'dp'=4,'expert'=8] {'dp'}, dimensions={0} | all-to-all | bytes 4096 | tf_op jit(solution)/shard_map/all_to_all | solution.py:21
  143.0 3.2 %all-to-all-start.5 = ((f32[4,1,512]{2,1,0:T(1,128)}), f32[4,1,512]{2,1,0:T(1,128)S(1)}, u32[]{:S(2)}, u32[]{:S(2)}) async-start(f32[4,1,512]{2,1,0:T(1,128)} %broadcast_in_dim.132), calls=%async_computation.6 | async-start | bytes 16384 | tf_op jit(solution)/shard_map/all_to_all | solution.py:17
  146.3 5.2 %all-to-all-done.5 = f32[4,1,512]{2,1,0:T(1,128)S(1)} async-done(((f32[4,1,512]{2,1,0:T(1,128)}), f32[4,1,512]{2,1,0:T(1,128)S(1)}, u32[]{:S(2)}, u32[]{:S(2)}) %all-to-all-start.5) | async-done | bytes 8224 | tf_op jit(solution)/shard_map/all_to_all | solution.py:17
  152.2 24.0 %reduce-scatter.2.cloned.1.call-done = bf16[512,512]{1,0:T(8,128)(2,1)} async-done(((bf16[4096,512]{1,0:T(8,128)(2,1)}), bf16[512,512]{1,0:T(8,128)(2,1)}) %reduce-scatter.2.cloned.1.call-update) | async-done | bytes 524304 | tf_op jit(solution)/shard_map/reduce_scatter | solution.py:322
  176.2 3.5 %all-to-all-start.6 = ((bf16[4,128,512]{2,1,0:T(8,128)(2,1)}), bf16[4,128,512]{2,1,0:T(8,128)(2,1)S(1)}, u32[]{:S(2)}, u32[]{:S(2)}) async-start(bf16[4,128,512]{2,1,0:T(8,128)(2,1)} %bitcast.88), calls=%async_computation.7 | async-start | bytes 1048576 | tf_op jit(solution)/shard_map/all_to_all | solution.py:21
  179.7 10.2 %all-to-all-done.6 = bf16[4,128,512]{2,1,0:T(8,128)(2,1)S(1)} async-done(((bf16[4,128,512]{2,1,0:T(8,128)(2,1)}), bf16[4,128,512]{2,1,0:T(8,128)(2,1)S(1)}, u32[]{:S(2)}, u32[]{:S(2)}) %all-to-all-start.6) | async-done | bytes 524320 | tf_op jit(solution)/shard_map/all_to_all | solution.py:21
  190.2 5.5 %collective-permute-start.1 = (bf16[128,512]{1,0:T(8,128)(2,1)S(1)}, bf16[128,512]{1,0:T(8,128)(2,1)S(1)}, u32[]{:S(2)}, u32[]{:S(2)}) collective-permute-start(bf16[128,512]{1,0:T(8,128)(2,1)S(1)} %fusion.3), channel_id=1, source_target_pairs={{32,0},{64,32},{96,64},{128,96},{160,128},{192,160},{224,192},{256... | collective-permute-start | bytes 393224 | tf_op jit(solution)/shard_map/ppermute | solution.py:27
  196.0 1.9 collective-permute-start
  198.3 6.7 %collective-permute-done = bf16[128,512]{1,0:T(8,128)(2,1)S(1)} collective-permute-done((bf16[128,512]{1,0:T(8,128)(2,1)S(1)}, bf16[128,512]{1,0:T(8,128)(2,1)S(1)}, u32[]{:S(2)}, u32[]{:S(2)}) %collective-permute-start) | collective-permute-done | bytes 131104 | tf_op jit(solution)/shard_map/ppermute | solution.py:27
  (100 shorter events, 10.6 us)
Async XLA Ops:
  7.2 21.2 %copy-start = (bf16[1,512,4]{1,2,0:T(4,128)(2,1)S(1)}, bf16[1,512,4]{1,2,0:T(4,128)(2,1)}, u32[]{:S(2)}) copy-start(bf16[1,512,4]{1,2,0:T(4,128)(2,1)} %param.15) | copy-start | bytes 12292
  7.2 34.4 %copy-start.9 = (s32[1,128,2]{1,2,0:T(2,128)S(1)}, s32[1,128,2]{1,2,0:T(2,128)}, u32[]{:S(2)}) copy-start(s32[1,128,2]{1,2,0:T(2,128)} %param.12) | copy-start | bytes 3076
  7.2 34.4 %copy-start.8 = (s32[1,128,2]{1,2,0:T(2,128)S(1)}, s32[1,128,2]{1,2,0:T(2,128)}, u32[]{:S(2)}) copy-start(s32[1,128,2]{1,2,0:T(2,128)} %param.13) | copy-start | bytes 3076
  7.2 47.7 %copy-start.1 = (bf16[1,1,4096,2,128]{4,3,2,1,0:T(2,128)(2,1)S(1)}, bf16[1,1,4096,2,128]{4,3,2,1,0:T(2,128)(2,1)}, u32[]{:S(2)}) copy-start(bf16[1,1,4096,2,128]{4,3,2,1,0:T(2,128)(2,1)} %param.16) | copy-start | bytes 6291460
  7.2 101.2 %all-gather.2.cloned.1.call-start = ((), (), s32[]{:S(2)}) async-start(), calls=%async_computation.8 | async-start | bytes 7077888 | tf_op jit(solution)/shard_map/all_gather | solution.py:253
  31.2 18.8 %all-to-all-start.1 = ((f32[8,16,128]{2,1,0:T(8,128)}), f32[8,16,128]{2,1,0:T(8,128)S(1)}, u32[]{:S(2)}, u32[]{:S(2)}) async-start(f32[8,16,128]{2,1,0:T(8,128)} %broadcast_in_dim.123), calls=%async_computation.1 | async-start | bytes 131072 | tf_op jit(solution)/shard_map/all_to_all | solution.py:17
  51.5 8.5 %all-to-all-start.2 = ((f32[4,1,256]{2,1,0:T(1,128)}), f32[4,1,256]{2,1,0:T(1,128)S(1)}, u32[]{:S(2)}, u32[]{:S(2)}) async-start(f32[4,1,256]{2,1,0:T(1,128)} %reshape.257), calls=%async_computation.2 | async-start | bytes 8192 | tf_op jit(solution)/shard_map/all_to_all | solution.py:21
  54.8 121.4 %reduce-scatter.2.cloned.1.call-start = ((), (), s32[]{:S(2)}) async-start(), calls=%async_computation.9 | async-start | bytes 4718592 | tf_op jit(solution)/shard_map/reduce_scatter | solution.py:322
  119.2 0.9 copy-start.7
  119.2 1.0 copy-start.6
  119.2 1.1 copy-start.10
  119.2 22.9 %copy-start.3 = (bf16[1,128,512]{2,1,0:T(8,128)(2,1)S(1)}, bf16[1,128,512]{2,1,0:T(8,128)(2,1)}, u32[]{:S(2)}) copy-start(bf16[1,128,512]{2,1,0:T(8,128)(2,1)} %param.11) | copy-start | bytes 393220
  119.2 23.2 %copy-start.11 = (f32[1,512]{1,0:T(1,128)S(1)}, f32[1,512]{1,0:T(1,128)}, u32[]{:S(2)}) copy-start(f32[1,512]{1,0:T(1,128)} %gain.1) | copy-start | bytes 6148
  119.2 70.7 %copy-start.4 = (bf16[1,128,512]{2,1,0:T(8,128)(2,1)S(1)}, bf16[1,128,512]{2,1,0:T(8,128)(2,1)}, u32[]{:S(2)}) copy-start(bf16[1,128,512]{2,1,0:T(8,128)(2,1)} %param.10) | copy-start | bytes 393220
  119.2 76.5 %copy-start.2 = (bf16[1,128,512]{2,1,0:T(8,128)(2,1)S(1)}, bf16[1,128,512]{2,1,0:T(8,128)(2,1)}, u32[]{:S(2)}) copy-start(bf16[1,128,512]{2,1,0:T(8,128)(2,1)} %param.9) | copy-start | bytes 393220
  143.0 8.5 %all-to-all-start.5 = ((f32[4,1,512]{2,1,0:T(1,128)}), f32[4,1,512]{2,1,0:T(1,128)S(1)}, u32[]{:S(2)}, u32[]{:S(2)}) async-start(f32[4,1,512]{2,1,0:T(1,128)} %broadcast_in_dim.132), calls=%async_computation.6 | async-start | bytes 16384 | tf_op jit(solution)/shard_map/all_to_all | solution.py:17
  176.2 13.8 %all-to-all-start.6 = ((bf16[4,128,512]{2,1,0:T(8,128)(2,1)}), bf16[4,128,512]{2,1,0:T(8,128)(2,1)S(1)}, u32[]{:S(2)}, u32[]{:S(2)}) async-start(bf16[4,128,512]{2,1,0:T(8,128)(2,1)} %bitcast.88), calls=%async_computation.7 | async-start | bytes 1048576 | tf_op jit(solution)/shard_map/all_to_all | solution.py:21
  190.2 16.1 %copy-start.12 = (bf16[128,512]{1,0:T(8,128)(2,1)}, bf16[128,512]{1,0:T(8,128)(2,1)S(1)}, u32[]{:S(2)}) copy-start(bf16[128,512]{1,0:T(8,128)(2,1)S(1)} %fusion.3) | copy-start | bytes 393220
  190.2 8.0 %collective-permute-start.1 = (bf16[128,512]{1,0:T(8,128)(2,1)S(1)}, bf16[128,512]{1,0:T(8,128)(2,1)S(1)}, u32[]{:S(2)}, u32[]{:S(2)}) collective-permute-start(bf16[128,512]{1,0:T(8,128)(2,1)S(1)} %fusion.3), channel_id=1, source_target_pairs={{32,0},{64,32},{96,64},{128,96},{160,128},{192,160},{224,192},{256... | collective-permute-start | bytes 393224 | tf_op jit(solution)/shard_map/ppermute | solution.py:27
  196.0 10.3 %copy-start.5 = (bf16[128,512]{1,0:T(8,128)(2,1)}, bf16[128,512]{1,0:T(8,128)(2,1)S(1)}, u32[]{:S(2)}) copy-start(bf16[128,512]{1,0:T(8,128)(2,1)S(1)} %fusion.2) | copy-start | bytes 393220
  196.0 9.0 %collective-permute-start = (bf16[128,512]{1,0:T(8,128)(2,1)S(1)}, bf16[128,512]{1,0:T(8,128)(2,1)S(1)}, u32[]{:S(2)}, u32[]{:S(2)}) collective-permute-start(bf16[128,512]{1,0:T(8,128)(2,1)S(1)} %fusion.2), channel_id=1, source_target_pairs={{0,32},{32,64},{64,96},{96,128},{128,160},{160,192},{192,224},{224... | collective-permute-start | bytes 393224 | tf_op jit(solution)/shard_map/ppermute | solution.py:27
Sparse Core Ops, SparseCore 0:
  27.4 81.0 all-gather.1
  119.4 56.7 reduce-scatter.1

commit v7 on v4

--- a/solution.py
+++ b/solution.py
@@ -133,33 +133,30 @@
     slots = experts * capacity
     hidden = down_w.shape[0]
 
-    def fetch(z, k):
-        return pltpu.make_async_copy(
-            whole.at[z, :, pl.ds(k * capacity, capacity), :], rows.at[z, k], took.at[z, k]
-        )
+    def fetch(z):
+        return pltpu.make_async_copy(whole.at[z], rows.at[z], took.at[z])
+
+    def taken(z, k):
+        return rows[z, :, k * capacity : (k + 1) * capacity, :].reshape(slots, width)
 
     def load(z):
         part = pl.ds(z * width, width)
         return pltpu.make_async_copy(gate_up_hbm.at[part, :], gate_up.at[part, :], loaded.at[z])
 
-    def put(z, k):
-        return pltpu.make_async_copy(
-            outs.at[z, k], partial.at[z, :, pl.ds(k * capacity, capacity), :], left.at[z, k]
-        )
+    def put(z):
+        return pltpu.make_async_copy(outs.at[z], partial.at[z], left.at[z])
 
     for z in range(pieces):
         load(z).start()
-        for k in range(3):
-            fetch(z, k).start()
+        fetch(z).start()
     weighted = None
     for z in range(pieces):
         part = slice(z * width, (z + 1) * width)
         load(z).wait()
-        for k in range(3):
-            fetch(z, k).wait()
-        values = rows[z, 0:2].reshape(2 * slots, width)
+        fetch(z).wait()
+        values = jnp.concatenate([taken(z, 0), taken(z, 1)], axis=0)
         product = jnp.dot(values, gate_up[part, :], preferred_element_type=F32)
-        incoming = rows[z, 2].reshape(slots, width)
+        incoming = taken(z, 2)
         product_w = lax.dot_general(
             incoming, down_w[:, part], (((1,), (1,)), ((), ())), preferred_element_type=F32
         )
@@ -187,21 +184,19 @@
     for z in range(pieces):
         part = slice(z * width, (z + 1) * width)
         out_f = jnp.dot(inner_f, down_w[:, part], preferred_element_type=F32) * gate_f
-        outs[z, 0] = out_f.astype(BF16).reshape(experts, capacity, width)
-        put(z, 0).start()
+        outs[z, :, :capacity, :] = out_f.astype(BF16).reshape(experts, capacity, width)
         out_b = (
             lax.dot_general(
                 grads, gate_up[part, :], (((1,), (1,)), ((), ())), preferred_element_type=F32
             )
             * gate_b
         )
-        outs[z, 1] = out_b.astype(BF16).reshape(experts, capacity, width)
-        put(z, 1).start()
-        stashed = rows[z, 1].reshape(slots, width).astype(F32)
+        outs[z, :, capacity:, :] = out_b.astype(BF16).reshape(experts, capacity, width)
+        put(z).start()
+        stashed = taken(z, 1).astype(F32)
         gain_part[z : z + 1, :] = jnp.sum(out_b * r_b * stashed, axis=0, keepdims=True)
     for z in range(pieces):
-        for k in range(2):
-            put(z, k).wait()
+        put(z).wait()
 
 
 def local(
@@ -303,13 +298,13 @@
         in_specs=[hbm] * 2 + [vmem] * 3,
         out_specs=(hbm, vmem, vmem, vmem),
         scratch_shapes=[
-            pltpu.VMEM((pieces, 3, experts, capacity, width), BF16),
-            pltpu.VMEM((pieces, 2, experts, capacity, width), BF16),
+            pltpu.VMEM((pieces, experts, 3 * capacity, width), BF16),
+            pltpu.VMEM((pieces, experts, 2 * capacity, width), BF16),
             pltpu.VMEM((2 * slots, 2 * hidden), F32),
             pltpu.VMEM((D, 2 * hidden), BF16),
-            pltpu.SemaphoreType.DMA((pieces, 3)),
             pltpu.SemaphoreType.DMA((pieces,)),
-            pltpu.SemaphoreType.DMA((pieces, 2)),
+            pltpu.SemaphoreType.DMA((pieces,)),
+            pltpu.SemaphoreType.DMA((pieces,)),
         ],
     )(whole.reshape(pieces, experts, 3 * capacity, width), gate_up, down_w, row_r, row_gate)
     summed = lax.psum_scatter(

time: 213 us -> 212 us (level)
  no operation moved by 1% of the time
where the time goes in v7:
time: 212 us; the launch traced here: 211 us
  waiting for transfers between devices  103 us (49%)
  blocking collectives  37.7 us (18%)
  starting transfers between devices  27.8 us (13%)
  between operations  14.4 us (7%)
  Pallas kernels  11.4 us (5%)
  local copies, waits for them, and re-layouts  9.32 us (4%)
  other arithmetic  4.15 us (2%)
  matrix products  3.2 us (2%)
    all_gather x1, waiting for transfers between devices, local(): lax.all_gather(arrived.reshape(3 * slots, width), 'expert', axis=0, tiled...  45 us
    all_to_all x3, blocking collectives, exchanged(): return lax.all_to_all(blocks, axis, split_axis=0, concat_axis=0, tiled=True)  37.7 us
    reduce_scatter x1, waiting for transfers between devices, local(): lax.psum_scatter(partial.reshape(pieces * 2 * slots, width), 'expert', sc...  24 us
    all_to_all x2, waiting for transfers between devices, exchanged(): return lax.all_to_all(blocks, axis, split_axis=0, concat_axis=0, tiled=True)  13.8 us
    all_to_all x2, starting transfers between devices, summed_over(): lax.all_to_all(copies, axis, split_axis=0, concat_axis=0, tiled=True)  13.6 us
    all_to_all x2, waiting for transfers between devices, summed_over(): lax.all_to_all(copies, axis, split_axis=0, concat_axis=0, tiled=True)  13.4 us
    pallas_call x1, Pallas kernels, local(): pl.pallas_call(expert_kernel, out_shape=(jax.ShapeDtypeStruct((pieces, ex...  8.82 us
    ppermute x2, starting transfers between devices, shifted(): return lax.ppermute(block, axis, route)  7.45 us
  transfers between devices with their start and end apart: 8, of which 8 were waited for; matrix products, arithmetic and copies ran while one was open for 7% of the time, Pallas kernels for 0%

profile of v7, /device:TPU:2, one launch (start us, length us, event | category | flops | bytes accessed | tf_op | source)
XLA Modules:
  0.0 211.3 jit_solution(10547123827636379613)
XLA Ops:
  7.3 2.6 %shard_map.128 = bf16[4,192,512]{2,1,0:T(8,128)(2,1)} custom-call(s32[2,128]{1,0:T(2,128)} %bitcast.101, s32[2,128]{1,0:T(2,128)} %bitcast.96, f32[1,512]{1,0:T(1,128)} %gain.1, bf16[128,512]{1,0:T(8,128)(2,1)} %bitcast.77, bf16[128,512]{1,0:T(8,128)(2,1)} %bitcast.81, bf16[128,512]{1,0:T(8,128)(2,1)} %bitcast.90), custom_call_target="tpu_custom_call" | custom-call | tf_op jit(solution)/shard_map/pallas_call | solution.py:227
  9.8 17.4 %all_to_all.35 = bf16[4,192,512]{2,1,0:T(8,128)(2,1)} all-to-all(bf16[4,192,512]{2,1,0:T(8,128)(2,1)} %shard_map.128), channel_id=1, replica_groups=mesh['pipe'=16,'dp'=4,'expert'=8] {'dp'}, dimensions={0} | all-to-all | bytes 1572864 | tf_op jit(solution)/shard_map/all_to_all | solution.py:21
  27.2 1.1 fusion.4
  28.4 1.1 convolution_bitcast_fusion
  29.4 1.1 convolution_bitcast_fusion.1
  31.2 10.3 %all-to-all-start.1 = ((f32[8,16,128]{2,1,0:T(8,128)}), f32[8,16,128]{2,1,0:T(8,128)S(1)}, u32[]{:S(2)}, u32[]{:S(2)}) async-start(f32[8,16,128]{2,1,0:T(8,128)} %broadcast_in_dim.123), calls=%async_computation.1 | async-start | bytes 131072 | tf_op jit(solution)/shard_map/all_to_all | solution.py:17
  41.8 8.2 %all-to-all-done.1 = f32[8,16,128]{2,1,0:T(8,128)S(1)} async-done(((f32[8,16,128]{2,1,0:T(8,128)}), f32[8,16,128]{2,1,0:T(8,128)S(1)}, u32[]{:S(2)}, u32[]{:S(2)}) %all-to-all-start.1) | async-done | bytes 65568 | tf_op jit(solution)/shard_map/all_to_all | solution.py:17
  51.5 3.2 %all-to-all-start.2 = ((f32[4,1,256]{2,1,0:T(1,128)}), f32[4,1,256]{2,1,0:T(1,128)S(1)}, u32[]{:S(2)}, u32[]{:S(2)}) async-start(f32[4,1,256]{2,1,0:T(1,128)} %reshape.257), calls=%async_computation.2 | async-start | bytes 8192 | tf_op jit(solution)/shard_map/all_to_all | solution.py:21
  54.9 1.6 copy.35
  56.4 3.6 %all-to-all-done.2 = f32[4,1,256]{2,1,0:T(1,128)S(1)} async-done(((f32[4,1,256]{2,1,0:T(1,128)}), f32[4,1,256]{2,1,0:T(1,128)S(1)}, u32[]{:S(2)}, u32[]{:S(2)}) %all-to-all-start.2) | async-done | bytes 4128 | tf_op jit(solution)/shard_map/all_to_all | solution.py:21
  61.5 0.9 copy.28.row_gate
  62.6 0.9 copy.27.row_r
  63.4 45.0 %all-gather.2.cloned.1.call-done = bf16[6144,512]{1,0:T(8,128)(2,1)} async-done(((bf16[768,512]{1,0:T(8,128)(2,1)}), bf16[6144,512]{1,0:T(8,128)(2,1)}) %all-gather.2.cloned.1.call-update) | async-done | bytes 6291472 | tf_op jit(solution)/shard_map/all_gather | solution.py:241
  108.4 8.8 %shard_map.129 = (bf16[8,4,128,512]{3,2,1,0:T(8,128)(2,1)}, f32[256,1]{1,0:T(8,128)}, f32[256,1]{1,0:T(8,128)}, f32[8,512]{1,0:T(8,128)}) custom-call(bf16[8,4,192,512]{3,2,1,0:T(8,128)(2,1)} %bitcast.73, bf16[4096,256]{1,0:T(8,128)(2,1)} %bitcast.72, bf16[128,4096]{1,0:T(8,128)(2,1)} %bitcast.86, f32[512,1]{1,0:T(8,128)} %copy.27.row_r, f32[512,1]{1,0:T(8,128)} %copy.28.row_gate), custom_call_target="tpu_custom_call" | custom-call | tf_op jit(solution)/shard_map/pallas_call | solution.py:290
  118.5 11.9 %all_to_all.36 = f32[8,2,512]{2,1,0:T(2,128)S(1)} all-to-all(f32[8,2,512]{2,1,0:T(2,128)S(1)} %copy.29), channel_id=1, replica_groups=mesh['pipe'=16,'dp'=4,'expert'=8] {'expert'}, dimensions={0} | all-to-all | bytes 65536 | tf_op jit(solution)/shard_map/all_to_all | solution.py:21
  130.6 8.4 %all_to_all.37 = f32[4,1,128]{2,1,0:T(1,128)S(1)} all-to-all(f32[4,1,128]{2,1,0:T(1,128)S(1)} %reshape.259), channel_id=1, replica_groups=mesh['pipe'=16,'dp'=4,'expert'=8] {'dp'}, dimensions={0} | all-to-all | bytes 4096 | tf_op jit(solution)/shard_map/all_to_all | solution.py:21
  141.1 3.2 %all-to-all-start.5 = ((f32[4,1,512]{2,1,0:T(1,128)}), f32[4,1,512]{2,1,0:T(1,128)S(1)}, u32[]{:S(2)}, u32[]{:S(2)}) async-start(f32[4,1,512]{2,1,0:T(1,128)} %broadcast_in_dim.132), calls=%async_computation.6 | async-start | bytes 16384 | tf_op jit(solution)/shard_map/all_to_all | solution.py:17
  144.5 5.2 %all-to-all-done.5 = f32[4,1,512]{2,1,0:T(1,128)S(1)} async-done(((f32[4,1,512]{2,1,0:T(1,128)}), f32[4,1,512]{2,1,0:T(1,128)S(1)}, u32[]{:S(2)}, u32[]{:S(2)}) %all-to-all-start.5) | async-done | bytes 8224 | tf_op jit(solution)/shard_map/all_to_all | solution.py:17
  150.3 24.0 %reduce-scatter.2.cloned.1.call-done = bf16[512,512]{1,0:T(8,128)(2,1)} async-done(((bf16[4096,512]{1,0:T(8,128)(2,1)}), bf16[512,512]{1,0:T(8,128)(2,1)}) %reduce-scatter.2.cloned.1.call-update) | async-done | bytes 524304 | tf_op jit(solution)/shard_map/reduce_scatter | solution.py:310
  174.3 3.5 %all-to-all-start.6 = ((bf16[4,128,512]{2,1,0:T(8,128)(2,1)}), bf16[4,128,512]{2,1,0:T(8,128)(2,1)S(1)}, u32[]{:S(2)}, u32[]{:S(2)}) async-start(bf16[4,128,512]{2,1,0:T(8,128)(2,1)} %bitcast.88), calls=%async_computation.7 | async-start | bytes 1048576 | tf_op jit(solution)/shard_map/all_to_all | solution.py:21
  177.8 10.2 %all-to-all-done.6 = bf16[4,128,512]{2,1,0:T(8,128)(2,1)S(1)} async-done(((bf16[4,128,512]{2,1,0:T(8,128)(2,1)}), bf16[4,128,512]{2,1,0:T(8,128)(2,1)S(1)}, u32[]{:S(2)}, u32[]{:S(2)}) %all-to-all-start.6) | async-done | bytes 524320 | tf_op jit(solution)/shard_map/all_to_all | solution.py:21
  188.3 5.5 %collective-permute-start.1 = (bf16[128,512]{1,0:T(8,128)(2,1)S(1)}, bf16[128,512]{1,0:T(8,128)(2,1)S(1)}, u32[]{:S(2)}, u32[]{:S(2)}) collective-permute-start(bf16[128,512]{1,0:T(8,128)(2,1)S(1)} %fusion.3), channel_id=1, source_target_pairs={{32,0},{64,32},{96,64},{128,96},{160,128},{192,160},{224,192},{256... | collective-permute-start | bytes 393224 | tf_op jit(solution)/shard_map/ppermute | solution.py:27
  194.1 1.9 collective-permute-start
  196.4 6.7 %collective-permute-done = bf16[128,512]{1,0:T(8,128)(2,1)S(1)} collective-permute-done((bf16[128,512]{1,0:T(8,128)(2,1)S(1)}, bf16[128,512]{1,0:T(8,128)(2,1)S(1)}, u32[]{:S(2)}, u32[]{:S(2)}) %collective-permute-start) | collective-permute-done | bytes 131104 | tf_op jit(solution)/shard_map/ppermute | solution.py:27
  (100 shorter events, 10.6 us)
Async XLA Ops:
  7.2 21.2 %copy-start = (bf16[1,512,4]{1,2,0:T(4,128)(2,1)S(1)}, bf16[1,512,4]{1,2,0:T(4,128)(2,1)}, u32[]{:S(2)}) copy-start(bf16[1,512,4]{1,2,0:T(4,128)(2,1)} %param.15) | copy-start | bytes 12292
  7.2 34.4 %copy-start.9 = (s32[1,128,2]{1,2,0:T(2,128)S(1)}, s32[1,128,2]{1,2,0:T(2,128)}, u32[]{:S(2)}) copy-start(s32[1,128,2]{1,2,0:T(2,128)} %param.12) | copy-start | bytes 3076
  7.2 34.4 %copy-start.8 = (s32[1,128,2]{1,2,0:T(2,128)S(1)}, s32[1,128,2]{1,2,0:T(2,128)}, u32[]{:S(2)}) copy-start(s32[1,128,2]{1,2,0:T(2,128)} %param.13) | copy-start | bytes 3076
  7.2 47.7 %copy-start.1 = (bf16[1,1,4096,2,128]{4,3,2,1,0:T(2,128)(2,1)S(1)}, bf16[1,1,4096,2,128]{4,3,2,1,0:T(2,128)(2,1)}, u32[]{:S(2)}) copy-start(bf16[1,1,4096,2,128]{4,3,2,1,0:T(2,128)(2,1)} %param.16) | copy-start | bytes 6291460
  7.2 101.2 %all-gather.2.cloned.1.call-start = ((), (), s32[]{:S(2)}) async-start(), calls=%async_computation.8 | async-start | bytes 7077888 | tf_op jit(solution)/shard_map/all_gather | solution.py:241
  31.2 18.8 %all-to-all-start.1 = ((f32[8,16,128]{2,1,0:T(8,128)}), f32[8,16,128]{2,1,0:T(8,128)S(1)}, u32[]{:S(2)}, u32[]{:S(2)}) async-start(f32[8,16,128]{2,1,0:T(8,128)} %broadcast_in_dim.123), calls=%async_computation.1 | async-start | bytes 131072 | tf_op jit(solution)/shard_map/all_to_all | solution.py:17
  51.5 8.5 %all-to-all-start.2 = ((f32[4,1,256]{2,1,0:T(1,128)}), f32[4,1,256]{2,1,0:T(1,128)S(1)}, u32[]{:S(2)}, u32[]{:S(2)}) async-start(f32[4,1,256]{2,1,0:T(1,128)} %reshape.257), calls=%async_computation.2 | async-start | bytes 8192 | tf_op jit(solution)/shard_map/all_to_all | solution.py:21
  54.8 119.5 %reduce-scatter.2.cloned.1.call-start = ((), (), s32[]{:S(2)}) async-start(), calls=%async_computation.9 | async-start | bytes 4718592 | tf_op jit(solution)/shard_map/reduce_scatter | solution.py:310
  117.3 0.9 copy-start.7
  117.3 1.0 copy-start.6
  117.3 1.1 copy-start.10
  117.3 22.9 %copy-start.3 = (bf16[1,128,512]{2,1,0:T(8,128)(2,1)S(1)}, bf16[1,128,512]{2,1,0:T(8,128)(2,1)}, u32[]{:S(2)}) copy-start(bf16[1,128,512]{2,1,0:T(8,128)(2,1)} %param.11) | copy-start | bytes 393220
  117.3 23.2 %copy-start.11 = (f32[1,512]{1,0:T(1,128)S(1)}, f32[1,512]{1,0:T(1,128)}, u32[]{:S(2)}) copy-start(f32[1,512]{1,0:T(1,128)} %gain.1) | copy-start | bytes 6148
  117.3 70.7 %copy-start.4 = (bf16[1,128,512]{2,1,0:T(8,128)(2,1)S(1)}, bf16[1,128,512]{2,1,0:T(8,128)(2,1)}, u32[]{:S(2)}) copy-start(bf16[1,128,512]{2,1,0:T(8,128)(2,1)} %param.10) | copy-start | bytes 393220
  117.3 76.5 %copy-start.2 = (bf16[1,128,512]{2,1,0:T(8,128)(2,1)S(1)}, bf16[1,128,512]{2,1,0:T(8,128)(2,1)}, u32[]{:S(2)}) copy-start(bf16[1,128,512]{2,1,0:T(8,128)(2,1)} %param.9) | copy-start | bytes 393220
  141.1 8.5 %all-to-all-start.5 = ((f32[4,1,512]{2,1,0:T(1,128)}), f32[4,1,512]{2,1,0:T(1,128)S(1)}, u32[]{:S(2)}, u32[]{:S(2)}) async-start(f32[4,1,512]{2,1,0:T(1,128)} %broadcast_in_dim.132), calls=%async_computation.6 | async-start | bytes 16384 | tf_op jit(solution)/shard_map/all_to_all | solution.py:17
  174.3 13.8 %all-to-all-start.6 = ((bf16[4,128,512]{2,1,0:T(8,128)(2,1)}), bf16[4,128,512]{2,1,0:T(8,128)(2,1)S(1)}, u32[]{:S(2)}, u32[]{:S(2)}) async-start(bf16[4,128,512]{2,1,0:T(8,128)(2,1)} %bitcast.88), calls=%async_computation.7 | async-start | bytes 1048576 | tf_op jit(solution)/shard_map/all_to_all | solution.py:21
  188.3 16.1 %copy-start.12 = (bf16[128,512]{1,0:T(8,128)(2,1)}, bf16[128,512]{1,0:T(8,128)(2,1)S(1)}, u32[]{:S(2)}) copy-start(bf16[128,512]{1,0:T(8,128)(2,1)S(1)} %fusion.3) | copy-start | bytes 393220
  188.3 8.0 %collective-permute-start.1 = (bf16[128,512]{1,0:T(8,128)(2,1)S(1)}, bf16[128,512]{1,0:T(8,128)(2,1)S(1)}, u32[]{:S(2)}, u32[]{:S(2)}) collective-permute-start(bf16[128,512]{1,0:T(8,128)(2,1)S(1)} %fusion.3), channel_id=1, source_target_pairs={{32,0},{64,32},{96,64},{128,96},{160,128},{192,160},{224,192},{256... | collective-permute-start | bytes 393224 | tf_op jit(solution)/shard_map/ppermute | solution.py:27
  194.1 10.3 %copy-start.5 = (bf16[128,512]{1,0:T(8,128)(2,1)}, bf16[128,512]{1,0:T(8,128)(2,1)S(1)}, u32[]{:S(2)}) copy-start(bf16[128,512]{1,0:T(8,128)(2,1)S(1)} %fusion.2) | copy-start | bytes 393220
  194.1 9.0 %collective-permute-start = (bf16[128,512]{1,0:T(8,128)(2,1)S(1)}, bf16[128,512]{1,0:T(8,128)(2,1)S(1)}, u32[]{:S(2)}, u32[]{:S(2)}) collective-permute-start(bf16[128,512]{1,0:T(8,128)(2,1)S(1)} %fusion.2), channel_id=1, source_target_pairs={{0,32},{32,64},{64,96},{96,128},{128,160},{160,192},{192,224},{224... | collective-permute-start | bytes 393224 | tf_op jit(solution)/shard_map/ppermute | solution.py:27
Sparse Core Ops, SparseCore 0:
  27.4 81.0 all-gather.1
  117.5 56.7 reduce-scatter.1
